TPU v7x, 32 devices: a whole 2x2x4 slice. The times are simulated.
32 devices in a mesh: samp: 4 (over z), atom: 8 (over y, x, core).
Axes of the slice: x: 2, y: 2, z: 4, core: 2. Of those that a mesh axis runs over, the one named last changes fastest.
Arguments:
- atom_state: bfloat16 [16, 2560, 128], P('samp', 'atom'), may hold values from -6 to 6, as said below
- atom_token: int32 [2560], P('atom'), may hold values from 0 to 319, never falling along the last dimension, each value on 1 to 24 neighbouring positions
- window_valid: int32 [80], P('atom'), may hold values from 1 to 32
- attend_gain: float32 [128], replicated, may hold values from 0.25 to 1.75
- project_weight: bfloat16 [128, 384], replicated, may hold values from -4 to 4
- output_weight: bfloat16 [128, 128], replicated, may hold values from -1.5 to 1.5
- token_bias: float32 [4], replicated, may hold values from -2 to 2
- transit_gain: float32 [128], replicated, may hold values from 0.25 to 1.75
- transit_weight: bfloat16 [128, 512], replicated, may hold values from -0.5 to 0.5
- return_weight: bfloat16 [256, 128], replicated, may hold values from -0.375 to 0.375
- cotangent: bfloat16 [16, 2560, 128], P('samp', 'atom'), may hold values from -6 to 6
Outputs:
- block_out: bfloat16 [16, 2560, 128], P('samp', 'atom')
- state_grad: bfloat16 [16, 2560, 128], P('samp', 'atom')
- grad_attend_gain: float32 [128], replicated
- grad_project: float32 [128, 384], replicated
- grad_output: float32 [128, 128], replicated
- grad_bias: float32 [4], replicated
- grad_transit_gain: float32 [128], replicated
- grad_transit: float32 [128, 512], replicated
- grad_return: float32 [256, 128], replicated
Inputs may be any that keep to these rules, and one draw needn't show every extreme that they name: atom_state is finite. `atom_token`: tokens are numbered in order along the atoms; a token has 1 to 24 atoms.
All inputs are finite; a program needn't handle non-finite values.
Results may differ from a plain program's by a relative error of at most 0.025.
The roundings to bfloat16 on the way count: a program that leaves them out, or rounds other values in their place, can miss the bound.
Values may be sent and summed in bfloat16 or wider, within the bound.
No kernel may reach another device: no remote copies, remote signals or barrier semaphores. Data moves between devices by JAX's collectives and lax.ppermute only.
A program may use at most 64 MiB of HBM per device.

v0:
```python
import jax
import jax.numpy as jnp
from jax import lax
from jax.sharding import PartitionSpec as P

HEADS = 4
TRANS = 256
QWIN = 32
KWIN = 128
HALO = 48


PRECISE = lax.Precision.HIGHEST
EPSILON = 1e-05
CLIP_NORM = 256.0


def with_halo(value, sides, width):
    for axis, dim in sides:
        size, length = (lax.axis_size(axis), value.shape[dim])
        up = [(i, (i + 1) % size) for i in range(size - 1)]
        down = [(j, i) for i, j in up]
        last = lax.slice_in_dim(value, length - width, length, axis=dim)
        first = lax.slice_in_dim(value, 0, width, axis=dim)
        before = lax.ppermute(last, axis, up)
        after = lax.ppermute(first, axis, down)
        value = jnp.concatenate([before, value, after], axis=dim)
    return value


def passed_along(value, axis, by):
    size = lax.axis_size(axis)
    pairs = [(i, i + by) for i in range(size) if 0 <= i + by < size]
    return lax.ppermute(value, axis, pairs)


def normalize(values, scaling):
    values = values.astype(jnp.float32)
    center = jnp.mean(values, axis=-1, keepdims=True)
    shifted = values - center
    variance = jnp.mean(shifted * shifted, axis=-1, keepdims=True)
    return shifted * lax.rsqrt(variance + EPSILON) * scaling


def token_codes(atom_token, window_valid):
    windows_here = window_valid.shape[0]
    slots = lax.broadcasted_iota(jnp.int32, (windows_here, QWIN), 1)
    inside = (slots < window_valid[:, None]).reshape(-1)
    return jnp.where(inside, atom_token + 1, 0)


def attend(queries, pairs, query_ids, ext_ids, token_bias):
    channels = queries.shape[1]
    window_count = queries.shape[0] // QWIN
    extra_blocks = 2 * HALO // QWIN
    span_blocks = KWIN // QWIN
    head_dim = channels // HEADS
    blocks = pairs.reshape(window_count + extra_blocks, QWIN, 2 * channels)
    gathered = jnp.concatenate(
        [blocks[offset : offset + window_count] for offset in range(span_blocks)], axis=1
    )
    code_blocks = ext_ids.reshape(window_count + extra_blocks, QWIN)
    key_ids = jnp.concatenate(
        [code_blocks[offset : offset + window_count] for offset in range(span_blocks)], axis=1
    )
    query_blocks = queries.reshape(window_count, QWIN, HEADS, head_dim)
    keys_in = gathered[:, :, :channels].reshape(window_count, KWIN, HEADS, head_dim)
    values_in = gathered[:, :, channels:].reshape(window_count, KWIN, HEADS, head_dim)
    scores = jnp.einsum("wqhd,wkhd->whqk", query_blocks, keys_in, precision=PRECISE) / jnp.sqrt(
        float(head_dim)
    )
    query_codes = query_ids.reshape(window_count, QWIN)
    same_token = (query_codes[:, :, None] == key_ids[:, None, :]).astype(jnp.float32)
    scores = scores + token_bias[None, :, None, None] * same_token[:, None, :, :]
    usable_key = (key_ids > 0)[:, None, None, :]
    scores = jnp.where(usable_key, scores, -1e30)
    highest = lax.stop_gradient(jnp.max(scores, axis=-1, keepdims=True))
    weights = jnp.exp(scores - highest)
    weights = weights / jnp.sum(weights, axis=-1, keepdims=True)
    outcome = jnp.einsum("whqk,wkhd->wqhd", weights, values_in, precision=PRECISE)
    return outcome.reshape(window_count * QWIN, channels)


def place_rims(center, from_before, from_after):
    atoms_here = center.shape[1]
    lower = jnp.pad(from_before, ((0, 0), (0, atoms_here - HALO), (0, 0)))
    upper = jnp.pad(from_after, ((0, 0), (atoms_here - HALO, 0), (0, 0)))
    return center + lower + upper


def on_device(
    atom_state,
    atom_token,
    window_valid,
    attend_gain,
    project_weight,
    output_weight,
    token_bias,
    transit_gain,
    transit_weight,
    return_weight,
    cotangent,
):
    channels = atom_state.shape[2]
    atoms_here = atom_state.shape[1]
    query_ids = token_codes(atom_token, window_valid)
    ext_ids = with_halo(query_ids, (("atom", 0),), HALO)
    normed = normalize(atom_state, attend_gain).astype(jnp.bfloat16)
    query_part = project_weight[:, :channels]
    pair_part = project_weight[:, channels:]
    ext_normed = with_halo(normed, (("atom", 1),), HALO)
    queries = jnp.dot(normed, query_part, preferred_element_type=jnp.float32).astype(jnp.bfloat16)
    ext_pairs = jnp.dot(ext_normed, pair_part, preferred_element_type=jnp.float32).astype(
        jnp.bfloat16
    )

    def forward_one(operands):
        query_rows, pair_rows = operands
        return attend(
            query_rows.astype(jnp.float32),
            pair_rows.astype(jnp.float32),
            query_ids,
            ext_ids,
            token_bias,
        )

    attended = lax.map(forward_one, (queries, ext_pairs)).astype(jnp.bfloat16)
    residual = (
        atom_state.astype(jnp.float32)
        + jnp.dot(attended, output_weight, preferred_element_type=jnp.float32)
    ).astype(jnp.bfloat16)
    transit_in = normalize(residual, transit_gain).astype(jnp.bfloat16)
    both_parts = jnp.dot(transit_in, transit_weight, preferred_element_type=jnp.float32)
    gate_part = both_parts[:, :, :TRANS]
    up_part = both_parts[:, :, TRANS:]
    gated = (jax.nn.silu(gate_part) * up_part).astype(jnp.bfloat16)
    block_out = (
        residual.astype(jnp.float32)
        + jnp.dot(gated, return_weight, preferred_element_type=jnp.float32)
    ).astype(jnp.bfloat16)
    grad_return = jnp.einsum("sai,sac->ic", gated, cotangent, preferred_element_type=jnp.float32)
    back_gated = jnp.einsum(
        "sac,ic->sai", cotangent, return_weight, preferred_element_type=jnp.float32
    )
    sigmoid_gate = jax.nn.sigmoid(gate_part)
    back_gate = back_gated * up_part * sigmoid_gate * (1.0 + gate_part * (1.0 - sigmoid_gate))
    back_up = back_gated * gate_part * sigmoid_gate
    back_hidden = jnp.concatenate([back_gate, back_up], axis=-1).astype(jnp.bfloat16)
    grad_transit = jnp.einsum(
        "sac,sae->ce", transit_in, back_hidden, preferred_element_type=jnp.float32
    )
    back_transit = jnp.einsum(
        "sae,ce->sac", back_hidden, transit_weight, preferred_element_type=jnp.float32
    )
    _, pull_second = jax.vjp(normalize, residual.astype(jnp.float32), transit_gain)
    back_res_norm, grad_transit_gain = pull_second(back_transit)
    back_residual = cotangent.astype(jnp.float32) + back_res_norm
    back_res16 = back_residual.astype(jnp.bfloat16)
    grad_output = jnp.einsum(
        "sac,sae->ce", attended, back_res16, preferred_element_type=jnp.float32
    )
    back_attended = jnp.einsum(
        "sae,ce->sac", back_res16, output_weight, preferred_element_type=jnp.float32
    )

    def backward_one(operands):
        query_rows, pair_rows, back_rows = operands

        def local_attend(query_in, pairs_in, bias_in):
            return attend(query_in, pairs_in, query_ids, ext_ids, bias_in)

        _, pull_attend = jax.vjp(
            local_attend, query_rows.astype(jnp.float32), pair_rows.astype(jnp.float32), token_bias
        )
        return pull_attend(back_rows)

    back_queries, back_ext, bias_parts = lax.map(backward_one, (queries, ext_pairs, back_attended))
    grad_bias = jnp.sum(bias_parts, axis=0)
    grad_query = jnp.einsum(
        "sac,sae->ce", normed.astype(jnp.float32), back_queries, precision=PRECISE
    )
    grad_pairs = jnp.einsum(
        "sac,sae->ce", ext_normed.astype(jnp.float32), back_ext, precision=PRECISE
    )
    grad_project = jnp.concatenate([grad_query, grad_pairs], axis=1)
    back_ext_normed = jnp.einsum(
        "sae,ce->sac", back_ext, pair_part.astype(jnp.float32), precision=PRECISE
    )
    from_before = passed_along(
        back_ext_normed[:, HALO + atoms_here :].astype(jnp.bfloat16), "atom", 1
    ).astype(jnp.float32)
    from_after = passed_along(back_ext_normed[:, :HALO].astype(jnp.bfloat16), "atom", -1).astype(
        jnp.float32
    )
    own_rows = back_ext_normed[:, HALO : HALO + atoms_here] + jnp.einsum(
        "sae,ce->sac", back_queries, query_part.astype(jnp.float32), precision=PRECISE
    )
    back_normed = place_rims(own_rows, from_before, from_after)
    _, pull_first = jax.vjp(normalize, atom_state.astype(jnp.float32), attend_gain)
    back_state_norm, grad_attend_gain = pull_first(back_normed)
    state_grad = (back_residual + back_state_norm).astype(jnp.bfloat16)
    gradients = (
        grad_attend_gain,
        grad_project,
        grad_output,
        grad_bias,
        grad_transit_gain,
        grad_transit,
        grad_return,
    )
    totals = lax.psum(
        (
            gradients[0],
            gradients[1],
            gradients[2],
            gradients[3],
            gradients[4],
            gradients[5],
            gradients[6],
        ),
        ("samp", "atom"),
    )
    squares = sum((jnp.sum(member * member) for member in totals))
    factor = CLIP_NORM / jnp.sqrt(squares + CLIP_NORM * CLIP_NORM)
    clipped = tuple((member * factor for member in totals))
    return (
        block_out,
        state_grad,
        clipped[0],
        clipped[1],
        clipped[2],
        clipped[3],
        clipped[4],
        clipped[5],
        clipped[6],
    )


def solution(mesh):
    return jax.shard_map(
        on_device,
        mesh=mesh,
        in_specs=(
            P("samp", "atom", None),
            P("atom"),
            P("atom"),
            P(),
            P(),
            P(),
            P(),
            P(),
            P(),
            P(),
            P("samp", "atom", None),
        ),
        out_specs=(
            P("samp", "atom", None),
            P("samp", "atom", None),
            P(),
            P(),
            P(),
            P(),
            P(),
            P(),
            P(),
        ),
        check_vma=False,
    )
```

profile of v0, /device:TPU:0, one launch (start us, length us, event | category | flops | bytes accessed | tf_op | source)
XLA Modules:
  0.0 380.1 jit_solution(13928921964016010154)
XLA Ops:
  8.9 2.4 collective-permute-start.2
  16.6 5.1 %collective-permute-start = (bf16[4,48,128]{2,1,0:T(8,128)(2,1)S(1)}, bf16[4,48,128]{2,1,0:T(8,128)(2,1)S(1)}, u32[]{:S(2)}, u32[]{:S(2)}) collective-permute-start(bf16[4,48,128]{2,1,0:T(8,128)(2,1)S(1)} %get-tuple-element.304), channel_id=1, source_target_pairs={{0,1},{1,2},{2,3},{3,4},{4,5},{5,6},{6,7},{8,9},{9,10},{10,11},{11... | collective-permute-start | bytes 147464 | tf_op jit(solution)/shard_map/ppermute | solution.py:25
  27.4 67.5 %while.30 = (s32[]{:T(128)}, bf16[4,320,128]{2,1,0:T(8,128)(2,1)}, bf16[4,416,256]{2,1,0:T(8,128)(2,1)}, s32[10,1,1,128]{3,0,2,1:T(8,128)S(1)}, bf16[4,320,128]{...) while((s32[]{:T(128)}, bf16[4,320,128]{2,1,0:T(8,128)(2,1)}, ...), condition=%wide.region_5.6_spmd.clone, body=%wide.region_2.5_spmd.sunk.clone | while | flops 128473856 | bytes 16410097 | solution.py:127
  33.0 2.4 copy.101
  36.9 2.8 pad_maximum_fusion.13
  49.9 2.4 copy.101
  53.8 2.8 pad_maximum_fusion.13
  66.7 2.4 copy.101
  70.7 2.8 pad_maximum_fusion.13
  83.6 2.4 copy.101
  87.5 2.8 pad_maximum_fusion.13
  106.7 102.9 %while.31 = (s32[]{:T(128)}, f32[4,320,128]{2,1,0:T(8,128)}, f32[4,416,256]{2,1,0:T(8,128)}, f32[4,4]{1,0:T(4,128)S(1)}, s32[10,1,1,128]{3,0,2,1:T(8,128)S(1)}, ...) while((s32[]{:T(128)}, f32[4,320,128]{2,1,0:T(8,128)}, ...), condition=%wide.region_15.16_spmd.clone, body=%wide.region_10.15_spmd.sunk.clone | while | flops 319997184 | bytes 31044328 | solution.py:177
  114.3 2.4 copy.108
  116.7 2.4 copy.109
  119.2 2.8 pad_maximum_fusion.14
  139.9 2.4 copy.108
  142.4 2.4 copy.109
  144.8 2.8 pad_maximum_fusion.14
  165.6 2.4 copy.108
  168.1 2.4 copy.109
  170.5 2.8 pad_maximum_fusion.14
  191.3 2.4 copy.108
  193.7 2.4 copy.109
  196.2 2.8 pad_maximum_fusion.14
  209.6 2.5 fusion.84
  212.7 4.7 %collective-permute-start.4 = (bf16[4,48,128]{2,1,0:T(8,128)(2,1)S(1)}, bf16[4,48,128]{2,1,0:T(8,128)(2,1)S(1)}, u32[]{:S(2)}, u32[]{:S(2)}) collective-permute-start(bf16[4,48,128]{2,1,0:T(8,128)(2,1)S(1)} %get-tuple-element.302), channel_id=1, source_target_pairs={{0,1},{1,2},{2,3},{3,4},{4,5},{5,6},{6,7},{8,9},{9,10},{10,11},{11... | collective-permute-start | bytes 147464 | tf_op jit(solution)/shard_map/ppermute | solution.py:34
  221.2 1.8 fusion.42
  223.9 44.4 %all-reduce.8 = (f32[128]{0:T(128)S(1)}, f32[4]{0:T(128)S(1)}, f32[128]{0:T(128)S(1)}) all-reduce(f32[128]{0:T(128)S(1)} %get-tuple-element.226, f32[4]{0:T(128)S(1)} %reduce_sum.232, f32[128]{0:T(128)S(1)} %copy-done.29), channel_id=1, replica_groups=mesh['samp'=4,'atom'=8] {'samp','atom'}, use_global_device_ids=true, to_apply=%region_19.20 | all-reduce | flops 260 | bytes 2080 | tf_op jit(solution)/shard_map/psum | solution.py:211
  270.2 1.7 add_convert_fusion
  271.9 84.5 %all-reduce.12.cloned.1.call-done = (f32[128,384]{1,0:T(8,128)}, f32[128,128]{1,0:T(8,128)}, f32[128,512]{1,0:T(8,128)}, f32[256,128]{1,0:T(8,128)}) async-done(((f32[128,384]{1,0:T(8,128)}, f32[128,128]{1,0:T(8,128)}, f32[128,512]{1,0:T(8,128)}, f32[256,128]{1,0:T(8,128)}), (f32[128,384]{1,0:T(8,128)}, f32[128,128]{1,0:T(8,128)}, f32[128,512]{1,0:T(8,128)}, ...) | async-done | bytes 655376 | tf_op jit(solution)/shard_map/psum | solution.py:211
  358.0 1.6 multiply_reduce_fusion.5
  369.2 1.7 broadcast_multiply_fusion
  (341 shorter events, 158.1 us)
Async XLA Ops:
  7.2 89.7 %copy-start = (bf16[128,512]{1,0:T(8,128)(2,1)S(1)}, bf16[128,512]{1,0:T(8,128)(2,1)}, u32[]{:S(2)}) copy-start(bf16[128,512]{1,0:T(8,128)(2,1)} %param.23) | copy-start | bytes 393220
  7.2 16.6 %copy-start.15 = (bf16[128,384]{1,0:T(8,128)(2,1)S(1)}, bf16[128,384]{1,0:T(8,128)(2,1)}, u32[]{:S(2)}) copy-start(bf16[128,384]{1,0:T(8,128)(2,1)} %param.19) | copy-start | bytes 294916
  7.2 349.2 %all-reduce.12.cloned.1.call-start = ((), (), s32[]{:S(2)}) async-start(), calls=%async_computation | async-start | bytes 1310720 | tf_op jit(solution)/shard_map/psum | solution.py:211
  8.9 15.9 %collective-permute-start.2 = (s32[48]{0:T(128)S(1)}, s32[48]{0:T(128)S(1)}, u32[]{:S(2)}, u32[]{:S(2)}) collective-permute-start(s32[48]{0:T(128)S(1)} %get-tuple-element.310), channel_id=1, source_target_pairs={{0,1},{1,2},{2,3},{3,4},{4,5},{5,6},{6,7},{8,9},{9,10},{10,11},{11... | collective-permute-start | bytes 584 | tf_op jit(solution)/shard_map/ppermute | solution.py:25
  11.3 13.5 %collective-permute-start.3 = (s32[48]{0:T(128)S(1)}, s32[48]{0:T(128)S(1)}, u32[]{:S(2)}, u32[]{:S(2)}) collective-permute-start(s32[48]{0:T(128)S(1)} %get-tuple-element.311), channel_id=1, source_target_pairs={{1,0},{2,1},{3,2},{4,3},{5,4},{6,5},{7,6},{9,8},{10,9},{11,10},{12... | collective-permute-start | bytes 584 | tf_op jit(solution)/shard_map/ppermute | solution.py:26
  16.6 10.8 %copy-start.5 = (bf16[4,320,128]{2,1,0:T(8,128)(2,1)}, bf16[4,320,128]{2,1,0:T(8,128)(2,1)S(1)}, u32[]{:S(2)}) copy-start(bf16[4,320,128]{2,1,0:T(8,128)(2,1)S(1)} %fusion.39) | copy-start | bytes 983044
  16.6 9.1 %collective-permute-start = (bf16[4,48,128]{2,1,0:T(8,128)(2,1)S(1)}, bf16[4,48,128]{2,1,0:T(8,128)(2,1)S(1)}, u32[]{:S(2)}, u32[]{:S(2)}) collective-permute-start(bf16[4,48,128]{2,1,0:T(8,128)(2,1)S(1)} %get-tuple-element.304), channel_id=1, source_target_pairs={{0,1},{1,2},{2,3},{3,4},{4,5},{5,6},{6,7},{8,9},{9,10},{10,11},{11... | collective-permute-start | bytes 147464 | tf_op jit(solution)/shard_map/ppermute | solution.py:25
  21.7 4.4 %collective-permute-start.1 = (bf16[4,48,128]{2,1,0:T(8,128)(2,1)S(1)}, bf16[4,48,128]{2,1,0:T(8,128)(2,1)S(1)}, u32[]{:S(2)}, u32[]{:S(2)}) collective-permute-start(bf16[4,48,128]{2,1,0:T(8,128)(2,1)S(1)} %get-tuple-element.305), channel_id=1, source_target_pairs={{1,0},{2,1},{3,2},{4,3},{5,4},{6,5},{7,6},{9,8},{10,9},{11,10},{12... | collective-permute-start | bytes 147464 | tf_op jit(solution)/shard_map/ppermute | solution.py:26
  25.7 1.6 copy-start.20
  26.1 1.3 copy-start.22
  94.8 2.0 copy-start.25
  104.4 2.3 copy-start.7
  104.4 2.3 copy-start.19
  104.4 2.3 copy-start.26
  122.1 1.3 copy-start.1
  147.7 1.3 copy-start.1
  209.6 2.5 copy-start.27
  209.6 2.5 copy-start.6
  209.6 2.5 copy-start.12
  209.6 9.2 %copy-start.4 = (f32[4,416,256]{2,1,0:T(8,128)S(1)}, f32[4,416,256]{2,1,0:T(8,128)}, u32[]{:S(2)}) copy-start(f32[4,416,256]{2,1,0:T(8,128)} %get-tuple-element.221) | copy-start | bytes 5111812
  209.6 9.3 %copy-start.21 = (bf16[4,48,128]{2,1,0:T(8,128)(2,1)S(1)}, bf16[4,48,128]{2,1,0:T(8,128)(2,1)}, u32[]{:S(2)}) copy-start(bf16[4,48,128]{2,1,0:T(8,128)(2,1)} %copy-done.20) | copy-start | bytes 147460
  209.6 9.3 %copy-start.23 = (bf16[4,48,128]{2,1,0:T(8,128)(2,1)S(1)}, bf16[4,48,128]{2,1,0:T(8,128)(2,1)}, u32[]{:S(2)}) copy-start(bf16[4,48,128]{2,1,0:T(8,128)(2,1)} %copy-done.22) | copy-start | bytes 147460
  212.7 7.8 %collective-permute-start.4 = (bf16[4,48,128]{2,1,0:T(8,128)(2,1)S(1)}, bf16[4,48,128]{2,1,0:T(8,128)(2,1)S(1)}, u32[]{:S(2)}, u32[]{:S(2)}) collective-permute-start(bf16[4,48,128]{2,1,0:T(8,128)(2,1)S(1)} %get-tuple-element.302), channel_id=1, source_target_pairs={{0,1},{1,2},{2,3},{3,4},{4,5},{5,6},{6,7},{8,9},{9,10},{10,11},{11... | collective-permute-start | bytes 147464 | tf_op jit(solution)/shard_map/ppermute | solution.py:34
  217.4 3.1 copy-start.28
  217.4 3.8 copy-start.3
  217.4 3.8 copy-start.24
  217.4 3.7 collective-permute-start.5
  221.2 2.8 copy-start.29
  221.2 49.1 %copy-start.8 = (f32[4,320,128]{2,1,0:T(8,128)S(1)}, f32[4,320,128]{2,1,0:T(8,128)}, u32[]{:S(2)}) copy-start(f32[4,320,128]{2,1,0:T(8,128)} %copy-done.7) | copy-start | bytes 1966084
  221.2 49.1 %copy-start.10 = (bf16[4,320,128]{2,1,0:T(8,128)(2,1)S(1)}, bf16[4,320,128]{2,1,0:T(8,128)(2,1)}, u32[]{:S(2)}) copy-start(bf16[4,320,128]{2,1,0:T(8,128)(2,1)} %param.25) | copy-start | bytes 983044
  356.4 15.1 %copy-start.14 = (f32[128,128]{1,0:T(8,128)S(1)}, f32[128,128]{1,0:T(8,128)}, u32[]{:S(2)}) copy-start(f32[128,128]{1,0:T(8,128)} %get-tuple-element.270) | copy-start | bytes 196612
  356.4 15.7 %copy-start.13 = (f32[128,384]{1,0:T(8,128)S(1)}, f32[128,384]{1,0:T(8,128)}, u32[]{:S(2)}) copy-start(f32[128,384]{1,0:T(8,128)} %get-tuple-element.269) | copy-start | bytes 589828
  (14 other events, 14.2 us)
Sparse Core Ops, SparseCore 0:
  220.6 135.7 all-reduce.11
where the time goes:
time: 383 us; the launch traced here: 380 us
  local copies, waits for them, and re-layouts  96.1 us (25%)
  waiting for transfers between devices  85.5 us (22%)
  other arithmetic  71.7 us (19%)
  matrix products  46 us (12%)
  blocking collectives  44.4 us (12%)
  between operations  19 us (5%)
  starting transfers between devices  16.2 us (4%)
    psum x1, waiting for transfers between devices, on_device(): lax.psum((gradients[0], gradients[1], gradients[2], gradients[3], gradien...  84.5 us
    slice x40, local copies, waits for them, and re-layouts, attend(): blocks[offset:offset + window_count]  57.2 us
    psum x1, blocking collectives, on_device(): lax.psum((gradients[0], gradients[1], gradients[2], gradients[3], gradien...  44.4 us
    concatenate x8, other arithmetic, attend(): jnp.concatenate([blocks[offset:offset + window_count] for offset in range...  22.3 us
    dot_general x12, matrix products, attend(): jnp.einsum('whqk,wkhd->wqhd', weights, values_in, precision=PRECISE)  16.2 us
    dot_general x16, matrix products, attend(): jnp.einsum('wqhd,wkhd->whqk', query_blocks, keys_in, precision=PRECISE)  12.1 us
    reduce_sum x7, other arithmetic, on_device(): squares = sum((jnp.sum(member * member) for member in totals))  8.12 us
  transfers between devices with their start and end apart: 7, of which 3 were waited for; matrix products, arithmetic and copies ran while one was open for 4% of the time, Pallas kernels for 0%

commit v1 on v0

v1 whole, which is shorter than its diff:
```python
import functools
import math

import jax
import jax.numpy as jnp
from jax import lax
from jax.experimental import pallas as pl
from jax.experimental.pallas import tpu as pltpu
from jax.sharding import PartitionSpec as P

HEADS = 4
TRANS = 256
QWIN = 32
KWIN = 128
HALO = 48
EPSILON = 1e-05
CLIP_NORM = 256.0
LANES = 128
SMALL_ROWS = 64
LOG2E = 1.0 / math.log(2.0)

F32 = jnp.float32
BF16 = jnp.bfloat16


def mm(a, b):
    return lax.dot_general(a, b, (((1,), (0,)), ((), ())), preferred_element_type=F32)


def mm_nt(a, b):
    return lax.dot_general(a, b, (((1,), (1,)), ((), ())), preferred_element_type=F32)


def mm_tn(a, b):
    return lax.dot_general(a, b, (((0,), (0,)), ((), ())), preferred_element_type=F32)


def row_mean(x):
    return jnp.sum(x, axis=-1, keepdims=True) * (1.0 / x.shape[-1])


def column_sum(x):
    return jnp.sum(x, axis=0, keepdims=True)


def split_norm(x):
    shifted = x - row_mean(x)
    inverse = lax.rsqrt(row_mean(shifted * shifted) + EPSILON)
    return shifted * inverse, inverse


def norm_grad(grad, unit, inverse):
    return inverse * (grad - row_mean(grad) - unit * row_mean(grad * unit))


def head_of_lane(rows):
    return lax.broadcasted_iota(jnp.int32, (rows, LANES), 1) // (LANES // HEADS)


def spread_heads(rows):
    head = head_of_lane(QWIN)
    return jnp.concatenate(
        [jnp.where(head == h, rows, jnp.zeros_like(rows)) for h in range(HEADS)], axis=0
    )


def gather_heads(rows):
    head = head_of_lane(QWIN)
    total = rows[:QWIN]
    for h in range(1, HEADS):
        total = jnp.where(head == h, rows[h * QWIN : (h + 1) * QWIN], total)
    return total


def block_kernel(
    flags,
    state,
    pair_rows,
    link_rows,
    own_codes,
    attend_gain,
    project_weight,
    output_weight,
    bias_row,
    transit_gain,
    transit_weight,
    return_weight,
    cot,
    block_out,
    back_norm,
    back_res,
    to_before,
    to_after,
    keep,
    send,
    norm_ext,
    unit_ext,
    q_all,
    k_all,
    v_all,
    codes,
    probs,
    att,
    d_att,
    dq_all,
    dk_all,
    dv_all,
    grads,
    bias_acc,
):
    samples, atoms, channels = state.shape
    ext = atoms + 2 * HALO
    windows = atoms // QWIN
    is_odd = flags[0] == 1
    halo_rows = samples * HALO
    scale = 1.0 / math.sqrt(channels // HEADS)

    before = jnp.where(is_odd, pair_rows[...], link_rows[...])
    after = jnp.where(is_odd, link_rows[...], pair_rows[...])

    def edge_codes(part):
        high = part[halo_rows : halo_rows + 1, :].astype(F32)
        low = part[halo_rows + 1 : halo_rows + 2, :].astype(F32)
        return high * 256.0 + low

    def down_lanes(row):
        return jnp.transpose(jnp.broadcast_to(row, (LANES, LANES)))

    codes[0:HALO, :] = down_lanes(edge_codes(before))[0:HALO]
    for i in range(own_codes.shape[0]):
        count = min(LANES, atoms - i * LANES)
        codes[HALO + i * LANES : HALO + i * LANES + count, :] = down_lanes(own_codes[i : i + 1, :])[0:count]
    codes[HALO + atoms : ext, :] = down_lanes(edge_codes(after))[0:HALO]

    grads[...] = jnp.zeros_like(grads)
    bias_acc[...] = jnp.zeros_like(bias_acc)
    dk_all[...] = jnp.zeros_like(dk_all)
    dv_all[...] = jnp.zeros_like(dv_all)

    gain_one = attend_gain[...]
    gain_two = transit_gain[...]
    for s in range(samples):
        rows = jnp.concatenate(
            [before[s * HALO : (s + 1) * HALO], state[s], after[s * HALO : (s + 1) * HALO]], axis=0
        ).astype(F32)
        unit, _ = split_norm(rows)
        unit_ext[s] = unit
        normed = (unit * gain_one).astype(BF16)
        norm_ext[s] = normed
        projected = mm(normed, project_weight[...]).astype(BF16)
        q_all[s] = projected[HALO : HALO + atoms, :channels]
        k_all[s] = projected[:, channels : 2 * channels]
        v_all[s] = projected[:, 2 * channels :]

    def window_mask(start):
        key_code = codes[pl.ds(start, KWIN), :]
        query = codes[pl.ds(start + HALO, QWIN), :]
        query_code = jnp.transpose(jnp.concatenate([query] * HEADS, axis=0))
        return key_code, key_code == query_code

    def forward_window(w, carry):
        start = pl.multiple_of(w * QWIN, QWIN)
        key_code, same = window_mask(start)
        offset = jnp.where(same, bias_row[...] * LOG2E, 0.0)
        offset = jnp.where(key_code > 0, offset, -1e30)
        for s in range(samples):
            queries = spread_heads(q_all[s, pl.ds(start, QWIN), :])
            keys = k_all[s, pl.ds(start, KWIN), :]
            values = v_all[s, pl.ds(start, KWIN), :]
            scores = mm_nt(keys, queries) * (scale * LOG2E) + offset
            weights = jnp.exp2(scores - jnp.max(scores, axis=0, keepdims=True))
            weights = weights * (1.0 / column_sum(weights))
            probs[w * samples + s] = weights
            outcome = gather_heads(mm_tn(weights.astype(BF16), values))
            att[s, pl.ds(start, QWIN), :] = outcome.astype(BF16)
        return carry

    lax.fori_loop(0, windows, forward_window, 0)

    def transition(s, gain_grad):
        attended = att[s]
        residual = (state[s].astype(F32) + mm(attended, output_weight[...])).astype(BF16)
        residual = residual.astype(F32)
        unit, inverse = split_norm(residual)
        transit_in = (unit * gain_two).astype(BF16)
        both = mm(transit_in, transit_weight[...])
        gate = both[:, :TRANS]
        up = both[:, TRANS:]
        sigmoid = 1.0 / (1.0 + jnp.exp(-gate))
        silu = gate * sigmoid
        gated = (silu * up).astype(BF16)
        block_out[s] = (residual + mm(gated, return_weight[...])).astype(BF16)
        cot16 = cot[s]
        back_gated = mm_nt(cot16, return_weight[...])
        back_gate = back_gated * up * sigmoid * (1.0 + gate * (1.0 - sigmoid))
        back_hidden = jnp.concatenate([back_gate, back_gated * silu], axis=1).astype(BF16)
        grads[pl.ds(8 * channels, TRANS), :] += mm_tn(gated, cot16)
        grad_transit = mm_tn(transit_in, back_hidden)
        for i in range(2 * TRANS // LANES):
            grads[pl.ds((4 + i) * channels, channels), :] += grad_transit[:, i * LANES : (i + 1) * LANES]
        back_transit = mm_nt(back_hidden, transit_weight[...])
        gain_grad = gain_grad + column_sum(back_transit * unit)
        back_residual = cot16.astype(F32) + norm_grad(back_transit * gain_two, unit, inverse)
        back_res[s] = back_residual
        back16 = back_residual.astype(BF16)
        grads[pl.ds(3 * channels, channels), :] += mm_tn(attended, back16)
        d_att[s] = mm_nt(back16, output_weight[...]).astype(BF16)
        return gain_grad

    zero_row = jnp.zeros((1, channels), F32)
    gain_grad_two = lax.fori_loop(0, samples, transition, zero_row)

    def backward_window(w, carry):
        start = pl.multiple_of(w * QWIN, QWIN)
        _, same = window_mask(start)
        bias_part = None
        for s in range(samples):
            queries = spread_heads(q_all[s, pl.ds(start, QWIN), :])
            back = spread_heads(d_att[s, pl.ds(start, QWIN), :])
            keys = k_all[s, pl.ds(start, KWIN), :]
            values = v_all[s, pl.ds(start, KWIN), :]
            weights = probs[w * samples + s]
            back_weights = mm_nt(values, back)
            weighted = weights * back_weights
            back_scores = weighted - weights * column_sum(weighted)
            bias_part = back_scores if bias_part is None else bias_part + back_scores
            scores16 = back_scores.astype(BF16)
            span = pl.ds(start, KWIN)
            dv_all[s, span, :] += mm(weights.astype(BF16), back)
            dk_all[s, span, :] += mm(scores16, queries)
            dq_all[s, pl.ds(start, QWIN), :] = gather_heads(mm_tn(scores16, keys))
        bias_acc[...] += jnp.where(same, bias_part, 0.0)
        return carry

    lax.fori_loop(0, windows, backward_window, 0)

    rim = jnp.zeros((HALO, channels), BF16)

    def projection(s, gain_grad):
        back_q = (dq_all[s] * scale).astype(BF16)
        back_q = jnp.concatenate([rim, back_q, rim], axis=0)
        back_k = (dk_all[s] * scale).astype(BF16)
        back_v = dv_all[s].astype(BF16)
        back_all = jnp.concatenate([back_q, back_k, back_v], axis=1)
        back_normed = mm_nt(back_all, project_weight[...])
        grad_project = mm_tn(norm_ext[s], back_all)
        for i in range(3):
            grads[pl.ds(i * channels, channels), :] += grad_project[:, i * LANES : (i + 1) * LANES]
        gain_grad = gain_grad + column_sum(back_normed * unit_ext[s])
        back_norm[s] = back_normed[HALO : HALO + atoms]
        rows = pl.ds(pl.multiple_of(s * HALO, HALO), HALO)
        to_before[rows, :] = back_normed[:HALO].astype(BF16)
        to_after[rows, :] = back_normed[HALO + atoms :].astype(BF16)
        return gain_grad

    gain_grad_one = lax.fori_loop(0, samples, projection, zero_row)

    tail = 8 * channels + TRANS
    grads[pl.ds(tail, 1), :] = gain_grad_one
    grads[pl.ds(tail + 1, 1), :] = gain_grad_two
    grads[pl.ds(tail + 2, 1), :] = column_sum(bias_acc[...])

    half = keep.shape[0]
    mine = flags[1]
    keep[...] = grads[pl.ds(pl.multiple_of(mine * half, 8), half), :].astype(BF16)
    send[...] = grads[pl.ds(pl.multiple_of((1 - mine) * half, 8), half), :].astype(BF16)


def rim_kernel(flags, state, gain, back_norm, back_res, pair_back, link_back, out):
    samples, atoms, channels = state.shape
    is_odd = flags[0] == 1
    from_before = jnp.where(is_odd, pair_back[...], link_back[...]).astype(F32)
    from_after = jnp.where(is_odd, link_back[...], pair_back[...]).astype(F32)
    for s in range(samples):
        grad = back_norm[s]
        part = slice(s * HALO, (s + 1) * HALO)
        grad = jnp.concatenate(
            [
                grad[:HALO] + from_before[part],
                grad[HALO : atoms - HALO],
                grad[atoms - HALO :] + from_after[part],
            ],
            axis=0,
        )
        unit, inverse = split_norm(state[s].astype(F32))
        out[s] = (back_res[s] + norm_grad(grad * gain[...], unit, inverse)).astype(BF16)


def clip_kernel(flags, own, other, attend, project, output, bias, transit_gain, transit, back):
    first = flags[0] == 0
    channels = LANES
    low = jnp.where(first, own[...], other[...]).astype(F32)
    high = jnp.where(first, other[...], own[...]).astype(F32)
    total = jnp.concatenate([low, high], axis=0)
    tail = 8 * channels + TRANS
    lane = lax.broadcasted_iota(jnp.int32, (1, LANES), 1)
    bias_row = total[tail + 2 : tail + 3]
    width = LANES // HEADS
    heads = jnp.zeros((1, LANES), F32)
    for h in range(HEADS):
        inside = (lane >= h * width) & (lane < (h + 1) * width)
        sum_h = jnp.sum(jnp.where(inside, bias_row, 0.0), axis=1, keepdims=True)
        heads = jnp.where(lane == h, sum_h, heads)
    plain = total[: tail + 2]
    squares = jnp.sum(column_sum(plain * plain) + heads * heads, axis=1, keepdims=True)
    factor = CLIP_NORM * lax.rsqrt(squares + CLIP_NORM * CLIP_NORM)
    for i in range(3):
        project[:, i * LANES : (i + 1) * LANES] = total[i * channels : (i + 1) * channels] * factor
    output[...] = total[3 * channels : 4 * channels] * factor
    for i in range(2 * TRANS // LANES):
        transit[:, i * LANES : (i + 1) * LANES] = total[(4 + i) * channels : (5 + i) * channels] * factor
    back[...] = total[8 * channels : 8 * channels + TRANS] * factor
    attend[...] = total[tail : tail + 1] * factor
    transit_gain[...] = total[tail + 1 : tail + 2] * factor
    bias[...] = heads * factor


def swap(value, axis, mask):
    return lax.ppermute(value, axis, [(i, i ^ mask) for i in range(lax.axis_size(axis))])


def pair_exchange(to_partner, to_link, axis):
    size = lax.axis_size(axis)
    links = [(i, i + 1) for i in range(1, size - 1, 2)]
    links = links + [(j, i) for i, j in links]
    return lax.ppermute(to_link, axis, links), swap(to_partner, axis, 1)


def token_codes(atom_token, window_valid):
    windows_here = window_valid.shape[0]
    slots = lax.broadcasted_iota(jnp.int32, (windows_here, QWIN), 1)
    inside = (slots < window_valid[:, None]).reshape(-1)
    return jnp.where(inside, atom_token + 1, 0)


def edge_pack(state, codes, at_end):
    samples, atoms, channels = state.shape
    start = jnp.where(at_end, atoms - HALO, 0)
    rows = lax.dynamic_slice_in_dim(state, start, HALO, axis=1).reshape(samples * HALO, channels)
    part = lax.dynamic_slice_in_dim(codes, start, HALO, axis=0)
    digits = jnp.stack([part // 256, part % 256]).astype(BF16)
    digits = jnp.pad(digits, ((0, 14), (0, channels - HALO)))
    return jnp.concatenate([rows, digits], axis=0)


def whole(*shape):
    return pl.BlockSpec(memory_space=pltpu.VMEM)


def call(kernel, operands, outs, scratch=(), flops=0):
    vmem = pl.BlockSpec(memory_space=pltpu.VMEM)
    smem = pl.BlockSpec(memory_space=pltpu.SMEM)
    moved = sum(x.size * x.dtype.itemsize for x in operands)
    return pl.pallas_call(
        kernel,
        out_shape=[jax.ShapeDtypeStruct(shape, dtype) for shape, dtype in outs],
        in_specs=[smem] + [vmem] * (len(operands) - 1),
        out_specs=[vmem] * len(outs),
        scratch_shapes=list(scratch),
        cost_estimate=pl.CostEstimate(flops=flops, bytes_accessed=moved, transcendentals=0),
        compiler_params=pltpu.CompilerParams(vmem_limit_bytes=48 * 1024 * 1024),
    )(*operands)


def on_device(
    atom_state,
    atom_token,
    window_valid,
    attend_gain,
    project_weight,
    output_weight,
    token_bias,
    transit_gain,
    transit_weight,
    return_weight,
    cotangent,
):
    samples, atoms, channels = atom_state.shape
    ext = atoms + 2 * HALO
    windows = atoms // QWIN
    place = lax.axis_index("atom")
    odd = place % 2
    codes = token_codes(atom_token, window_valid)
    link_rows, pair_rows = pair_exchange(
        edge_pack(atom_state, codes, odd == 0), edge_pack(atom_state, codes, odd == 1), "atom"
    )
    code_rows = -(-atoms // LANES)
    own_codes = jnp.pad(codes.astype(F32), (0, code_rows * LANES - atoms)).reshape(code_rows, LANES)
    flags = jnp.stack([odd, odd]).astype(jnp.int32)
    total_rows = 8 * channels + TRANS + SMALL_ROWS
    half = total_rows // 2
    halo_rows = samples * HALO
    block_out, back_norm, back_res, to_before, to_after, keep, send = call(
        block_kernel,
        (
            flags,
            atom_state,
            pair_rows,
            link_rows,
            own_codes,
            attend_gain.reshape(1, channels),
            project_weight,
            output_weight,
            jnp.repeat(token_bias, QWIN).reshape(1, HEADS * QWIN),
            transit_gain.reshape(1, channels),
            transit_weight,
            return_weight,
            cotangent,
        ),
        (
            ((samples, atoms, channels), BF16),
            ((samples, atoms, channels), F32),
            ((samples, atoms, channels), F32),
            ((halo_rows, channels), BF16),
            ((halo_rows, channels), BF16),
            ((half, channels), BF16),
            ((half, channels), BF16),
        ),
        (
            pltpu.VMEM((samples, ext, channels), BF16),
            pltpu.VMEM((samples, ext, channels), F32),
            pltpu.VMEM((samples, atoms, channels), BF16),
            pltpu.VMEM((samples, ext, channels), BF16),
            pltpu.VMEM((samples, ext, channels), BF16),
            pltpu.VMEM((ext, LANES), F32),
            pltpu.VMEM((windows * samples, KWIN, HEADS * QWIN), F32),
            pltpu.VMEM((samples, atoms, channels), BF16),
            pltpu.VMEM((samples, atoms, channels), BF16),
            pltpu.VMEM((samples, atoms, channels), F32),
            pltpu.VMEM((samples, ext, channels), F32),
            pltpu.VMEM((samples, ext, channels), F32),
            pltpu.VMEM((total_rows, channels), F32),
            pltpu.VMEM((KWIN, HEADS * QWIN), F32),
        ),
        flops=4_000_000_000,
    )

    got = swap(send, "atom", 1)
    part = keep + got
    x_bit = (place // 2) % 2
    quarter = half // 2
    mine = lax.dynamic_slice_in_dim(part, x_bit * quarter, quarter)
    theirs = lax.dynamic_slice_in_dim(part, (1 - x_bit) * quarter, quarter)
    sums = mine + swap(theirs, "atom", 2)
    mask = 4
    while mask < lax.axis_size("atom"):
        sums = sums + swap(sums, "atom", mask)
        mask *= 2
    mask = 1
    while mask < lax.axis_size("samp"):
        sums = sums + swap(sums, "samp", mask)
        mask *= 2
    other = swap(sums, "atom", 2)
    sums = jnp.where(
        x_bit == 0,
        jnp.concatenate([sums, other], axis=0),
        jnp.concatenate([other, sums], axis=0),
    )
    other = swap(sums, "atom", 1)
    clipped = call(
        clip_kernel,
        (flags, sums, other),
        (
            ((1, channels), F32),
            ((channels, 3 * channels), F32),
            ((channels, channels), F32),
            ((1, LANES), F32),
            ((1, channels), F32),
            ((channels, 2 * TRANS), F32),
            ((TRANS, channels), F32),
        ),
    )

    odd_here = odd == 1
    to_link = jnp.where(odd_here, to_after, to_before)
    to_partner = jnp.where(odd_here, to_before, to_after)
    link_back, pair_back = pair_exchange(to_partner, to_link, "atom")
    (state_grad,) = call(
        rim_kernel,
        (flags, atom_state, attend_gain.reshape(1, channels), back_norm, back_res, pair_back, link_back),
        (((samples, atoms, channels), BF16),),
        flops=100_000_000,
    )
    return (
        block_out,
        state_grad,
        clipped[0].reshape(channels),
        clipped[1],
        clipped[2],
        clipped[3][0, :HEADS],
        clipped[4].reshape(channels),
        clipped[5],
        clipped[6],
    )


def solution(mesh):
    return jax.shard_map(
        on_device,
        mesh=mesh,
        in_specs=(
            P("samp", "atom", None),
            P("atom"),
            P("atom"),
            P(),
            P(),
            P(),
            P(),
            P(),
            P(),
            P(),
            P("samp", "atom", None),
        ),
        out_specs=(
            P("samp", "atom", None),
            P("samp", "atom", None),
            P(),
            P(),
            P(),
            P(),
            P(),
            P(),
            P(),
        ),
        check_vma=False,
    )
```

time: 383 us -> 81.9 us (0.21)
  the two profiles are of different devices: /device:TPU:0 before, /device:TPU:27 now
where the time goes in v1:
time: 81.9 us; the launch traced here: 81.5 us
  Pallas kernels  34.2 us (42%)
  waiting for transfers between devices  25.9 us (32%)
  starting transfers between devices  13.1 us (16%)
  local copies, waits for them, and re-layouts  5.56 us (7%)
  other arithmetic  1.88 us (2%)
  between operations  0.85 us (1%)
    pallas_call x3, Pallas kernels, call(): pl.pallas_call(kernel, out_shape=[jax.ShapeDtypeStruct(shape, dtype) for...  34.2 us
    ppermute x9, waiting for transfers between devices, swap(): lax.ppermute(value, axis, [(i, i ^ mask) for i in range(lax.axis_size(axi...  20.2 us
    ppermute x9, starting transfers between devices, swap(): lax.ppermute(value, axis, [(i, i ^ mask) for i in range(lax.axis_size(axi...  7.15 us
    ppermute x2, starting transfers between devices, pair_exchange(): return (lax.ppermute(to_link, axis, links), swap(to_partner, axis, 1))  5.99 us
    ppermute x2, waiting for transfers between devices, pair_exchange(): return (lax.ppermute(to_link, axis, links), swap(to_partner, axis, 1))  5.75 us
    unnamed x18, local copies, waits for them, and re-layouts  3.94 us
  transfers between devices with their start and end apart: 11, of which 8 were waited for; matrix products, arithmetic and copies ran while one was open for 0% of the time, Pallas kernels for 3%

profile of v1, /device:TPU:27, one launch (start us, length us, event | category | flops | bytes accessed | tf_op | source)
XLA Modules:
  0.0 81.5 jit_solution(14994389175195716420)
XLA Ops:
  0.7 0.8 iota_compare_fusion.2
  1.4 0.1 lt.45
  1.5 0.7 fusion.15
  2.2 0.1 convert_bitcast_fusion
  2.3 0.8 %constant_dynamic-slice_fusion.1 = (bf16[4,48,128]{2,1,0:T(8,128)(2,1)S(1)}, bf16[4,48,128]{2,1,0:T(8,128)(2,1)S(1)}) fusion(bf16[4,320,128]{2,1,0:T(8,128)(2,1)} %state.3, s32[]{:T(128)S(6)} %select_n.79, s32[]{:T(128)S(6)} %select_n.75), kind=kLoop, calls=%fused_computation.33 | loop fusion | bytes 196616 | tf_op jit(solution)/shard_map/dynamic_slice | solution.py:339
  3.2 0.7 collective-permute-start
  4.0 3.0 %collective-permute-start.1 = (bf16[208,128]{1,0:T(8,128)(2,1)S(1)}, bf16[208,128]{1,0:T(8,128)(2,1)S(1)}, u32[]{:S(2)}, u32[]{:S(2)}) collective-permute-start(bf16[208,128]{1,0:T(8,128)(2,1)S(1)} %pad_maximum_fusion.1), channel_id=1, source_target_pairs={{1,2},{3,4},{5,6},{2,1},{4,3},{6,5},{9,10},{11,12},{13,14},{10,9},... | collective-permute-start | bytes 159752 | tf_op jit(solution)/shard_map/ppermute | solution.py:326
  7.1 0.1 pad_add_fusion.flags
  7.1 0.6 copy-done.8
  7.8 0.1 reshape_reshape.3.bias_row
  7.9 2.5 %collective-permute-done.1.link_rows = bf16[208,128]{1,0:T(8,128)(2,1)S(1)} collective-permute-done((bf16[208,128]{1,0:T(8,128)(2,1)S(1)}, bf16[208,128]{1,0:T(8,128)(2,1)S(1)}, u32[]{:S(2)}, u32[]{:S(2)}) %collective-permute-start.1) | collective-permute-done | bytes 53280 | tf_op jit(solution)/shard_map/ppermute | solution.py:326
  10.4 0.6 copy-done.1
  11.0 1.0 %copy-done.2 = bf16[4,320,128]{2,1,0:T(8,128)(2,1)S(1)} copy-done((bf16[4,320,128]{2,1,0:T(8,128)(2,1)S(1)}, bf16[4,320,128]{2,1,0:T(8,128)(2,1)}, u32[]{:S(2)}) %copy-start.2) | copy-done | bytes 327704
  12.0 0.9 %copy-done.4 = bf16[128,384]{1,0:T(8,128)(2,1)S(1)} copy-done((bf16[128,384]{1,0:T(8,128)(2,1)S(1)}, bf16[128,384]{1,0:T(8,128)(2,1)}, u32[]{:S(2)}) %copy-start.4) | copy-done | bytes 98328
  12.9 0.8 %copy-done.5 = bf16[256,128]{1,0:T(8,128)(2,1)S(1)} copy-done((bf16[256,128]{1,0:T(8,128)(2,1)S(1)}, bf16[256,128]{1,0:T(8,128)(2,1)}, u32[]{:S(2)}) %copy-start.5) | copy-done | bytes 65560
  13.7 30.3 %shard_map.178 = (bf16[4,320,128]{2,1,0:T(8,128)(2,1)}, f32[4,320,128]{2,1,0:T(8,128)S(1)}, f32[4,320,128]{2,1,0:T(8,128)S(1)}, bf16[192,128]{1,0:T(8,128)(2,1)S...) custom-call(s32[2]{0:T(128)S(1)} %pad_add_fusion.flags, ...), custom_call_target="tpu_custom_call" | custom-call | flops 4000000000 | bytes 1092616 | tf_op jit(solution)/shard_map/pallas_call | solution.py:354
  44.0 1.4 %collective-permute-done.4 = bf16[672,128]{1,0:T(8,128)(2,1)S(1)} collective-permute-done((bf16[672,128]{1,0:T(8,128)(2,1)S(1)}, bf16[672,128]{1,0:T(8,128)(2,1)S(1)}, u32[]{:S(2)}, u32[]{:S(2)}) %collective-permute-start.4) | collective-permute-done | bytes 172064 | tf_op jit(solution)/shard_map/ppermute | solution.py:319
  45.5 0.1 collective-permute-start.5
  45.6 3.9 %collective-permute-done.5 = bf16[336,128]{1,0:T(8,128)(2,1)S(1)} collective-permute-done((bf16[336,128]{1,0:T(8,128)(2,1)S(1)}, bf16[336,128]{1,0:T(8,128)(2,1)S(1)}, u32[]{:S(2)}, u32[]{:S(2)}) %collective-permute-start.5) | collective-permute-done | bytes 86048 | tf_op jit(solution)/shard_map/ppermute | solution.py:319
  49.6 3.3 %collective-permute-done.6 = bf16[336,128]{1,0:T(8,128)(2,1)S(1)} collective-permute-done((bf16[336,128]{1,0:T(8,128)(2,1)S(1)}, bf16[336,128]{1,0:T(8,128)(2,1)S(1)}, u32[]{:S(2)}, u32[]{:S(2)}) %collective-permute-start.6) | collective-permute-done | bytes 86048 | tf_op jit(solution)/shard_map/ppermute | solution.py:319
  53.0 0.2 collective-permute-start.7
  53.2 3.2 %collective-permute-done.7 = bf16[336,128]{1,0:T(8,128)(2,1)S(1)} collective-permute-done((bf16[336,128]{1,0:T(8,128)(2,1)S(1)}, bf16[336,128]{1,0:T(8,128)(2,1)S(1)}, u32[]{:S(2)}, u32[]{:S(2)}) %collective-permute-start.7) | collective-permute-done | bytes 86048 | tf_op jit(solution)/shard_map/ppermute | solution.py:319
  56.4 0.1 collective-permute-start.8
  56.5 5.0 %collective-permute-done.8 = bf16[336,128]{1,0:T(8,128)(2,1)S(1)} collective-permute-done((bf16[336,128]{1,0:T(8,128)(2,1)S(1)}, bf16[336,128]{1,0:T(8,128)(2,1)S(1)}, u32[]{:S(2)}, u32[]{:S(2)}) %collective-permute-start.8) | collective-permute-done | bytes 86048 | tf_op jit(solution)/shard_map/ppermute | solution.py:319
  61.6 0.4 collective-permute-start.9
  61.9 3.3 %collective-permute-done.9 = bf16[336,128]{1,0:T(8,128)(2,1)S(1)} collective-permute-done((bf16[336,128]{1,0:T(8,128)(2,1)S(1)}, bf16[336,128]{1,0:T(8,128)(2,1)S(1)}, u32[]{:S(2)}, u32[]{:S(2)}) %collective-permute-start.9) | collective-permute-done | bytes 86048 | tf_op jit(solution)/shard_map/ppermute | solution.py:319
  65.3 5.5 %collective-permute-start.10 = (bf16[672,128]{1,0:T(8,128)(2,1)S(1)}, bf16[672,128]{1,0:T(8,128)(2,1)S(1)}, u32[]{:S(2)}, u32[]{:S(2)}) collective-permute-start(bf16[672,128]{1,0:T(8,128)(2,1)S(1)} %maximum_select_fusion.own), channel_id=1, source_target_pairs={{0,1},{1,0},{2,3},{3,2},{4,5},{5,4},{6,7},{7,6},{8,9},{9,8},{10,11... | collective-permute-start | bytes 516104 | tf_op jit(solution)/shard_map/ppermute | solution.py:319
  70.8 3.0 %collective-permute-start.3 = (bf16[192,128]{1,0:T(8,128)(2,1)S(1)}, bf16[192,128]{1,0:T(8,128)(2,1)S(1)}, u32[]{:S(2)}, u32[]{:S(2)}) collective-permute-start(bf16[192,128]{1,0:T(8,128)(2,1)S(1)} %get-tuple-element.45), channel_id=1, source_target_pairs={{1,2},{3,4},{5,6},{2,1},{4,3},{6,5},{9,10},{11,12},{13,14},{10,9},... | collective-permute-start | bytes 147464 | tf_op jit(solution)/shard_map/ppermute | solution.py:326
  73.8 3.3 %collective-permute-done.3.link_back = bf16[192,128]{1,0:T(8,128)(2,1)S(1)} collective-permute-done((bf16[192,128]{1,0:T(8,128)(2,1)S(1)}, bf16[192,128]{1,0:T(8,128)(2,1)S(1)}, u32[]{:S(2)}, u32[]{:S(2)}) %collective-permute-start.3) | collective-permute-done | bytes 49184 | tf_op jit(solution)/shard_map/ppermute | solution.py:326
  77.1 2.2 %shard_map.179 = bf16[4,320,128]{2,1,0:T(8,128)(2,1)} custom-call(s32[2]{0:T(128)S(1)} %pad_add_fusion.flags, bf16[4,320,128]{2,1,0:T(8,128)(2,1)S(1)} %copy-done, f32[1,128]{1,0:T(1,128)S(1)} %bitcast.20, f32[4,320,128]{2,1,0:T(8,128)S(1)} %get-tuple-element.24.back_norm, f32[4,320,128]{2,1,0:T(8,128)S(1)} %get-tuple-element.25.back_res, ...), custom_call_target="tpu_custom_call" | custom-call | flops 100000000 | bytes 1737224 | tf_op jit(solution)/shard_map/pallas_call | solution.py:354
  79.3 1.7 %shard_map.180 = (f32[1,128]{1,0:T(1,128)}, f32[128,384]{1,0:T(8,128)}, f32[128,128]{1,0:T(8,128)}, f32[1,128]{1,0:T(1,128)S(1)}, f32[1,128]{1,0:T(1,128)}, /*index=5*/f32[128,512]{1,0:T(8,128)}, f32[256,128]{1,0:T(8,128)}) custom-call(s32[2]{0:T(128)S(1)} %pad_add_fusion.flags, bf16[672,128]{1,0:T(8,128)(2,1)S(1)} %maximum_select_fusion.own, ...), custom_call_target="tpu_custom_call" | custom-call | bytes 344072 | tf_op jit(solution)/shard_map/pallas_call | solution.py:354
  81.0 0.5 slice_bitcast_fusion
  (35 shorter events, 0.5 us)
Async XLA Ops:
  0.6 9.7 %copy-start = (bf16[4,320,128]{2,1,0:T(8,128)(2,1)S(1)}, bf16[4,320,128]{2,1,0:T(8,128)(2,1)}, u32[]{:S(2)}) copy-start(bf16[4,320,128]{2,1,0:T(8,128)(2,1)} %state.3) | copy-start | bytes 983044
  3.2 7.2 %copy-start.3 = (bf16[128,512]{1,0:T(8,128)(2,1)S(1)}, bf16[128,512]{1,0:T(8,128)(2,1)}, u32[]{:S(2)}) copy-start(bf16[128,512]{1,0:T(8,128)(2,1)} %transit_weight.1) | copy-start | bytes 393220
  3.2 4.7 %collective-permute-start = (bf16[208,128]{1,0:T(8,128)(2,1)S(1)}, bf16[208,128]{1,0:T(8,128)(2,1)S(1)}, u32[]{:S(2)}, u32[]{:S(2)}) collective-permute-start(bf16[208,128]{1,0:T(8,128)(2,1)S(1)} %pad_maximum_fusion), channel_id=1, source_target_pairs={{0,1},{1,0},{2,3},{3,2},{4,5},{5,4},{6,7},{7,6},{8,9},{9,8},{10,11... | collective-permute-start | bytes 159752 | tf_op jit(solution)/shard_map/ppermute | solution.py:319
  4.0 6.4 %copy-start.6 = (bf16[128,128]{1,0:T(8,128)(2,1)S(1)}, bf16[128,128]{1,0:T(8,128)(2,1)}, u32[]{:S(2)}) copy-start(bf16[128,128]{1,0:T(8,128)(2,1)} %output_weight.1) | copy-start | bytes 98308
  4.0 6.4 %collective-permute-start.1 = (bf16[208,128]{1,0:T(8,128)(2,1)S(1)}, bf16[208,128]{1,0:T(8,128)(2,1)S(1)}, u32[]{:S(2)}, u32[]{:S(2)}) collective-permute-start(bf16[208,128]{1,0:T(8,128)(2,1)S(1)} %pad_maximum_fusion.1), channel_id=1, source_target_pairs={{1,2},{3,4},{5,6},{2,1},{4,3},{6,5},{9,10},{11,12},{13,14},{10,9},... | collective-permute-start | bytes 159752 | tf_op jit(solution)/shard_map/ppermute | solution.py:326
  7.0 0.7 copy-start.8
  10.3 0.7 copy-start.1
  10.3 0.7 copy-start.7
  11.0 1.0 %copy-start.2 = (bf16[4,320,128]{2,1,0:T(8,128)(2,1)S(1)}, bf16[4,320,128]{2,1,0:T(8,128)(2,1)}, u32[]{:S(2)}) copy-start(bf16[4,320,128]{2,1,0:T(8,128)(2,1)} %cot.1) | copy-start | bytes 983044
  12.0 0.9 %copy-start.4 = (bf16[128,384]{1,0:T(8,128)(2,1)S(1)}, bf16[128,384]{1,0:T(8,128)(2,1)}, u32[]{:S(2)}) copy-start(bf16[128,384]{1,0:T(8,128)(2,1)} %project_weight.1) | copy-start | bytes 294916
  12.9 0.8 %copy-start.5 = (bf16[256,128]{1,0:T(8,128)(2,1)S(1)}, bf16[256,128]{1,0:T(8,128)(2,1)}, u32[]{:S(2)}) copy-start(bf16[256,128]{1,0:T(8,128)(2,1)} %return_weight.1) | copy-start | bytes 196612
  44.0 1.4 %collective-permute-start.4 = (bf16[672,128]{1,0:T(8,128)(2,1)S(1)}, bf16[672,128]{1,0:T(8,128)(2,1)S(1)}, u32[]{:S(2)}, u32[]{:S(2)}) collective-permute-start(bf16[672,128]{1,0:T(8,128)(2,1)S(1)} %get-tuple-element.29), channel_id=1, source_target_pairs={{0,1},{1,0},{2,3},{3,2},{4,5},{5,4},{6,7},{7,6},{8,9},{9,8},{10,11... | collective-permute-start | bytes 516104 | tf_op jit(solution)/shard_map/ppermute | solution.py:319
  45.5 4.0 %collective-permute-start.5 = (bf16[336,128]{1,0:T(8,128)(2,1)S(1)}, bf16[336,128]{1,0:T(8,128)(2,1)S(1)}, u32[]{:S(2)}, u32[]{:S(2)}) collective-permute-start(bf16[336,128]{1,0:T(8,128)(2,1)S(1)} %constant_dynamic-slice_fusion), channel_id=1, source_target_pairs={{0,2},{1,3},{2,0},{3,1},{4,6},{5,7},{6,4},{7,5},{8,10},{9,11},{10,... | collective-permute-start | bytes 258056 | tf_op jit(solution)/shard_map/ppermute | solution.py:319
  49.6 3.4 %collective-permute-start.6 = (bf16[336,128]{1,0:T(8,128)(2,1)S(1)}, bf16[336,128]{1,0:T(8,128)(2,1)S(1)}, u32[]{:S(2)}, u32[]{:S(2)}) collective-permute-start(bf16[336,128]{1,0:T(8,128)(2,1)S(1)} %dynamic-slice_add_fusion), channel_id=1, source_target_pairs={{0,4},{1,5},{2,6},{3,7},{4,0},{5,1},{6,2},{7,3},{8,12},{9,13},{10,... | collective-permute-start | bytes 258056 | tf_op jit(solution)/shard_map/ppermute | solution.py:319
  53.0 3.4 %collective-permute-start.7 = (bf16[336,128]{1,0:T(8,128)(2,1)S(1)}, bf16[336,128]{1,0:T(8,128)(2,1)S(1)}, u32[]{:S(2)}, u32[]{:S(2)}) collective-permute-start(bf16[336,128]{1,0:T(8,128)(2,1)S(1)} %add.67), channel_id=1, source_target_pairs={{0,8},{8,0},{16,24},{24,16},{1,9},{9,1},{17,25},{25,17},{2,10},{10... | collective-permute-start | bytes 258056 | tf_op jit(solution)/shard_map/ppermute | solution.py:319
  56.4 5.1 %collective-permute-start.8 = (bf16[336,128]{1,0:T(8,128)(2,1)S(1)}, bf16[336,128]{1,0:T(8,128)(2,1)S(1)}, u32[]{:S(2)}, u32[]{:S(2)}) collective-permute-start(bf16[336,128]{1,0:T(8,128)(2,1)S(1)} %add.68), channel_id=1, source_target_pairs={{0,16},{8,24},{16,0},{24,8},{1,17},{9,25},{17,1},{25,9},{2,18},{10... | collective-permute-start | bytes 258056 | tf_op jit(solution)/shard_map/ppermute | solution.py:319
  61.6 3.7 %collective-permute-start.9 = (bf16[336,128]{1,0:T(8,128)(2,1)S(1)}, bf16[336,128]{1,0:T(8,128)(2,1)S(1)}, u32[]{:S(2)}, u32[]{:S(2)}) collective-permute-start(bf16[336,128]{1,0:T(8,128)(2,1)S(1)} %add.69), channel_id=1, source_target_pairs={{0,2},{1,3},{2,0},{3,1},{4,6},{5,7},{6,4},{7,5},{8,10},{9,11},{10,... | collective-permute-start | bytes 258056 | tf_op jit(solution)/shard_map/ppermute | solution.py:319
  65.3 14.0 %collective-permute-start.10 = (bf16[672,128]{1,0:T(8,128)(2,1)S(1)}, bf16[672,128]{1,0:T(8,128)(2,1)S(1)}, u32[]{:S(2)}, u32[]{:S(2)}) collective-permute-start(bf16[672,128]{1,0:T(8,128)(2,1)S(1)} %maximum_select_fusion.own), channel_id=1, source_target_pairs={{0,1},{1,0},{2,3},{3,2},{4,5},{5,4},{6,7},{7,6},{8,9},{9,8},{10,11... | collective-permute-start | bytes 516104 | tf_op jit(solution)/shard_map/ppermute | solution.py:319
  70.8 6.3 %collective-permute-start.3 = (bf16[192,128]{1,0:T(8,128)(2,1)S(1)}, bf16[192,128]{1,0:T(8,128)(2,1)S(1)}, u32[]{:S(2)}, u32[]{:S(2)}) collective-permute-start(bf16[192,128]{1,0:T(8,128)(2,1)S(1)} %get-tuple-element.45), channel_id=1, source_target_pairs={{1,2},{3,4},{5,6},{2,1},{4,3},{6,5},{9,10},{11,12},{13,14},{10,9},... | collective-permute-start | bytes 147464 | tf_op jit(solution)/shard_map/ppermute | solution.py:326
  73.8 3.3 %collective-permute-start.2 = (bf16[192,128]{1,0:T(8,128)(2,1)S(1)}, bf16[192,128]{1,0:T(8,128)(2,1)S(1)}, u32[]{:S(2)}, u32[]{:S(2)}) collective-permute-start(bf16[192,128]{1,0:T(8,128)(2,1)S(1)} %get-tuple-element.46), channel_id=1, source_target_pairs={{0,1},{1,0},{2,3},{3,2},{4,5},{5,4},{6,7},{7,6},{8,9},{9,8},{10,11... | collective-permute-start | bytes 147464 | tf_op jit(solution)/shard_map/ppermute | solution.py:319

commit v2 on v1

--- a/solution.py
+++ b/solution.py
@@ -16,7 +16,8 @@
 EPSILON = 1e-05
 CLIP_NORM = 256.0
 LANES = 128
-SMALL_ROWS = 64
+GROUP = 2
+SLOT = 16
 LOG2E = 1.0 / math.log(2.0)
 
 F32 = jnp.float32
@@ -72,27 +73,45 @@
     return total
 
 
+def bias_slots(row, place, rows):
+    slot_lane = lax.broadcasted_iota(jnp.int32, (1, LANES), 1)
+    width = LANES // HEADS
+    line = jnp.zeros((1, LANES), F32)
+    for h in range(HEADS):
+        inside = (slot_lane // width) == h
+        total = jnp.sum(jnp.where(inside, row, 0.0), axis=1, keepdims=True)
+        high = total.astype(BF16).astype(F32)
+        middle = (total - high).astype(BF16).astype(F32)
+        low = total - high - middle
+        for digit, value in enumerate((high, middle, low)):
+            line = jnp.where(slot_lane % SLOT == h * 4 + digit, value, line)
+    per_row = LANES // SLOT
+    lane = lax.broadcasted_iota(jnp.int32, (rows, LANES), 1)
+    row_index = lax.broadcasted_iota(jnp.int32, (rows, LANES), 0)
+    here = (lane // SLOT == place % per_row) & (row_index == place // per_row)
+    return jnp.where(here, jnp.broadcast_to(line, (rows, LANES)), 0.0)
+
+
 def block_kernel(
-    flags,
-    state,
+    own_codes,
     pair_rows,
     link_rows,
-    own_codes,
     attend_gain,
+    bias_row,
+    transit_gain,
+    state,
     project_weight,
     output_weight,
-    bias_row,
-    transit_gain,
     transit_weight,
     return_weight,
     cot,
     block_out,
     back_norm,
     back_res,
-    to_before,
-    to_after,
-    keep,
-    send,
+    to_partner,
+    to_link,
+    packed_keep,
+    packed_send,
     norm_ext,
     unit_ext,
     q_all,
@@ -111,10 +130,11 @@
     samples, atoms, channels = state.shape
     ext = atoms + 2 * HALO
     windows = atoms // QWIN
-    is_odd = flags[0] == 1
+    place = lax.axis_index("atom")
+    places = lax.axis_size("atom")
+    is_odd = place % 2 == 1
     halo_rows = samples * HALO
     scale = 1.0 / math.sqrt(channels // HEADS)
-
     before = jnp.where(is_odd, pair_rows[...], link_rows[...])
     after = jnp.where(is_odd, link_rows[...], pair_rows[...])
 
@@ -126,11 +146,14 @@
     def down_lanes(row):
         return jnp.transpose(jnp.broadcast_to(row, (LANES, LANES)))
 
-    codes[0:HALO, :] = down_lanes(edge_codes(before))[0:HALO]
+    first_code = jnp.where(place == 0, 0.0, edge_codes(before))
+    last_code = jnp.where(place == places - 1, 0.0, edge_codes(after))
+    last_lane = (atoms - HALO) % LANES
+    codes[0:HALO, :] = down_lanes(first_code)[last_lane : last_lane + HALO]
     for i in range(own_codes.shape[0]):
         count = min(LANES, atoms - i * LANES)
         codes[HALO + i * LANES : HALO + i * LANES + count, :] = down_lanes(own_codes[i : i + 1, :])[0:count]
-    codes[HALO + atoms : ext, :] = down_lanes(edge_codes(after))[0:HALO]
+    codes[HALO + atoms : ext, :] = down_lanes(last_code)[0:HALO]
 
     grads[...] = jnp.zeros_like(grads)
     bias_acc[...] = jnp.zeros_like(bias_acc)
@@ -158,24 +181,40 @@
         query_code = jnp.transpose(jnp.concatenate([query] * HEADS, axis=0))
         return key_code, key_code == query_code
 
-    def forward_window(w, carry):
-        start = pl.multiple_of(w * QWIN, QWIN)
-        key_code, same = window_mask(start)
-        offset = jnp.where(same, bias_row[...] * LOG2E, 0.0)
-        offset = jnp.where(key_code > 0, offset, -1e30)
-        for s in range(samples):
-            queries = spread_heads(q_all[s, pl.ds(start, QWIN), :])
-            keys = k_all[s, pl.ds(start, KWIN), :]
-            values = v_all[s, pl.ds(start, KWIN), :]
-            scores = mm_nt(keys, queries) * (scale * LOG2E) + offset
-            weights = jnp.exp2(scores - jnp.max(scores, axis=0, keepdims=True))
+    def group_units(g):
+        starts = [pl.multiple_of((g * GROUP + i) * QWIN, QWIN) for i in range(GROUP)]
+        return starts, [(i, s) for i in range(GROUP) for s in range(samples)]
+
+    def forward_group(g, carry):
+        starts, units = group_units(g)
+        scores = [
+            mm_nt(
+                k_all[s, pl.ds(starts[i], KWIN), :],
+                spread_heads(q_all[s, pl.ds(starts[i], QWIN), :]),
+            )
+            for i, s in units
+        ]
+        offsets = []
+        for start in starts:
+            key_code, same = window_mask(start)
+            offset = jnp.where(same, bias_row[...] * LOG2E, 0.0)
+            offsets.append(jnp.where(key_code > 0, offset, -1e30))
+        packed = []
+        for (i, s), score in zip(units, scores):
+            score = score * (scale * LOG2E) + offsets[i]
+            weights = jnp.exp2(score - jnp.max(score, axis=0, keepdims=True))
             weights = weights * (1.0 / column_sum(weights))
-            probs[w * samples + s] = weights
-            outcome = gather_heads(mm_tn(weights.astype(BF16), values))
-            att[s, pl.ds(start, QWIN), :] = outcome.astype(BF16)
+            probs[(g * GROUP + i) * samples + s] = weights
+            packed.append(weights.astype(BF16))
+        outcomes = [
+            mm_tn(weights, v_all[s, pl.ds(starts[i], KWIN), :])
+            for (i, s), weights in zip(units, packed)
+        ]
+        for (i, s), outcome in zip(units, outcomes):
+            att[s, pl.ds(starts[i], QWIN), :] = gather_heads(outcome).astype(BF16)
         return carry
 
-    lax.fori_loop(0, windows, forward_window, 0)
+    lax.fori_loop(0, windows // GROUP, forward_group, 0)
 
     def transition(s, gain_grad):
         attended = att[s]
@@ -210,29 +249,42 @@
     zero_row = jnp.zeros((1, channels), F32)
     gain_grad_two = lax.fori_loop(0, samples, transition, zero_row)
 
-    def backward_window(w, carry):
-        start = pl.multiple_of(w * QWIN, QWIN)
-        _, same = window_mask(start)
-        bias_part = None
-        for s in range(samples):
-            queries = spread_heads(q_all[s, pl.ds(start, QWIN), :])
-            back = spread_heads(d_att[s, pl.ds(start, QWIN), :])
-            keys = k_all[s, pl.ds(start, KWIN), :]
-            values = v_all[s, pl.ds(start, KWIN), :]
-            weights = probs[w * samples + s]
-            back_weights = mm_nt(values, back)
-            weighted = weights * back_weights
+    def backward_group(g, carry):
+        starts, units = group_units(g)
+        backs = [spread_heads(d_att[s, pl.ds(starts[i], QWIN), :]) for i, s in units]
+        back_weights = [
+            mm_nt(v_all[s, pl.ds(starts[i], KWIN), :], back) for (i, s), back in zip(units, backs)
+        ]
+        packed = []
+        scores16 = []
+        bias_parts = [None] * GROUP
+        for (i, s), back_weight in zip(units, back_weights):
+            weights = probs[(g * GROUP + i) * samples + s]
+            weighted = weights * back_weight
             back_scores = weighted - weights * column_sum(weighted)
-            bias_part = back_scores if bias_part is None else bias_part + back_scores
-            scores16 = back_scores.astype(BF16)
-            span = pl.ds(start, KWIN)
-            dv_all[s, span, :] += mm(weights.astype(BF16), back)
-            dk_all[s, span, :] += mm(scores16, queries)
-            dq_all[s, pl.ds(start, QWIN), :] = gather_heads(mm_tn(scores16, keys))
-        bias_acc[...] += jnp.where(same, bias_part, 0.0)
+            bias_parts[i] = back_scores if bias_parts[i] is None else bias_parts[i] + back_scores
+            packed.append(weights.astype(BF16))
+            scores16.append(back_scores.astype(BF16))
+        back_values = [mm(weights, back) for weights, back in zip(packed, backs)]
+        back_keys = [
+            mm(scores, spread_heads(q_all[s, pl.ds(starts[i], QWIN), :]))
+            for (i, s), scores in zip(units, scores16)
+        ]
+        back_queries = [
+            mm_tn(scores, k_all[s, pl.ds(starts[i], KWIN), :])
+            for (i, s), scores in zip(units, scores16)
+        ]
+        for (i, s), value, key, query in zip(units, back_values, back_keys, back_queries):
+            span = pl.ds(starts[i], KWIN)
+            dv_all[s, span, :] += value
+            dk_all[s, span, :] += key
+            dq_all[s, pl.ds(starts[i], QWIN), :] = gather_heads(query)
+        for start, bias_part in zip(starts, bias_parts):
+            _, same = window_mask(start)
+            bias_acc[...] += jnp.where(same, bias_part, 0.0)
         return carry
 
-    lax.fori_loop(0, windows, backward_window, 0)
+    lax.fori_loop(0, windows // GROUP, backward_group, 0)
 
     rim = jnp.zeros((HALO, channels), BF16)
 
@@ -249,8 +301,10 @@
         gain_grad = gain_grad + column_sum(back_normed * unit_ext[s])
         back_norm[s] = back_normed[HALO : HALO + atoms]
         rows = pl.ds(pl.multiple_of(s * HALO, HALO), HALO)
-        to_before[rows, :] = back_normed[:HALO].astype(BF16)
-        to_after[rows, :] = back_normed[HALO + atoms :].astype(BF16)
+        low = back_normed[:HALO]
+        high = back_normed[HALO + atoms :]
+        to_partner[rows, :] = jnp.where(is_odd, low, high).astype(BF16)
+        to_link[rows, :] = jnp.where(is_odd, high, low).astype(BF16)
         return gain_grad
 
     gain_grad_one = lax.fori_loop(0, samples, projection, zero_row)
@@ -258,17 +312,62 @@
     tail = 8 * channels + TRANS
     grads[pl.ds(tail, 1), :] = gain_grad_one
     grads[pl.ds(tail + 1, 1), :] = gain_grad_two
-    grads[pl.ds(tail + 2, 1), :] = column_sum(bias_acc[...])
-
-    half = keep.shape[0]
-    mine = flags[1]
-    keep[...] = grads[pl.ds(pl.multiple_of(mine * half, 8), half), :].astype(BF16)
-    send[...] = grads[pl.ds(pl.multiple_of((1 - mine) * half, 8), half), :].astype(BF16)
-
-
-def rim_kernel(flags, state, gain, back_norm, back_res, pair_back, link_back, out):
+    slots = grads.shape[0] - tail - SLOT
+    device = lax.axis_index("samp") * places + place
+    grads[tail + SLOT :, :] = bias_slots(column_sum(bias_acc[...]), device, slots)
+    half = packed_keep.shape[0]
+    mine = place % 2
+    packed_keep[...] = grads[pl.ds(pl.multiple_of(mine * half, 8), half), :].astype(BF16)
+    packed_send[...] = grads[pl.ds(pl.multiple_of((1 - mine) * half, 8), half), :].astype(BF16)
+
+
+def pack_kernel(valid, state, token, own_codes, partner, link, line, sem):
+    samples, atoms, _ = state.shape
+    odd = lax.axis_index("atom") % 2
+    copies = []
+    for target, start in (
+        (partner, (1 - odd) * (atoms - HALO)),
+        (link, odd * (atoms - HALO)),
+    ):
+        for s in range(samples):
+            copies.append(
+                pltpu.make_async_copy(
+                    state.at[s, pl.ds(pl.multiple_of(start, 16), HALO)],
+                    target.at[pl.ds(s * HALO, HALO)],
+                    sem.at[len(copies)],
+                )
+            )
+            copies[-1].start()
+    rows = own_codes.shape[0]
+    line[...] = jnp.zeros_like(line)
+    line[:, :atoms] = token[...].reshape(1, atoms)
+    lane = lax.broadcasted_iota(jnp.int32, (1, LANES), 1)
+    codes = []
+    for r in range(rows):
+        limit = jnp.zeros((1, LANES), jnp.int32)
+        for i in range(LANES // QWIN):
+            w = r * (LANES // QWIN) + i
+            if w * QWIN < atoms:
+                limit = jnp.where(lane // QWIN == i, valid[w], limit)
+        code = jnp.where(lane % QWIN < limit, line[:, r * LANES : (r + 1) * LANES] + 1, 0)
+        codes.append(code)
+        own_codes[r : r + 1, :] = code.astype(F32)
+    tail_row = jnp.zeros((14, LANES), F32)
+    ends = []
+    for code in (codes[0], codes[-1]):
+        ends.append(
+            jnp.concatenate([(code // 256).astype(F32), (code % 256).astype(F32), tail_row], axis=0)
+        )
+    base = samples * HALO
+    partner[base:, :] = jnp.where(odd == 1, ends[0], ends[1]).astype(BF16)
+    link[base:, :] = jnp.where(odd == 1, ends[1], ends[0]).astype(BF16)
+    for copy in copies:
+        copy.wait()
+
+
+def rim_kernel(state, gain, back_norm, back_res, pair_back, link_back, out):
     samples, atoms, channels = state.shape
-    is_odd = flags[0] == 1
+    is_odd = lax.axis_index("atom") % 2 == 1
     from_before = jnp.where(is_odd, pair_back[...], link_back[...]).astype(F32)
     from_after = jnp.where(is_odd, link_back[...], pair_back[...]).astype(F32)
     for s in range(samples):
@@ -286,22 +385,20 @@
         out[s] = (back_res[s] + norm_grad(grad * gain[...], unit, inverse)).astype(BF16)
 
 
-def clip_kernel(flags, own, other, attend, project, output, bias, transit_gain, transit, back):
-    first = flags[0] == 0
+def clip_kernel(own, other, attend, project, output, bias, transit_gain, transit, back):
     channels = LANES
+    first = lax.axis_index("atom") % 2 == 0
     low = jnp.where(first, own[...], other[...]).astype(F32)
     high = jnp.where(first, other[...], own[...]).astype(F32)
     total = jnp.concatenate([low, high], axis=0)
     tail = 8 * channels + TRANS
     lane = lax.broadcasted_iota(jnp.int32, (1, LANES), 1)
-    bias_row = total[tail + 2 : tail + 3]
-    width = LANES // HEADS
+    digits = column_sum(total[tail + SLOT :])
     heads = jnp.zeros((1, LANES), F32)
     for h in range(HEADS):
-        inside = (lane >= h * width) & (lane < (h + 1) * width)
-        sum_h = jnp.sum(jnp.where(inside, bias_row, 0.0), axis=1, keepdims=True)
+        sum_h = jnp.sum(jnp.where((lane // 4) % 4 == h, digits, 0.0), axis=1, keepdims=True)
         heads = jnp.where(lane == h, sum_h, heads)
-    plain = total[: tail + 2]
+    plain = total[: tail + SLOT]
     squares = jnp.sum(column_sum(plain * plain) + heads * heads, axis=1, keepdims=True)
     factor = CLIP_NORM * lax.rsqrt(squares + CLIP_NORM * CLIP_NORM)
     for i in range(3):
@@ -312,7 +409,7 @@
     back[...] = total[8 * channels : 8 * channels + TRANS] * factor
     attend[...] = total[tail : tail + 1] * factor
     transit_gain[...] = total[tail + 1 : tail + 2] * factor
-    bias[...] = heads * factor
+    bias[...] = (heads * factor)[:, :HEADS]
 
 
 def swap(value, axis, mask):
@@ -321,44 +418,26 @@
 
 def pair_exchange(to_partner, to_link, axis):
     size = lax.axis_size(axis)
-    links = [(i, i + 1) for i in range(1, size - 1, 2)]
+    links = [(i, (i + 1) % size) for i in range(1, size, 2)]
     links = links + [(j, i) for i, j in links]
     return lax.ppermute(to_link, axis, links), swap(to_partner, axis, 1)
 
 
-def token_codes(atom_token, window_valid):
-    windows_here = window_valid.shape[0]
-    slots = lax.broadcasted_iota(jnp.int32, (windows_here, QWIN), 1)
-    inside = (slots < window_valid[:, None]).reshape(-1)
-    return jnp.where(inside, atom_token + 1, 0)
-
-
-def edge_pack(state, codes, at_end):
-    samples, atoms, channels = state.shape
-    start = jnp.where(at_end, atoms - HALO, 0)
-    rows = lax.dynamic_slice_in_dim(state, start, HALO, axis=1).reshape(samples * HALO, channels)
-    part = lax.dynamic_slice_in_dim(codes, start, HALO, axis=0)
-    digits = jnp.stack([part // 256, part % 256]).astype(BF16)
-    digits = jnp.pad(digits, ((0, 14), (0, channels - HALO)))
-    return jnp.concatenate([rows, digits], axis=0)
-
-
-def whole(*shape):
-    return pl.BlockSpec(memory_space=pltpu.VMEM)
-
-
-def call(kernel, operands, outs, scratch=(), flops=0):
-    vmem = pl.BlockSpec(memory_space=pltpu.VMEM)
-    smem = pl.BlockSpec(memory_space=pltpu.SMEM)
+VMEM = pl.BlockSpec(memory_space=pltpu.VMEM)
+SMEM = pl.BlockSpec(memory_space=pltpu.SMEM)
+HBM = pl.BlockSpec(memory_space=pltpu.HBM)
+
+
+def call(kernel, operands, specs, outs, scratch=(), flops=0, limit=16):
     moved = sum(x.size * x.dtype.itemsize for x in operands)
     return pl.pallas_call(
         kernel,
         out_shape=[jax.ShapeDtypeStruct(shape, dtype) for shape, dtype in outs],
-        in_specs=[smem] + [vmem] * (len(operands) - 1),
-        out_specs=[vmem] * len(outs),
+        in_specs=list(specs),
+        out_specs=[VMEM] * len(outs),
         scratch_shapes=list(scratch),
-        cost_estimate=pl.CostEstimate(flops=flops, bytes_accessed=moved, transcendentals=0),
-        compiler_params=pltpu.CompilerParams(vmem_limit_bytes=48 * 1024 * 1024),
+        cost_estimate=pl.CostEstimate(flops=flops, bytes_accessed=moved + flops // 200, transcendentals=0),
+        compiler_params=pltpu.CompilerParams(vmem_limit_bytes=limit * 1024 * 1024),
     )(*operands)
 
 
@@ -379,34 +458,46 @@
     ext = atoms + 2 * HALO
     windows = atoms // QWIN
     place = lax.axis_index("atom")
-    odd = place % 2
-    codes = token_codes(atom_token, window_valid)
-    link_rows, pair_rows = pair_exchange(
-        edge_pack(atom_state, codes, odd == 0), edge_pack(atom_state, codes, odd == 1), "atom"
-    )
+    devices = lax.axis_size("samp") * lax.axis_size("atom")
+    slots = -(-devices * SLOT // LANES // SLOT) * SLOT
+    total_rows = 8 * channels + TRANS + SLOT + slots
+    half = total_rows // 2
     code_rows = -(-atoms // LANES)
-    own_codes = jnp.pad(codes.astype(F32), (0, code_rows * LANES - atoms)).reshape(code_rows, LANES)
-    flags = jnp.stack([odd, odd]).astype(jnp.int32)
-    total_rows = 8 * channels + TRANS + SMALL_ROWS
-    half = total_rows // 2
     halo_rows = samples * HALO
-    block_out, back_norm, back_res, to_before, to_after, keep, send = call(
+    pack_rows = halo_rows + SLOT
+    own_codes, to_partner, to_link = call(
+        pack_kernel,
+        (window_valid, atom_state, atom_token),
+        (SMEM, HBM, VMEM),
+        (
+            ((code_rows, LANES), F32),
+            ((pack_rows, channels), BF16),
+            ((pack_rows, channels), BF16),
+        ),
+        (
+            pltpu.VMEM((1, code_rows * LANES), jnp.int32),
+            pltpu.SemaphoreType.DMA((2 * samples,)),
+        ),
+        flops=10_000_000_000,
+    )
+    link_rows, pair_rows = pair_exchange(to_partner, to_link, "atom")
+    block_out, back_norm, back_res, to_partner, to_link, keep, send = call(
         block_kernel,
         (
-            flags,
-            atom_state,
+            own_codes,
             pair_rows,
             link_rows,
-            own_codes,
             attend_gain.reshape(1, channels),
+            jnp.repeat(token_bias, QWIN).reshape(1, HEADS * QWIN),
+            transit_gain.reshape(1, channels),
+            atom_state,
             project_weight,
             output_weight,
-            jnp.repeat(token_bias, QWIN).reshape(1, HEADS * QWIN),
-            transit_gain.reshape(1, channels),
             transit_weight,
             return_weight,
             cotangent,
         ),
+        (VMEM,) * 12,
         (
             ((samples, atoms, channels), BF16),
             ((samples, atoms, channels), F32),
@@ -433,23 +524,34 @@
             pltpu.VMEM((KWIN, HEADS * QWIN), F32),
         ),
         flops=4_000_000_000,
-    )
-
-    got = swap(send, "atom", 1)
-    part = keep + got
+        limit=48,
+    )
+
+    link_back, pair_back = pair_exchange(to_partner, to_link, "atom")
+    cores = lax.axis_size("atom")
+    part = keep + swap(send, "atom", 1)
     x_bit = (place // 2) % 2
     quarter = half // 2
     mine = lax.dynamic_slice_in_dim(part, x_bit * quarter, quarter)
     theirs = lax.dynamic_slice_in_dim(part, (1 - x_bit) * quarter, quarter)
     sums = mine + swap(theirs, "atom", 2)
+    sums, link_back, pair_back = lax.optimization_barrier((sums, link_back, pair_back))
+    (state_grad,) = call(
+        rim_kernel,
+        (atom_state, attend_gain.reshape(1, channels), back_norm, back_res, pair_back, link_back),
+        (VMEM,) * 6,
+        (((samples, atoms, channels), BF16),),
+        flops=100_000_000,
+    )
     mask = 4
-    while mask < lax.axis_size("atom"):
+    while mask < cores:
         sums = sums + swap(sums, "atom", mask)
         mask *= 2
     mask = 1
     while mask < lax.axis_size("samp"):
         sums = sums + swap(sums, "samp", mask)
         mask *= 2
+    sums, state_grad = lax.optimization_barrier((sums, state_grad))
     other = swap(sums, "atom", 2)
     sums = jnp.where(
         x_bit == 0,
@@ -459,27 +561,17 @@
     other = swap(sums, "atom", 1)
     clipped = call(
         clip_kernel,
-        (flags, sums, other),
+        (sums, other),
+        (VMEM,) * 2,
         (
             ((1, channels), F32),
             ((channels, 3 * channels), F32),
             ((channels, channels), F32),
-            ((1, LANES), F32),
+            ((1, HEADS), F32),
             ((1, channels), F32),
             ((channels, 2 * TRANS), F32),
             ((TRANS, channels), F32),
         ),
-    )
-
-    odd_here = odd == 1
-    to_link = jnp.where(odd_here, to_after, to_before)
-    to_partner = jnp.where(odd_here, to_before, to_after)
-    link_back, pair_back = pair_exchange(to_partner, to_link, "atom")
-    (state_grad,) = call(
-        rim_kernel,
-        (flags, atom_state, attend_gain.reshape(1, channels), back_norm, back_res, pair_back, link_back),
-        (((samples, atoms, channels), BF16),),
-        flops=100_000_000,
     )
     return (
         block_out,
@@ -487,7 +579,7 @@
         clipped[0].reshape(channels),
         clipped[1],
         clipped[2],
-        clipped[3][0, :HEADS],
+        clipped[3].reshape(HEADS),
         clipped[4].reshape(channels),
         clipped[5],
         clipped[6],

time: 81.9 us -> 55.4 us (0.68)
  the two profiles are of different devices: /device:TPU:27 before, /device:TPU:0 now
where the time goes in v2:
time: 55.4 us; the launch traced here: 55.2 us
  waiting for transfers between devices  18.3 us (33%)
  Pallas kernels  18.2 us (33%)
  starting transfers between devices  14.5 us (26%)
  local copies, waits for them, and re-layouts  3.12 us (6%)
  between operations  0.78 us (1%)
    pallas_call x4, Pallas kernels, call(): pl.pallas_call(kernel, out_shape=[jax.ShapeDtypeStruct(shape, dtype) for...  18.2 us
    ppermute x9, waiting for transfers between devices, swap(): lax.ppermute(value, axis, [(i, i ^ mask) for i in range(lax.axis_size(axi...  14.9 us
    ppermute x9, starting transfers between devices, swap(): lax.ppermute(value, axis, [(i, i ^ mask) for i in range(lax.axis_size(axi...  9.99 us
    ppermute x2, starting transfers between devices, pair_exchange(): return (lax.ppermute(to_link, axis, links), swap(to_partner, axis, 1))  4.54 us
    ppermute x2, waiting for transfers between devices, pair_exchange(): return (lax.ppermute(to_link, axis, links), swap(to_partner, axis, 1))  3.38 us
    unnamed x24, local copies, waits for them, and re-layouts  2.95 us
  transfers between devices with their start and end apart: 11, of which 9 were waited for; matrix products, arithmetic and copies ran while one was open for 0% of the time, Pallas kernels for 3%

profile of v2, /device:TPU:0, one launch (start us, length us, event | category | flops | bytes accessed | tf_op | source)
XLA Modules:
  0.0 55.2 jit_solution(11375143600966020977)
XLA Ops:
  0.7 1.0 %copy-done = bf16[4,320,128]{2,1,0:T(8,128)(2,1)S(1)} copy-done((bf16[4,320,128]{2,1,0:T(8,128)(2,1)S(1)}, bf16[4,320,128]{2,1,0:T(8,128)(2,1)}, u32[]{:S(2)}) %copy-start) | copy-done | bytes 327704
  1.6 0.7 %copy-done.8 = s32[320]{0:T(512)S(1)} copy-done((s32[320]{0:T(512)S(1)}, s32[320]{0:T(512)}, u32[]{:S(2)}) %copy-start.8) | copy-done | bytes 1304
  2.3 0.7 %copy-done.9 = s32[10]{0:T(128)S(1)} copy-done((s32[10]{0:T(128)S(1)}, s32[10]{0:T(128)}, u32[]{:S(2)}) %copy-start.9) | copy-done | bytes 64
  3.0 0.8 %shard_map.178 = (f32[3,128]{1,0:T(4,128)S(1)}, bf16[208,128]{1,0:T(8,128)(2,1)S(1)}, bf16[208,128]{1,0:T(8,128)(2,1)S(1)}) custom-call(s32[10]{0:T(128)S(1)} %copy-done.9, bf16[4,320,128]{2,1,0:T(8,128)(2,1)S(1)} %copy-done, s32[320]{0:T(512)S(1)} %copy-done.8), custom_call_target="tpu_custom_call" | custom-call | flops 10000000000 | bytes 50329000 | tf_op jit(solution)/shard_map/pallas_call | solution.py:433
  3.8 0.0 copy-start.11
  3.8 0.6 %collective-permute-start = (bf16[208,128]{1,0:T(8,128)(2,1)S(1)}, bf16[208,128]{1,0:T(8,128)(2,1)S(1)}, u32[]{:S(2)}, u32[]{:S(2)}) collective-permute-start(bf16[208,128]{1,0:T(8,128)(2,1)S(1)} %get-tuple-element.32), channel_id=1, source_target_pairs={{0,1},{1,0},{2,3},{3,2},{4,5},{5,4},{6,7},{7,6},{8,9},{9,8},{10,11... | collective-permute-start | bytes 159752 | tf_op jit(solution)/shard_map/ppermute | solution.py:416
  4.4 3.5 %collective-permute-start.1 = (bf16[208,128]{1,0:T(8,128)(2,1)S(1)}, bf16[208,128]{1,0:T(8,128)(2,1)S(1)}, u32[]{:S(2)}, u32[]{:S(2)}) collective-permute-start(bf16[208,128]{1,0:T(8,128)(2,1)S(1)} %get-tuple-element.33), channel_id=1, source_target_pairs={{1,2},{3,4},{5,6},{7,0},{2,1},{4,3},{6,5},{0,7},{9,10},{11,12},{13... | collective-permute-start | bytes 159752 | tf_op jit(solution)/shard_map/ppermute | solution.py:423
  7.9 0.1 broadcast_in_dim.3
  8.0 0.1 reshape_reshape.3.bias_row
  8.1 0.0 collective-permute-done.pair_rows
  8.1 1.7 %collective-permute-done.1.link_rows = bf16[208,128]{1,0:T(8,128)(2,1)S(1)} collective-permute-done((bf16[208,128]{1,0:T(8,128)(2,1)S(1)}, bf16[208,128]{1,0:T(8,128)(2,1)S(1)}, u32[]{:S(2)}, u32[]{:S(2)}) %collective-permute-start.1) | collective-permute-done | bytes 53280 | tf_op jit(solution)/shard_map/ppermute | solution.py:423
  9.8 0.6 %copy-done.2 = f32[128]{0:T(128)S(1)} copy-done((f32[128]{0:T(128)S(1)}, f32[128]{0:T(128)}, u32[]{:S(2)}) %copy-start.2) | copy-done | bytes 536
  10.4 0.0 copy-done.10
  10.4 14.6 %shard_map.179 = (bf16[4,320,128]{2,1,0:T(8,128)(2,1)}, f32[4,320,128]{2,1,0:T(8,128)S(1)}, f32[4,320,128]{2,1,0:T(8,128)S(1)}, bf16[192,128]{1,0:T(8,128)(2,1)S...) custom-call(f32[3,128]{1,0:T(4,128)S(1)} %get-tuple-element.31.own_codes, ...), custom_call_target="tpu_custom_call" | custom-call | flops 4000000000 | bytes 21092608 | tf_op jit(solution)/shard_map/pallas_call | solution.py:433
  25.0 1.4 %collective-permute-done.2 = bf16[656,128]{1,0:T(8,128)(2,1)S(1)} collective-permute-done((bf16[656,128]{1,0:T(8,128)(2,1)S(1)}, bf16[656,128]{1,0:T(8,128)(2,1)S(1)}, u32[]{:S(2)}, u32[]{:S(2)}) %collective-permute-start.2) | collective-permute-done | bytes 167968 | tf_op jit(solution)/shard_map/ppermute | solution.py:416
  26.5 1.8 %collective-permute-start.3 = (bf16[328,128]{1,0:T(8,128)(2,1)S(1)}, bf16[328,128]{1,0:T(8,128)(2,1)S(1)}, u32[]{:S(2)}, u32[]{:S(2)}) collective-permute-start(bf16[328,128]{1,0:T(8,128)(2,1)S(1)} %constant_dynamic-slice_fusion), channel_id=1, source_target_pairs={{0,2},{1,3},{2,0},{3,1},{4,6},{5,7},{6,4},{7,5},{8,10},{9,11},{10,... | collective-permute-start | bytes 251912 | tf_op jit(solution)/shard_map/ppermute | solution.py:416
  28.3 1.0 %collective-permute-start.4 = (bf16[192,128]{1,0:T(8,128)(2,1)S(1)}, bf16[192,128]{1,0:T(8,128)(2,1)S(1)}, u32[]{:S(2)}, u32[]{:S(2)}) collective-permute-start(bf16[192,128]{1,0:T(8,128)(2,1)S(1)} %get-tuple-element.37), channel_id=1, source_target_pairs={{1,2},{3,4},{5,6},{7,0},{2,1},{4,3},{6,5},{0,7},{9,10},{11,12},{13... | collective-permute-start | bytes 147464 | tf_op jit(solution)/shard_map/ppermute | solution.py:423
  29.3 0.0 collective-permute-start.5
  29.3 2.0 %collective-permute-done.3 = bf16[328,128]{1,0:T(8,128)(2,1)S(1)} collective-permute-done((bf16[328,128]{1,0:T(8,128)(2,1)S(1)}, bf16[328,128]{1,0:T(8,128)(2,1)S(1)}, u32[]{:S(2)}, u32[]{:S(2)}) %collective-permute-start.3) | collective-permute-done | bytes 84000 | tf_op jit(solution)/shard_map/ppermute | solution.py:416
  31.4 1.7 %collective-permute-done.4.link_back = bf16[192,128]{1,0:T(8,128)(2,1)S(1)} collective-permute-done((bf16[192,128]{1,0:T(8,128)(2,1)S(1)}, bf16[192,128]{1,0:T(8,128)(2,1)S(1)}, u32[]{:S(2)}, u32[]{:S(2)}) %collective-permute-start.4) | collective-permute-done | bytes 49184 | tf_op jit(solution)/shard_map/ppermute | solution.py:423
  33.1 1.1 %collective-permute-start.6 = (bf16[328,128]{1,0:T(8,128)(2,1)S(1)}, bf16[328,128]{1,0:T(8,128)(2,1)S(1)}, u32[]{:S(2)}, u32[]{:S(2)}) collective-permute-start(bf16[328,128]{1,0:T(8,128)(2,1)S(1)} %dynamic-slice_add_fusion), channel_id=1, source_target_pairs={{0,4},{1,5},{2,6},{3,7},{4,0},{5,1},{6,2},{7,3},{8,12},{9,13},{10,... | collective-permute-start | bytes 251912 | tf_op jit(solution)/shard_map/ppermute | solution.py:416
  34.2 3.3 %collective-permute-done.6 = bf16[328,128]{1,0:T(8,128)(2,1)S(1)} collective-permute-done((bf16[328,128]{1,0:T(8,128)(2,1)S(1)}, bf16[328,128]{1,0:T(8,128)(2,1)S(1)}, u32[]{:S(2)}, u32[]{:S(2)}) %collective-permute-start.6) | collective-permute-done | bytes 84000 | tf_op jit(solution)/shard_map/ppermute | solution.py:416
  37.6 1.8 %collective-permute-start.7 = (bf16[328,128]{1,0:T(8,128)(2,1)S(1)}, bf16[328,128]{1,0:T(8,128)(2,1)S(1)}, u32[]{:S(2)}, u32[]{:S(2)}) collective-permute-start(bf16[328,128]{1,0:T(8,128)(2,1)S(1)} %add.31), channel_id=1, source_target_pairs={{0,8},{8,0},{16,24},{24,16},{1,9},{9,1},{17,25},{25,17},{2,10},{10... | collective-permute-start | bytes 251912 | tf_op jit(solution)/shard_map/ppermute | solution.py:416
  39.4 2.7 %collective-permute-done.7 = bf16[328,128]{1,0:T(8,128)(2,1)S(1)} collective-permute-done((bf16[328,128]{1,0:T(8,128)(2,1)S(1)}, bf16[328,128]{1,0:T(8,128)(2,1)S(1)}, u32[]{:S(2)}, u32[]{:S(2)}) %collective-permute-start.7) | collective-permute-done | bytes 84000 | tf_op jit(solution)/shard_map/ppermute | solution.py:416
  42.1 3.3 %collective-permute-start.8 = (bf16[328,128]{1,0:T(8,128)(2,1)S(1)}, bf16[328,128]{1,0:T(8,128)(2,1)S(1)}, u32[]{:S(2)}, u32[]{:S(2)}) collective-permute-start(bf16[328,128]{1,0:T(8,128)(2,1)S(1)} %add.32), channel_id=1, source_target_pairs={{0,16},{8,24},{16,0},{24,8},{1,17},{9,25},{17,1},{25,9},{2,18},{10... | collective-permute-start | bytes 251912 | tf_op jit(solution)/shard_map/ppermute | solution.py:416
  45.5 1.6 %shard_map.180 = bf16[4,320,128]{2,1,0:T(8,128)(2,1)} custom-call(bf16[4,320,128]{2,1,0:T(8,128)(2,1)S(1)} %copy-done.1, f32[1,128]{1,0:T(1,128)S(1)} %bitcast.6, f32[4,320,128]{2,1,0:T(8,128)S(1)} %get-tuple-element.40.back_norm, f32[4,320,128]{2,1,0:T(8,128)S(1)} %get-tuple-element.41.back_res, bf16[192,128]{1,0:T(8,128)(2,1)S(1)} %collective-permute-done.5.pair_back, ...), custom_call_target="tpu_custom_call" | custom-call | flops 100000000 | bytes 2237216 | tf_op jit(solution)/shard_map/pallas_call | solution.py:433
  47.1 0.8 %collective-permute-done.8 = bf16[328,128]{1,0:T(8,128)(2,1)S(1)} collective-permute-done((bf16[328,128]{1,0:T(8,128)(2,1)S(1)}, bf16[328,128]{1,0:T(8,128)(2,1)S(1)}, u32[]{:S(2)}, u32[]{:S(2)}) %collective-permute-start.8) | collective-permute-done | bytes 84000 | tf_op jit(solution)/shard_map/ppermute | solution.py:416
  48.0 1.3 %collective-permute-start.9 = (bf16[328,128]{1,0:T(8,128)(2,1)S(1)}, bf16[328,128]{1,0:T(8,128)(2,1)S(1)}, u32[]{:S(2)}, u32[]{:S(2)}) collective-permute-start(bf16[328,128]{1,0:T(8,128)(2,1)S(1)} %add.33), channel_id=1, source_target_pairs={{0,2},{1,3},{2,0},{3,1},{4,6},{5,7},{6,4},{7,5},{8,10},{9,11},{10,... | collective-permute-start | bytes 251912 | tf_op jit(solution)/shard_map/ppermute | solution.py:416
  49.2 3.3 %collective-permute-done.9 = bf16[328,128]{1,0:T(8,128)(2,1)S(1)} collective-permute-done((bf16[328,128]{1,0:T(8,128)(2,1)S(1)}, bf16[328,128]{1,0:T(8,128)(2,1)S(1)}, u32[]{:S(2)}, u32[]{:S(2)}) %collective-permute-start.9) | collective-permute-done | bytes 84000 | tf_op jit(solution)/shard_map/ppermute | solution.py:416
  52.5 0.1 collective-permute-start.10
  52.6 1.4 %collective-permute-done.10.other = bf16[656,128]{1,0:T(8,128)(2,1)S(1)} collective-permute-done((bf16[656,128]{1,0:T(8,128)(2,1)S(1)}, bf16[656,128]{1,0:T(8,128)(2,1)S(1)}, u32[]{:S(2)}, u32[]{:S(2)}) %collective-permute-start.10) | collective-permute-done | bytes 167968 | tf_op jit(solution)/shard_map/ppermute | solution.py:416
  54.0 1.2 %shard_map.181 = (f32[1,128]{1,0:T(1,128)}, f32[128,384]{1,0:T(8,128)}, f32[128,128]{1,0:T(8,128)}, f32[1,4]{1,0:T(1,128)}, f32[1,128]{1,0:T(1,128)}, /*index=5*/f32[128,512]{1,0:T(8,128)}, f32[256,128]{1,0:T(8,128)}) custom-call(bf16[656,128]{1,0:T(8,128)(2,1)S(1)} %maximum_select_fusion.own, bf16[656,128]{1,0:T(8,128)(2,1)S(1)} %collective-permute-done.10.other), custom_call_target="tpu_custom_call" | custom-call | bytes 335872 | tf_op jit(solution)/shard_map/pallas_call | solution.py:433
  (27 shorter events, 0.3 us)
Async XLA Ops:
  0.6 1.0 %copy-start = (bf16[4,320,128]{2,1,0:T(8,128)(2,1)S(1)}, bf16[4,320,128]{2,1,0:T(8,128)(2,1)}, u32[]{:S(2)}) copy-start(bf16[4,320,128]{2,1,0:T(8,128)(2,1)} %state.5) | copy-start | bytes 983044
  1.6 0.7 %copy-start.8 = (s32[320]{0:T(512)S(1)}, s32[320]{0:T(512)}, u32[]{:S(2)}) copy-start(s32[320]{0:T(512)} %token_.1) | copy-start | bytes 3844
  2.3 0.7 %copy-start.9 = (s32[10]{0:T(128)S(1)}, s32[10]{0:T(128)}, u32[]{:S(2)}) copy-start(s32[10]{0:T(128)} %valid.1) | copy-start | bytes 124
  3.0 6.8 %copy-start.1 = (bf16[4,320,128]{2,1,0:T(8,128)(2,1)S(1)}, bf16[4,320,128]{2,1,0:T(8,128)(2,1)}, u32[]{:S(2)}) copy-start(bf16[4,320,128]{2,1,0:T(8,128)(2,1)} %state.5) | copy-start | bytes 983044
  3.0 6.8 %copy-start.3 = (bf16[4,320,128]{2,1,0:T(8,128)(2,1)S(1)}, bf16[4,320,128]{2,1,0:T(8,128)(2,1)}, u32[]{:S(2)}) copy-start(bf16[4,320,128]{2,1,0:T(8,128)(2,1)} %cot.1) | copy-start | bytes 983044
  3.0 6.8 %copy-start.4 = (bf16[128,512]{1,0:T(8,128)(2,1)S(1)}, bf16[128,512]{1,0:T(8,128)(2,1)}, u32[]{:S(2)}) copy-start(bf16[128,512]{1,0:T(8,128)(2,1)} %transit_weight.1) | copy-start | bytes 393220
  3.0 6.8 %copy-start.5 = (bf16[128,384]{1,0:T(8,128)(2,1)S(1)}, bf16[128,384]{1,0:T(8,128)(2,1)}, u32[]{:S(2)}) copy-start(bf16[128,384]{1,0:T(8,128)(2,1)} %project_weight.1) | copy-start | bytes 294916
  3.0 6.8 %copy-start.6 = (bf16[256,128]{1,0:T(8,128)(2,1)S(1)}, bf16[256,128]{1,0:T(8,128)(2,1)}, u32[]{:S(2)}) copy-start(bf16[256,128]{1,0:T(8,128)(2,1)} %return_weight.1) | copy-start | bytes 196612
  3.0 6.8 %copy-start.7 = (bf16[128,128]{1,0:T(8,128)(2,1)S(1)}, bf16[128,128]{1,0:T(8,128)(2,1)}, u32[]{:S(2)}) copy-start(bf16[128,128]{1,0:T(8,128)(2,1)} %output_weight.1) | copy-start | bytes 98308
  3.8 4.1 %copy-start.11 = (f32[4]{0:T(128)S(1)}, f32[4]{0:T(128)}, u32[]{:S(2)}) copy-start(f32[4]{0:T(128)} %param.17) | copy-start | bytes 52
  3.8 4.3 %collective-permute-start = (bf16[208,128]{1,0:T(8,128)(2,1)S(1)}, bf16[208,128]{1,0:T(8,128)(2,1)S(1)}, u32[]{:S(2)}, u32[]{:S(2)}) collective-permute-start(bf16[208,128]{1,0:T(8,128)(2,1)S(1)} %get-tuple-element.32), channel_id=1, source_target_pairs={{0,1},{1,0},{2,3},{3,2},{4,5},{5,4},{6,7},{7,6},{8,9},{9,8},{10,11... | collective-permute-start | bytes 159752 | tf_op jit(solution)/shard_map/ppermute | solution.py:416
  4.4 5.4 %collective-permute-start.1 = (bf16[208,128]{1,0:T(8,128)(2,1)S(1)}, bf16[208,128]{1,0:T(8,128)(2,1)S(1)}, u32[]{:S(2)}, u32[]{:S(2)}) collective-permute-start(bf16[208,128]{1,0:T(8,128)(2,1)S(1)} %get-tuple-element.33), channel_id=1, source_target_pairs={{1,2},{3,4},{5,6},{7,0},{2,1},{4,3},{6,5},{0,7},{9,10},{11,12},{13... | collective-permute-start | bytes 159752 | tf_op jit(solution)/shard_map/ppermute | solution.py:423
  9.7 0.7 %copy-start.2 = (f32[128]{0:T(128)S(1)}, f32[128]{0:T(128)}, u32[]{:S(2)}) copy-start(f32[128]{0:T(128)} %param.14) | copy-start | bytes 1540
  9.7 0.7 %copy-start.10 = (f32[128]{0:T(128)S(1)}, f32[128]{0:T(128)}, u32[]{:S(2)}) copy-start(f32[128]{0:T(128)} %param.18) | copy-start | bytes 1540
  25.0 1.4 %collective-permute-start.2 = (bf16[656,128]{1,0:T(8,128)(2,1)S(1)}, bf16[656,128]{1,0:T(8,128)(2,1)S(1)}, u32[]{:S(2)}, u32[]{:S(2)}) collective-permute-start(bf16[656,128]{1,0:T(8,128)(2,1)S(1)} %get-tuple-element.36), channel_id=1, source_target_pairs={{0,1},{1,0},{2,3},{3,2},{4,5},{5,4},{6,7},{7,6},{8,9},{9,8},{10,11... | collective-permute-start | bytes 503816 | tf_op jit(solution)/shard_map/ppermute | solution.py:416
  26.5 4.8 %collective-permute-start.3 = (bf16[328,128]{1,0:T(8,128)(2,1)S(1)}, bf16[328,128]{1,0:T(8,128)(2,1)S(1)}, u32[]{:S(2)}, u32[]{:S(2)}) collective-permute-start(bf16[328,128]{1,0:T(8,128)(2,1)S(1)} %constant_dynamic-slice_fusion), channel_id=1, source_target_pairs={{0,2},{1,3},{2,0},{3,1},{4,6},{5,7},{6,4},{7,5},{8,10},{9,11},{10,... | collective-permute-start | bytes 251912 | tf_op jit(solution)/shard_map/ppermute | solution.py:416
  28.3 4.8 %collective-permute-start.4 = (bf16[192,128]{1,0:T(8,128)(2,1)S(1)}, bf16[192,128]{1,0:T(8,128)(2,1)S(1)}, u32[]{:S(2)}, u32[]{:S(2)}) collective-permute-start(bf16[192,128]{1,0:T(8,128)(2,1)S(1)} %get-tuple-element.37), channel_id=1, source_target_pairs={{1,2},{3,4},{5,6},{7,0},{2,1},{4,3},{6,5},{0,7},{9,10},{11,12},{13... | collective-permute-start | bytes 147464 | tf_op jit(solution)/shard_map/ppermute | solution.py:423
  29.3 3.8 %collective-permute-start.5 = (bf16[192,128]{1,0:T(8,128)(2,1)S(1)}, bf16[192,128]{1,0:T(8,128)(2,1)S(1)}, u32[]{:S(2)}, u32[]{:S(2)}) collective-permute-start(bf16[192,128]{1,0:T(8,128)(2,1)S(1)} %get-tuple-element.38), channel_id=1, source_target_pairs={{0,1},{1,0},{2,3},{3,2},{4,5},{5,4},{6,7},{7,6},{8,9},{9,8},{10,11... | collective-permute-start | bytes 147464 | tf_op jit(solution)/shard_map/ppermute | solution.py:416
  33.1 4.5 %collective-permute-start.6 = (bf16[328,128]{1,0:T(8,128)(2,1)S(1)}, bf16[328,128]{1,0:T(8,128)(2,1)S(1)}, u32[]{:S(2)}, u32[]{:S(2)}) collective-permute-start(bf16[328,128]{1,0:T(8,128)(2,1)S(1)} %dynamic-slice_add_fusion), channel_id=1, source_target_pairs={{0,4},{1,5},{2,6},{3,7},{4,0},{5,1},{6,2},{7,3},{8,12},{9,13},{10,... | collective-permute-start | bytes 251912 | tf_op jit(solution)/shard_map/ppermute | solution.py:416
  37.6 4.5 %collective-permute-start.7 = (bf16[328,128]{1,0:T(8,128)(2,1)S(1)}, bf16[328,128]{1,0:T(8,128)(2,1)S(1)}, u32[]{:S(2)}, u32[]{:S(2)}) collective-permute-start(bf16[328,128]{1,0:T(8,128)(2,1)S(1)} %add.31), channel_id=1, source_target_pairs={{0,8},{8,0},{16,24},{24,16},{1,9},{9,1},{17,25},{25,17},{2,10},{10... | collective-permute-start | bytes 251912 | tf_op jit(solution)/shard_map/ppermute | solution.py:416
  42.1 5.8 %collective-permute-start.8 = (bf16[328,128]{1,0:T(8,128)(2,1)S(1)}, bf16[328,128]{1,0:T(8,128)(2,1)S(1)}, u32[]{:S(2)}, u32[]{:S(2)}) collective-permute-start(bf16[328,128]{1,0:T(8,128)(2,1)S(1)} %add.32), channel_id=1, source_target_pairs={{0,16},{8,24},{16,0},{24,8},{1,17},{9,25},{17,1},{25,9},{2,18},{10... | collective-permute-start | bytes 251912 | tf_op jit(solution)/shard_map/ppermute | solution.py:416
  48.0 4.5 %collective-permute-start.9 = (bf16[328,128]{1,0:T(8,128)(2,1)S(1)}, bf16[328,128]{1,0:T(8,128)(2,1)S(1)}, u32[]{:S(2)}, u32[]{:S(2)}) collective-permute-start(bf16[328,128]{1,0:T(8,128)(2,1)S(1)} %add.33), channel_id=1, source_target_pairs={{0,2},{1,3},{2,0},{3,1},{4,6},{5,7},{6,4},{7,5},{8,10},{9,11},{10,... | collective-permute-start | bytes 251912 | tf_op jit(solution)/shard_map/ppermute | solution.py:416
  52.5 1.5 %collective-permute-start.10 = (bf16[656,128]{1,0:T(8,128)(2,1)S(1)}, bf16[656,128]{1,0:T(8,128)(2,1)S(1)}, u32[]{:S(2)}, u32[]{:S(2)}) collective-permute-start(bf16[656,128]{1,0:T(8,128)(2,1)S(1)} %maximum_select_fusion.own), channel_id=1, source_target_pairs={{0,1},{1,0},{2,3},{3,2},{4,5},{5,4},{6,7},{7,6},{8,9},{9,8},{10,11... | collective-permute-start | bytes 503816 | tf_op jit(solution)/shard_map/ppermute | solution.py:416

commit v3 on v2

--- a/solution.py
+++ b/solution.py
@@ -16,7 +16,8 @@
 EPSILON = 1e-05
 CLIP_NORM = 256.0
 LANES = 128
-GROUP = 2
+GROUP = 10
+CHUNK = 2
 SLOT = 16
 LOG2E = 1.0 / math.log(2.0)
 
@@ -96,9 +97,7 @@
     own_codes,
     pair_rows,
     link_rows,
-    attend_gain,
-    bias_row,
-    transit_gain,
+    vectors,
     state,
     project_weight,
     output_weight,
@@ -160,8 +159,9 @@
     dk_all[...] = jnp.zeros_like(dk_all)
     dv_all[...] = jnp.zeros_like(dv_all)
 
-    gain_one = attend_gain[...]
-    gain_two = transit_gain[...]
+    gain_one = vectors[0:1, :]
+    gain_two = vectors[1:2, :]
+    bias_row = vectors[2:3, :]
     for s in range(samples):
         rows = jnp.concatenate(
             [before[s * HALO : (s + 1) * HALO], state[s], after[s * HALO : (s + 1) * HALO]], axis=0
@@ -197,7 +197,7 @@
         offsets = []
         for start in starts:
             key_code, same = window_mask(start)
-            offset = jnp.where(same, bias_row[...] * LOG2E, 0.0)
+            offset = jnp.where(same, bias_row * LOG2E, 0.0)
             offsets.append(jnp.where(key_code > 0, offset, -1e30))
         packed = []
         for (i, s), score in zip(units, scores):
@@ -216,9 +216,17 @@
 
     lax.fori_loop(0, windows // GROUP, forward_group, 0)
 
-    def transition(s, gain_grad):
-        attended = att[s]
-        residual = (state[s].astype(F32) + mm(attended, output_weight[...])).astype(BF16)
+    chunk_rows = CHUNK * atoms
+
+    def flat(ref, c):
+        return ref[pl.ds(c * CHUNK, CHUNK)].reshape(chunk_rows, channels)
+
+    def fill(ref, c, value):
+        ref[pl.ds(c * CHUNK, CHUNK)] = value.reshape(CHUNK, atoms, channels)
+
+    def transition(c, gain_grad):
+        attended = flat(att, c)
+        residual = (flat(state, c).astype(F32) + mm(attended, output_weight[...])).astype(BF16)
         residual = residual.astype(F32)
         unit, inverse = split_norm(residual)
         transit_in = (unit * gain_two).astype(BF16)
@@ -228,8 +236,8 @@
         sigmoid = 1.0 / (1.0 + jnp.exp(-gate))
         silu = gate * sigmoid
         gated = (silu * up).astype(BF16)
-        block_out[s] = (residual + mm(gated, return_weight[...])).astype(BF16)
-        cot16 = cot[s]
+        fill(block_out, c, (residual + mm(gated, return_weight[...])).astype(BF16))
+        cot16 = flat(cot, c)
         back_gated = mm_nt(cot16, return_weight[...])
         back_gate = back_gated * up * sigmoid * (1.0 + gate * (1.0 - sigmoid))
         back_hidden = jnp.concatenate([back_gate, back_gated * silu], axis=1).astype(BF16)
@@ -240,14 +248,14 @@
         back_transit = mm_nt(back_hidden, transit_weight[...])
         gain_grad = gain_grad + column_sum(back_transit * unit)
         back_residual = cot16.astype(F32) + norm_grad(back_transit * gain_two, unit, inverse)
-        back_res[s] = back_residual
+        fill(back_res, c, back_residual)
         back16 = back_residual.astype(BF16)
         grads[pl.ds(3 * channels, channels), :] += mm_tn(attended, back16)
-        d_att[s] = mm_nt(back16, output_weight[...]).astype(BF16)
+        fill(d_att, c, mm_nt(back16, output_weight[...]).astype(BF16))
         return gain_grad
 
     zero_row = jnp.zeros((1, channels), F32)
-    gain_grad_two = lax.fori_loop(0, samples, transition, zero_row)
+    gain_grad_two = lax.fori_loop(0, samples // CHUNK, transition, zero_row)
 
     def backward_group(g, carry):
         starts, units = group_units(g)
@@ -288,26 +296,33 @@
 
     rim = jnp.zeros((HALO, channels), BF16)
 
-    def projection(s, gain_grad):
-        back_q = (dq_all[s] * scale).astype(BF16)
-        back_q = jnp.concatenate([rim, back_q, rim], axis=0)
-        back_k = (dk_all[s] * scale).astype(BF16)
-        back_v = dv_all[s].astype(BF16)
-        back_all = jnp.concatenate([back_q, back_k, back_v], axis=1)
+    def projection(c, gain_grad):
+        parts = []
+        for i in range(CHUNK):
+            s = c * CHUNK + i
+            back_q = jnp.concatenate([rim, (dq_all[s] * scale).astype(BF16), rim], axis=0)
+            back_k = (dk_all[s] * scale).astype(BF16)
+            parts.append(jnp.concatenate([back_q, back_k, dv_all[s].astype(BF16)], axis=1))
+        back_all = jnp.concatenate(parts, axis=0)
         back_normed = mm_nt(back_all, project_weight[...])
-        grad_project = mm_tn(norm_ext[s], back_all)
+        normed = norm_ext[pl.ds(c * CHUNK, CHUNK)].reshape(CHUNK * ext, channels)
+        unit = unit_ext[pl.ds(c * CHUNK, CHUNK)].reshape(CHUNK * ext, channels)
+        grad_project = mm_tn(normed, back_all)
         for i in range(3):
             grads[pl.ds(i * channels, channels), :] += grad_project[:, i * LANES : (i + 1) * LANES]
-        gain_grad = gain_grad + column_sum(back_normed * unit_ext[s])
-        back_norm[s] = back_normed[HALO : HALO + atoms]
-        rows = pl.ds(pl.multiple_of(s * HALO, HALO), HALO)
-        low = back_normed[:HALO]
-        high = back_normed[HALO + atoms :]
-        to_partner[rows, :] = jnp.where(is_odd, low, high).astype(BF16)
-        to_link[rows, :] = jnp.where(is_odd, high, low).astype(BF16)
+        gain_grad = gain_grad + column_sum(back_normed * unit)
+        for i in range(CHUNK):
+            s = c * CHUNK + i
+            one = back_normed[i * ext : (i + 1) * ext]
+            back_norm[s] = one[HALO : HALO + atoms]
+            rows = pl.ds(pl.multiple_of(s * HALO, HALO), HALO)
+            low = one[:HALO]
+            high = one[HALO + atoms :]
+            to_partner[rows, :] = jnp.where(is_odd, low, high).astype(BF16)
+            to_link[rows, :] = jnp.where(is_odd, high, low).astype(BF16)
         return gain_grad
 
-    gain_grad_one = lax.fori_loop(0, samples, projection, zero_row)
+    gain_grad_one = lax.fori_loop(0, samples // CHUNK, projection, zero_row)
 
     tail = 8 * channels + TRANS
     grads[pl.ds(tail, 1), :] = gain_grad_one
@@ -321,7 +336,11 @@
     packed_send[...] = grads[pl.ds(pl.multiple_of((1 - mine) * half, 8), half), :].astype(BF16)
 
 
-def pack_kernel(valid, state, token, own_codes, partner, link, line, sem):
+def lead_kernel(out):
+    out[...] = jnp.zeros_like(out)
+
+
+def pack_kernel(valid, blank, state, token, own_codes, partner, link, line, sem):
     samples, atoms, _ = state.shape
     odd = lax.axis_index("atom") % 2
     copies = []
@@ -352,7 +371,7 @@
         code = jnp.where(lane % QWIN < limit, line[:, r * LANES : (r + 1) * LANES] + 1, 0)
         codes.append(code)
         own_codes[r : r + 1, :] = code.astype(F32)
-    tail_row = jnp.zeros((14, LANES), F32)
+    tail_row = blank[0:14, :]
     ends = []
     for code in (codes[0], codes[-1]):
         ends.append(
@@ -382,7 +401,7 @@
             axis=0,
         )
         unit, inverse = split_norm(state[s].astype(F32))
-        out[s] = (back_res[s] + norm_grad(grad * gain[...], unit, inverse)).astype(BF16)
+        out[s] = (back_res[s] + norm_grad(grad * gain[0:1, :], unit, inverse)).astype(BF16)
 
 
 def clip_kernel(own, other, attend, project, output, bias, transit_gain, transit, back):
@@ -465,10 +484,11 @@
     code_rows = -(-atoms // LANES)
     halo_rows = samples * HALO
     pack_rows = halo_rows + SLOT
+    (blank,) = call(lead_kernel, (), (), (((SLOT, LANES), F32),), flops=10_000_000_000)
     own_codes, to_partner, to_link = call(
         pack_kernel,
-        (window_valid, atom_state, atom_token),
-        (SMEM, HBM, VMEM),
+        (window_valid, blank, atom_state, atom_token),
+        (SMEM, VMEM, HBM, VMEM),
         (
             ((code_rows, LANES), F32),
             ((pack_rows, channels), BF16),
@@ -481,15 +501,14 @@
         flops=10_000_000_000,
     )
     link_rows, pair_rows = pair_exchange(to_partner, to_link, "atom")
+    vectors = jnp.stack([attend_gain, transit_gain, jnp.repeat(token_bias, QWIN)])
     block_out, back_norm, back_res, to_partner, to_link, keep, send = call(
         block_kernel,
         (
             own_codes,
             pair_rows,
             link_rows,
-            attend_gain.reshape(1, channels),
-            jnp.repeat(token_bias, QWIN).reshape(1, HEADS * QWIN),
-            transit_gain.reshape(1, channels),
+            vectors,
             atom_state,
             project_weight,
             output_weight,
@@ -497,7 +516,7 @@
             return_weight,
             cotangent,
         ),
-        (VMEM,) * 12,
+        (VMEM,) * 10,
         (
             ((samples, atoms, channels), BF16),
             ((samples, atoms, channels), F32),
@@ -535,18 +554,18 @@
     mine = lax.dynamic_slice_in_dim(part, x_bit * quarter, quarter)
     theirs = lax.dynamic_slice_in_dim(part, (1 - x_bit) * quarter, quarter)
     sums = mine + swap(theirs, "atom", 2)
-    sums, link_back, pair_back = lax.optimization_barrier((sums, link_back, pair_back))
-    (state_grad,) = call(
-        rim_kernel,
-        (atom_state, attend_gain.reshape(1, channels), back_norm, back_res, pair_back, link_back),
-        (VMEM,) * 6,
-        (((samples, atoms, channels), BF16),),
-        flops=100_000_000,
-    )
     mask = 4
     while mask < cores:
         sums = sums + swap(sums, "atom", mask)
         mask *= 2
+    sums, link_back, pair_back = lax.optimization_barrier((sums, link_back, pair_back))
+    (state_grad,) = call(
+        rim_kernel,
+        (atom_state, vectors, back_norm, back_res, pair_back, link_back),
+        (VMEM,) * 6,
+        (((samples, atoms, channels), BF16),),
+        flops=100_000_000,
+    )
     mask = 1
     while mask < lax.axis_size("samp"):
         sums = sums + swap(sums, "samp", mask)

time: 55.4 us -> 48.4 us (0.87)
  Pallas kernels: 18.2 us -> 13.6 us
  waiting for transfers between devices: 18.3 us -> 15.4 us
  starting transfers between devices: 14.5 us -> 16.5 us
  local copies, waits for them, and re-layouts: 3.12 us -> 1.83 us
    pallas_call x4 -> x5, Pallas kernels: 18.2 us -> 13.6 us  [call(): pl.pallas_call(kernel, out_shape=[jax.ShapeDtypeStruct(shape, dtype) for...]
    ppermute x9, starting transfers between devices: 9.99 us -> 12.4 us  [swap(): lax.ppermute(value, axis, [(i, i ^ mask) for i in range(lax.axis_size(axi...]
    ppermute x9, waiting for transfers between devices: 14.9 us -> 13 us  [swap(): lax.ppermute(value, axis, [(i, i ^ mask) for i in range(lax.axis_size(axi...]
    unnamed x24 -> x22, local copies, waits for them, and re-layouts: 2.95 us -> 1.66 us
    ppermute x2, waiting for transfers between devices: 3.38 us -> 2.39 us  [pair_exchange(): return (lax.ppermute(to_link, axis, links), swap(to_partner, axis, 1))]
where the time goes in v3:
time: 48.4 us; the launch traced here: 48.3 us
  starting transfers between devices  16.5 us (34%)
  waiting for transfers between devices  15.4 us (32%)
  Pallas kernels  13.6 us (28%)
  local copies, waits for them, and re-layouts  1.83 us (4%)
  between operations  0.79 us (2%)
    pallas_call x5, Pallas kernels, call(): pl.pallas_call(kernel, out_shape=[jax.ShapeDtypeStruct(shape, dtype) for...  13.6 us
    ppermute x9, waiting for transfers between devices, swap(): lax.ppermute(value, axis, [(i, i ^ mask) for i in range(lax.axis_size(axi...  13 us
    ppermute x9, starting transfers between devices, swap(): lax.ppermute(value, axis, [(i, i ^ mask) for i in range(lax.axis_size(axi...  12.4 us
    ppermute x2, starting transfers between devices, pair_exchange(): return (lax.ppermute(to_link, axis, links), swap(to_partner, axis, 1))  4.08 us
    ppermute x2, waiting for transfers between devices, pair_exchange(): return (lax.ppermute(to_link, axis, links), swap(to_partner, axis, 1))  2.39 us
    unnamed x22, local copies, waits for them, and re-layouts  1.66 us
  transfers between devices with their start and end apart: 11, of which 9 were waited for; matrix products, arithmetic and copies ran while one was open for 0% of the time, Pallas kernels for 3%

profile of v3, /device:TPU:0, one launch (start us, length us, event | category | flops | bytes accessed | tf_op | source)
XLA Modules:
  0.0 48.3 jit_solution(13672912883230930928)
XLA Ops:
  0.7 0.6 %copy-done.7 = s32[10]{0:T(128)S(1)} copy-done((s32[10]{0:T(128)S(1)}, s32[10]{0:T(128)}, u32[]{:S(2)}) %copy-start.7) | copy-done | bytes 64
  1.3 0.3 copy-done
  1.6 0.0 copy-start.4
  1.7 0.0 copy-start.5
  1.7 0.8 %shard_map.179 = (f32[3,128]{1,0:T(4,128)S(1)}, bf16[208,128]{1,0:T(8,128)(2,1)S(1)}, bf16[208,128]{1,0:T(8,128)(2,1)S(1)}) custom-call(s32[10]{0:T(128)S(1)} %copy-done.7, f32[16,128]{1,0:T(8,128)S(1)} %shard_map.178.blank, bf16[4,320,128]{2,1,0:T(8,128)(2,1)S(1)} %copy-done, s32[320]{0:T(512)S(1)} %copy-done.6), custom_call_target="tpu_custom_call" | custom-call | flops 10000000000 | bytes 50337192 | tf_op jit(solution)/shard_map/pallas_call | solution.py:452
  2.5 0.0 copy-start.8
  2.5 0.6 %collective-permute-start = (bf16[208,128]{1,0:T(8,128)(2,1)S(1)}, bf16[208,128]{1,0:T(8,128)(2,1)S(1)}, u32[]{:S(2)}, u32[]{:S(2)}) collective-permute-start(bf16[208,128]{1,0:T(8,128)(2,1)S(1)} %get-tuple-element.32), channel_id=1, source_target_pairs={{0,1},{1,0},{2,3},{3,2},{4,5},{5,4},{6,7},{7,6},{8,9},{9,8},{10,11... | collective-permute-start | bytes 159752 | tf_op jit(solution)/shard_map/ppermute | solution.py:435
  3.0 3.5 %collective-permute-start.1 = (bf16[208,128]{1,0:T(8,128)(2,1)S(1)}, bf16[208,128]{1,0:T(8,128)(2,1)S(1)}, u32[]{:S(2)}, u32[]{:S(2)}) collective-permute-start(bf16[208,128]{1,0:T(8,128)(2,1)S(1)} %get-tuple-element.33), channel_id=1, source_target_pairs={{1,2},{3,4},{5,6},{7,0},{2,1},{4,3},{6,5},{0,7},{9,10},{11,12},{13... | collective-permute-start | bytes 159752 | tf_op jit(solution)/shard_map/ppermute | solution.py:442
  6.6 0.1 broadcast_in_dim.3
  6.7 0.1 stack_reshape.3
  6.7 0.7 %copy-done.9 = f32[128]{0:T(128)S(1)} copy-done((f32[128]{0:T(128)S(1)}, f32[128]{0:T(128)}, u32[]{:S(2)}) %copy-start.9) | copy-done | bytes 536
  7.4 0.0 copy-done.10
  7.4 1.0 %collective-permute-done.1.link_rows = bf16[208,128]{1,0:T(8,128)(2,1)S(1)} collective-permute-done((bf16[208,128]{1,0:T(8,128)(2,1)S(1)}, bf16[208,128]{1,0:T(8,128)(2,1)S(1)}, u32[]{:S(2)}, u32[]{:S(2)}) %collective-permute-start.1) | collective-permute-done | bytes 53280 | tf_op jit(solution)/shard_map/ppermute | solution.py:442
  8.4 10.0 %shard_map.180 = (bf16[4,320,128]{2,1,0:T(8,128)(2,1)}, f32[4,320,128]{2,1,0:T(8,128)S(1)}, f32[4,320,128]{2,1,0:T(8,128)S(1)}, bf16[192,128]{1,0:T(8,128)(2,1)S...) custom-call(f32[3,128]{1,0:T(4,128)S(1)} %get-tuple-element.31.own_codes, ...), custom_call_target="tpu_custom_call" | custom-call | flops 4000000000 | bytes 21092608 | tf_op jit(solution)/shard_map/pallas_call | solution.py:452
  18.4 1.4 %collective-permute-done.2 = bf16[656,128]{1,0:T(8,128)(2,1)S(1)} collective-permute-done((bf16[656,128]{1,0:T(8,128)(2,1)S(1)}, bf16[656,128]{1,0:T(8,128)(2,1)S(1)}, u32[]{:S(2)}, u32[]{:S(2)}) %collective-permute-start.2) | collective-permute-done | bytes 167968 | tf_op jit(solution)/shard_map/ppermute | solution.py:435
  19.9 1.8 %collective-permute-start.3 = (bf16[328,128]{1,0:T(8,128)(2,1)S(1)}, bf16[328,128]{1,0:T(8,128)(2,1)S(1)}, u32[]{:S(2)}, u32[]{:S(2)}) collective-permute-start(bf16[328,128]{1,0:T(8,128)(2,1)S(1)} %constant_dynamic-slice_fusion), channel_id=1, source_target_pairs={{0,2},{1,3},{2,0},{3,1},{4,6},{5,7},{6,4},{7,5},{8,10},{9,11},{10,... | collective-permute-start | bytes 251912 | tf_op jit(solution)/shard_map/ppermute | solution.py:435
  21.7 3.0 %collective-permute-done.3 = bf16[328,128]{1,0:T(8,128)(2,1)S(1)} collective-permute-done((bf16[328,128]{1,0:T(8,128)(2,1)S(1)}, bf16[328,128]{1,0:T(8,128)(2,1)S(1)}, u32[]{:S(2)}, u32[]{:S(2)}) %collective-permute-start.3) | collective-permute-done | bytes 84000 | tf_op jit(solution)/shard_map/ppermute | solution.py:435
  24.7 1.6 %collective-permute-start.4 = (bf16[328,128]{1,0:T(8,128)(2,1)S(1)}, bf16[328,128]{1,0:T(8,128)(2,1)S(1)}, u32[]{:S(2)}, u32[]{:S(2)}) collective-permute-start(bf16[328,128]{1,0:T(8,128)(2,1)S(1)} %dynamic-slice_add_fusion), channel_id=1, source_target_pairs={{0,4},{1,5},{2,6},{3,7},{4,0},{5,1},{6,2},{7,3},{8,12},{9,13},{10,... | collective-permute-start | bytes 251912 | tf_op jit(solution)/shard_map/ppermute | solution.py:435
  26.3 0.5 %collective-permute-start.5 = (bf16[192,128]{1,0:T(8,128)(2,1)S(1)}, bf16[192,128]{1,0:T(8,128)(2,1)S(1)}, u32[]{:S(2)}, u32[]{:S(2)}) collective-permute-start(bf16[192,128]{1,0:T(8,128)(2,1)S(1)} %get-tuple-element.37), channel_id=1, source_target_pairs={{1,2},{3,4},{5,6},{7,0},{2,1},{4,3},{6,5},{0,7},{9,10},{11,12},{13... | collective-permute-start | bytes 147464 | tf_op jit(solution)/shard_map/ppermute | solution.py:442
  26.8 1.3 %collective-permute-start.6 = (bf16[192,128]{1,0:T(8,128)(2,1)S(1)}, bf16[192,128]{1,0:T(8,128)(2,1)S(1)}, u32[]{:S(2)}, u32[]{:S(2)}) collective-permute-start(bf16[192,128]{1,0:T(8,128)(2,1)S(1)} %get-tuple-element.38), channel_id=1, source_target_pairs={{0,1},{1,0},{2,3},{3,2},{4,5},{5,4},{6,7},{7,6},{8,9},{9,8},{10,11... | collective-permute-start | bytes 147464 | tf_op jit(solution)/shard_map/ppermute | solution.py:435
  28.2 1.1 %collective-permute-done.4 = bf16[328,128]{1,0:T(8,128)(2,1)S(1)} collective-permute-done((bf16[328,128]{1,0:T(8,128)(2,1)S(1)}, bf16[328,128]{1,0:T(8,128)(2,1)S(1)}, u32[]{:S(2)}, u32[]{:S(2)}) %collective-permute-start.4) | collective-permute-done | bytes 84000 | tf_op jit(solution)/shard_map/ppermute | solution.py:435
  29.3 1.4 %collective-permute-done.5.link_back = bf16[192,128]{1,0:T(8,128)(2,1)S(1)} collective-permute-done((bf16[192,128]{1,0:T(8,128)(2,1)S(1)}, bf16[192,128]{1,0:T(8,128)(2,1)S(1)}, u32[]{:S(2)}, u32[]{:S(2)}) %collective-permute-start.5) | collective-permute-done | bytes 49184 | tf_op jit(solution)/shard_map/ppermute | solution.py:442
  30.7 1.8 %collective-permute-start.7 = (bf16[328,128]{1,0:T(8,128)(2,1)S(1)}, bf16[328,128]{1,0:T(8,128)(2,1)S(1)}, u32[]{:S(2)}, u32[]{:S(2)}) collective-permute-start(bf16[328,128]{1,0:T(8,128)(2,1)S(1)} %add.31), channel_id=1, source_target_pairs={{0,8},{8,0},{16,24},{24,16},{1,9},{9,1},{17,25},{25,17},{2,10},{10... | collective-permute-start | bytes 251912 | tf_op jit(solution)/shard_map/ppermute | solution.py:435
  32.5 2.7 %collective-permute-done.7 = bf16[328,128]{1,0:T(8,128)(2,1)S(1)} collective-permute-done((bf16[328,128]{1,0:T(8,128)(2,1)S(1)}, bf16[328,128]{1,0:T(8,128)(2,1)S(1)}, u32[]{:S(2)}, u32[]{:S(2)}) %collective-permute-start.7) | collective-permute-done | bytes 84000 | tf_op jit(solution)/shard_map/ppermute | solution.py:435
  35.2 2.8 %collective-permute-start.8 = (bf16[328,128]{1,0:T(8,128)(2,1)S(1)}, bf16[328,128]{1,0:T(8,128)(2,1)S(1)}, u32[]{:S(2)}, u32[]{:S(2)}) collective-permute-start(bf16[328,128]{1,0:T(8,128)(2,1)S(1)} %add.32), channel_id=1, source_target_pairs={{0,16},{8,24},{16,0},{24,8},{1,17},{9,25},{17,1},{25,9},{2,18},{10... | collective-permute-start | bytes 251912 | tf_op jit(solution)/shard_map/ppermute | solution.py:435
  38.1 1.6 %shard_map.181 = bf16[4,320,128]{2,1,0:T(8,128)(2,1)} custom-call(bf16[4,320,128]{2,1,0:T(8,128)(2,1)S(1)} %copy-done, f32[3,128]{1,0:T(4,128)S(1)} %pad_maximum_fusion.vectors.gain, f32[4,320,128]{2,1,0:T(8,128)S(1)} %get-tuple-element.40.back_norm, f32[4,320,128]{2,1,0:T(8,128)S(1)} %get-tuple-element.41.back_res, ...), custom_call_target="tpu_custom_call" | custom-call | flops 100000000 | bytes 2238240 | tf_op jit(solution)/shard_map/pallas_call | solution.py:452
  39.7 1.0 %collective-permute-done.8 = bf16[328,128]{1,0:T(8,128)(2,1)S(1)} collective-permute-done((bf16[328,128]{1,0:T(8,128)(2,1)S(1)}, bf16[328,128]{1,0:T(8,128)(2,1)S(1)}, u32[]{:S(2)}, u32[]{:S(2)}) %collective-permute-start.8) | collective-permute-done | bytes 84000 | tf_op jit(solution)/shard_map/ppermute | solution.py:435
  40.7 2.4 %collective-permute-start.9 = (bf16[328,128]{1,0:T(8,128)(2,1)S(1)}, bf16[328,128]{1,0:T(8,128)(2,1)S(1)}, u32[]{:S(2)}, u32[]{:S(2)}) collective-permute-start(bf16[328,128]{1,0:T(8,128)(2,1)S(1)} %add.33), channel_id=1, source_target_pairs={{0,2},{1,3},{2,0},{3,1},{4,6},{5,7},{6,4},{7,5},{8,10},{9,11},{10,... | collective-permute-start | bytes 251912 | tf_op jit(solution)/shard_map/ppermute | solution.py:435
  43.1 2.4 %collective-permute-done.9 = bf16[328,128]{1,0:T(8,128)(2,1)S(1)} collective-permute-done((bf16[328,128]{1,0:T(8,128)(2,1)S(1)}, bf16[328,128]{1,0:T(8,128)(2,1)S(1)}, u32[]{:S(2)}, u32[]{:S(2)}) %collective-permute-start.9) | collective-permute-done | bytes 84000 | tf_op jit(solution)/shard_map/ppermute | solution.py:435
  45.6 0.1 collective-permute-start.10
  45.7 1.4 %collective-permute-done.10.other = bf16[656,128]{1,0:T(8,128)(2,1)S(1)} collective-permute-done((bf16[656,128]{1,0:T(8,128)(2,1)S(1)}, bf16[656,128]{1,0:T(8,128)(2,1)S(1)}, u32[]{:S(2)}, u32[]{:S(2)}) %collective-permute-start.10) | collective-permute-done | bytes 167968 | tf_op jit(solution)/shard_map/ppermute | solution.py:435
  47.1 1.2 %shard_map.182 = (f32[1,128]{1,0:T(1,128)}, f32[128,384]{1,0:T(8,128)}, f32[128,128]{1,0:T(8,128)}, f32[1,4]{1,0:T(1,128)}, f32[1,128]{1,0:T(1,128)}, /*index=5*/f32[128,512]{1,0:T(8,128)}, f32[256,128]{1,0:T(8,128)}) custom-call(bf16[656,128]{1,0:T(8,128)(2,1)S(1)} %maximum_select_fusion.own, bf16[656,128]{1,0:T(8,128)(2,1)S(1)} %collective-permute-done.10.other), custom_call_target="tpu_custom_call" | custom-call | bytes 335872 | tf_op jit(solution)/shard_map/pallas_call | solution.py:452
  (27 shorter events, 0.3 us)
Async XLA Ops:
  0.6 0.7 %copy-start.7 = (s32[10]{0:T(128)S(1)}, s32[10]{0:T(128)}, u32[]{:S(2)}) copy-start(s32[10]{0:T(128)} %valid.1) | copy-start | bytes 124
  0.7 1.0 %copy-start = (bf16[4,320,128]{2,1,0:T(8,128)(2,1)S(1)}, bf16[4,320,128]{2,1,0:T(8,128)(2,1)}, u32[]{:S(2)}) copy-start(bf16[4,320,128]{2,1,0:T(8,128)(2,1)} %state.5) | copy-start | bytes 983044
  0.7 1.0 %copy-start.6 = (s32[320]{0:T(512)S(1)}, s32[320]{0:T(512)}, u32[]{:S(2)}) copy-start(s32[320]{0:T(512)} %token_.1) | copy-start | bytes 3844
  1.6 6.8 %copy-start.1 = (bf16[4,320,128]{2,1,0:T(8,128)(2,1)S(1)}, bf16[4,320,128]{2,1,0:T(8,128)(2,1)}, u32[]{:S(2)}) copy-start(bf16[4,320,128]{2,1,0:T(8,128)(2,1)} %cot.1) | copy-start | bytes 983044
  1.6 6.8 %copy-start.2 = (bf16[128,512]{1,0:T(8,128)(2,1)S(1)}, bf16[128,512]{1,0:T(8,128)(2,1)}, u32[]{:S(2)}) copy-start(bf16[128,512]{1,0:T(8,128)(2,1)} %transit_weight.1) | copy-start | bytes 393220
  1.6 6.8 %copy-start.3 = (bf16[128,384]{1,0:T(8,128)(2,1)S(1)}, bf16[128,384]{1,0:T(8,128)(2,1)}, u32[]{:S(2)}) copy-start(bf16[128,384]{1,0:T(8,128)(2,1)} %project_weight.1) | copy-start | bytes 294916
  1.6 6.8 %copy-start.4 = (bf16[256,128]{1,0:T(8,128)(2,1)S(1)}, bf16[256,128]{1,0:T(8,128)(2,1)}, u32[]{:S(2)}) copy-start(bf16[256,128]{1,0:T(8,128)(2,1)} %return_weight.1) | copy-start | bytes 196612
  1.7 6.8 %copy-start.5 = (bf16[128,128]{1,0:T(8,128)(2,1)S(1)}, bf16[128,128]{1,0:T(8,128)(2,1)}, u32[]{:S(2)}) copy-start(bf16[128,128]{1,0:T(8,128)(2,1)} %output_weight.1) | copy-start | bytes 98308
  2.5 4.1 %copy-start.8 = (f32[4]{0:T(128)S(1)}, f32[4]{0:T(128)}, u32[]{:S(2)}) copy-start(f32[4]{0:T(128)} %param.17) | copy-start | bytes 52
  2.5 4.9 %collective-permute-start = (bf16[208,128]{1,0:T(8,128)(2,1)S(1)}, bf16[208,128]{1,0:T(8,128)(2,1)S(1)}, u32[]{:S(2)}, u32[]{:S(2)}) collective-permute-start(bf16[208,128]{1,0:T(8,128)(2,1)S(1)} %get-tuple-element.32), channel_id=1, source_target_pairs={{0,1},{1,0},{2,3},{3,2},{4,5},{5,4},{6,7},{7,6},{8,9},{9,8},{10,11... | collective-permute-start | bytes 159752 | tf_op jit(solution)/shard_map/ppermute | solution.py:435
  3.0 5.4 %collective-permute-start.1 = (bf16[208,128]{1,0:T(8,128)(2,1)S(1)}, bf16[208,128]{1,0:T(8,128)(2,1)S(1)}, u32[]{:S(2)}, u32[]{:S(2)}) collective-permute-start(bf16[208,128]{1,0:T(8,128)(2,1)S(1)} %get-tuple-element.33), channel_id=1, source_target_pairs={{1,2},{3,4},{5,6},{7,0},{2,1},{4,3},{6,5},{0,7},{9,10},{11,12},{13... | collective-permute-start | bytes 159752 | tf_op jit(solution)/shard_map/ppermute | solution.py:442
  6.7 0.7 %copy-start.9 = (f32[128]{0:T(128)S(1)}, f32[128]{0:T(128)}, u32[]{:S(2)}) copy-start(f32[128]{0:T(128)} %param.18) | copy-start | bytes 1540
  6.7 0.7 %copy-start.10 = (f32[128]{0:T(128)S(1)}, f32[128]{0:T(128)}, u32[]{:S(2)}) copy-start(f32[128]{0:T(128)} %param.14) | copy-start | bytes 1540
  18.4 1.4 %collective-permute-start.2 = (bf16[656,128]{1,0:T(8,128)(2,1)S(1)}, bf16[656,128]{1,0:T(8,128)(2,1)S(1)}, u32[]{:S(2)}, u32[]{:S(2)}) collective-permute-start(bf16[656,128]{1,0:T(8,128)(2,1)S(1)} %get-tuple-element.36), channel_id=1, source_target_pairs={{0,1},{1,0},{2,3},{3,2},{4,5},{5,4},{6,7},{7,6},{8,9},{9,8},{10,11... | collective-permute-start | bytes 503816 | tf_op jit(solution)/shard_map/ppermute | solution.py:435
  19.9 4.8 %collective-permute-start.3 = (bf16[328,128]{1,0:T(8,128)(2,1)S(1)}, bf16[328,128]{1,0:T(8,128)(2,1)S(1)}, u32[]{:S(2)}, u32[]{:S(2)}) collective-permute-start(bf16[328,128]{1,0:T(8,128)(2,1)S(1)} %constant_dynamic-slice_fusion), channel_id=1, source_target_pairs={{0,2},{1,3},{2,0},{3,1},{4,6},{5,7},{6,4},{7,5},{8,10},{9,11},{10,... | collective-permute-start | bytes 251912 | tf_op jit(solution)/shard_map/ppermute | solution.py:435
  24.7 4.5 %collective-permute-start.4 = (bf16[328,128]{1,0:T(8,128)(2,1)S(1)}, bf16[328,128]{1,0:T(8,128)(2,1)S(1)}, u32[]{:S(2)}, u32[]{:S(2)}) collective-permute-start(bf16[328,128]{1,0:T(8,128)(2,1)S(1)} %dynamic-slice_add_fusion), channel_id=1, source_target_pairs={{0,4},{1,5},{2,6},{3,7},{4,0},{5,1},{6,2},{7,3},{8,12},{9,13},{10,... | collective-permute-start | bytes 251912 | tf_op jit(solution)/shard_map/ppermute | solution.py:435
  26.3 4.4 %collective-permute-start.5 = (bf16[192,128]{1,0:T(8,128)(2,1)S(1)}, bf16[192,128]{1,0:T(8,128)(2,1)S(1)}, u32[]{:S(2)}, u32[]{:S(2)}) collective-permute-start(bf16[192,128]{1,0:T(8,128)(2,1)S(1)} %get-tuple-element.37), channel_id=1, source_target_pairs={{1,2},{3,4},{5,6},{7,0},{2,1},{4,3},{6,5},{0,7},{9,10},{11,12},{13... | collective-permute-start | bytes 147464 | tf_op jit(solution)/shard_map/ppermute | solution.py:442
  26.8 3.9 %collective-permute-start.6 = (bf16[192,128]{1,0:T(8,128)(2,1)S(1)}, bf16[192,128]{1,0:T(8,128)(2,1)S(1)}, u32[]{:S(2)}, u32[]{:S(2)}) collective-permute-start(bf16[192,128]{1,0:T(8,128)(2,1)S(1)} %get-tuple-element.38), channel_id=1, source_target_pairs={{0,1},{1,0},{2,3},{3,2},{4,5},{5,4},{6,7},{7,6},{8,9},{9,8},{10,11... | collective-permute-start | bytes 147464 | tf_op jit(solution)/shard_map/ppermute | solution.py:435
  30.7 4.5 %collective-permute-start.7 = (bf16[328,128]{1,0:T(8,128)(2,1)S(1)}, bf16[328,128]{1,0:T(8,128)(2,1)S(1)}, u32[]{:S(2)}, u32[]{:S(2)}) collective-permute-start(bf16[328,128]{1,0:T(8,128)(2,1)S(1)} %add.31), channel_id=1, source_target_pairs={{0,8},{8,0},{16,24},{24,16},{1,9},{9,1},{17,25},{25,17},{2,10},{10... | collective-permute-start | bytes 251912 | tf_op jit(solution)/shard_map/ppermute | solution.py:435
  35.2 5.4 %collective-permute-start.8 = (bf16[328,128]{1,0:T(8,128)(2,1)S(1)}, bf16[328,128]{1,0:T(8,128)(2,1)S(1)}, u32[]{:S(2)}, u32[]{:S(2)}) collective-permute-start(bf16[328,128]{1,0:T(8,128)(2,1)S(1)} %add.32), channel_id=1, source_target_pairs={{0,16},{8,24},{16,0},{24,8},{1,17},{9,25},{17,1},{25,9},{2,18},{10... | collective-permute-start | bytes 251912 | tf_op jit(solution)/shard_map/ppermute | solution.py:435
  40.7 4.9 %collective-permute-start.9 = (bf16[328,128]{1,0:T(8,128)(2,1)S(1)}, bf16[328,128]{1,0:T(8,128)(2,1)S(1)}, u32[]{:S(2)}, u32[]{:S(2)}) collective-permute-start(bf16[328,128]{1,0:T(8,128)(2,1)S(1)} %add.33), channel_id=1, source_target_pairs={{0,2},{1,3},{2,0},{3,1},{4,6},{5,7},{6,4},{7,5},{8,10},{9,11},{10,... | collective-permute-start | bytes 251912 | tf_op jit(solution)/shard_map/ppermute | solution.py:435
  45.6 1.5 %collective-permute-start.10 = (bf16[656,128]{1,0:T(8,128)(2,1)S(1)}, bf16[656,128]{1,0:T(8,128)(2,1)S(1)}, u32[]{:S(2)}, u32[]{:S(2)}) collective-permute-start(bf16[656,128]{1,0:T(8,128)(2,1)S(1)} %maximum_select_fusion.own), channel_id=1, source_target_pairs={{0,1},{1,0},{2,3},{3,2},{4,5},{5,4},{6,7},{7,6},{8,9},{9,8},{10,11... | collective-permute-start | bytes 503816 | tf_op jit(solution)/shard_map/ppermute | solution.py:435

commit v4 on v3

--- a/solution.py
+++ b/solution.py
@@ -18,6 +18,7 @@
 LANES = 128
 GROUP = 10
 CHUNK = 2
+SPAN = 2
 SLOT = 16
 LOG2E = 1.0 / math.log(2.0)
 
@@ -124,6 +125,8 @@
     dk_all,
     dv_all,
     grads,
+    project_grads,
+    total_sums,
     bias_acc,
 ):
     samples, atoms, channels = state.shape
@@ -154,7 +157,6 @@
         codes[HALO + i * LANES : HALO + i * LANES + count, :] = down_lanes(own_codes[i : i + 1, :])[0:count]
     codes[HALO + atoms : ext, :] = down_lanes(last_code)[0:HALO]
 
-    grads[...] = jnp.zeros_like(grads)
     bias_acc[...] = jnp.zeros_like(bias_acc)
     dk_all[...] = jnp.zeros_like(dk_all)
     dv_all[...] = jnp.zeros_like(dv_all)
@@ -175,14 +177,18 @@
         k_all[s] = projected[:, channels : 2 * channels]
         v_all[s] = projected[:, 2 * channels :]
 
-    def window_mask(start):
-        key_code = codes[pl.ds(start, KWIN), :]
-        query = codes[pl.ds(start + HALO, QWIN), :]
-        query_code = jnp.transpose(jnp.concatenate([query] * HEADS, axis=0))
-        return key_code, key_code == query_code
+    def query_row(w):
+        row, lane = divmod(w * QWIN, LANES)
+        return jnp.concatenate([own_codes[row : row + 1, lane : lane + QWIN]] * HEADS, axis=1)
+
+    query_rows = [query_row(w) for w in range(windows)]
+
+    def window_mask(w):
+        key_code = codes[w * QWIN : w * QWIN + KWIN, :]
+        return key_code, key_code == query_rows[w]
 
     def group_units(g):
-        starts = [pl.multiple_of((g * GROUP + i) * QWIN, QWIN) for i in range(GROUP)]
+        starts = [(g * GROUP + i) * QWIN for i in range(GROUP)]
         return starts, [(i, s) for i in range(GROUP) for s in range(samples)]
 
     def forward_group(g, carry):
@@ -195,8 +201,8 @@
             for i, s in units
         ]
         offsets = []
-        for start in starts:
-            key_code, same = window_mask(start)
+        for i in range(GROUP):
+            key_code, same = window_mask(g * GROUP + i)
             offset = jnp.where(same, bias_row * LOG2E, 0.0)
             offsets.append(jnp.where(key_code > 0, offset, -1e30))
         packed = []
@@ -214,7 +220,8 @@
             att[s, pl.ds(starts[i], QWIN), :] = gather_heads(outcome).astype(BF16)
         return carry
 
-    lax.fori_loop(0, windows // GROUP, forward_group, 0)
+    for g in range(windows // GROUP):
+        forward_group(g, 0)
 
     chunk_rows = CHUNK * atoms
 
@@ -241,21 +248,23 @@
         back_gated = mm_nt(cot16, return_weight[...])
         back_gate = back_gated * up * sigmoid * (1.0 + gate * (1.0 - sigmoid))
         back_hidden = jnp.concatenate([back_gate, back_gated * silu], axis=1).astype(BF16)
-        grads[pl.ds(8 * channels, TRANS), :] += mm_tn(gated, cot16)
+        grads[c, pl.ds(8 * channels, TRANS), :] = mm_tn(gated, cot16)
         grad_transit = mm_tn(transit_in, back_hidden)
         for i in range(2 * TRANS // LANES):
-            grads[pl.ds((4 + i) * channels, channels), :] += grad_transit[:, i * LANES : (i + 1) * LANES]
+            grads[c, pl.ds((4 + i) * channels, channels), :] = grad_transit[:, i * LANES : (i + 1) * LANES]
         back_transit = mm_nt(back_hidden, transit_weight[...])
         gain_grad = gain_grad + column_sum(back_transit * unit)
         back_residual = cot16.astype(F32) + norm_grad(back_transit * gain_two, unit, inverse)
         fill(back_res, c, back_residual)
         back16 = back_residual.astype(BF16)
-        grads[pl.ds(3 * channels, channels), :] += mm_tn(attended, back16)
+        grads[c, pl.ds(3 * channels, channels), :] = mm_tn(attended, back16)
         fill(d_att, c, mm_nt(back16, output_weight[...]).astype(BF16))
         return gain_grad
 
     zero_row = jnp.zeros((1, channels), F32)
-    gain_grad_two = lax.fori_loop(0, samples // CHUNK, transition, zero_row)
+    gain_grad_two = zero_row
+    for c in range(samples // CHUNK):
+        gain_grad_two = transition(c, gain_grad_two)
 
     def backward_group(g, carry):
         starts, units = group_units(g)
@@ -287,32 +296,33 @@
             dv_all[s, span, :] += value
             dk_all[s, span, :] += key
             dq_all[s, pl.ds(starts[i], QWIN), :] = gather_heads(query)
-        for start, bias_part in zip(starts, bias_parts):
-            _, same = window_mask(start)
+        for i, bias_part in enumerate(bias_parts):
+            _, same = window_mask(g * GROUP + i)
             bias_acc[...] += jnp.where(same, bias_part, 0.0)
         return carry
 
-    lax.fori_loop(0, windows // GROUP, backward_group, 0)
+    for g in range(windows // GROUP):
+        backward_group(g, 0)
 
     rim = jnp.zeros((HALO, channels), BF16)
 
     def projection(c, gain_grad):
         parts = []
-        for i in range(CHUNK):
-            s = c * CHUNK + i
+        for i in range(SPAN):
+            s = c * SPAN + i
             back_q = jnp.concatenate([rim, (dq_all[s] * scale).astype(BF16), rim], axis=0)
             back_k = (dk_all[s] * scale).astype(BF16)
             parts.append(jnp.concatenate([back_q, back_k, dv_all[s].astype(BF16)], axis=1))
         back_all = jnp.concatenate(parts, axis=0)
         back_normed = mm_nt(back_all, project_weight[...])
-        normed = norm_ext[pl.ds(c * CHUNK, CHUNK)].reshape(CHUNK * ext, channels)
-        unit = unit_ext[pl.ds(c * CHUNK, CHUNK)].reshape(CHUNK * ext, channels)
+        normed = norm_ext[pl.ds(c * SPAN, SPAN)].reshape(SPAN * ext, channels)
+        unit = unit_ext[pl.ds(c * SPAN, SPAN)].reshape(SPAN * ext, channels)
         grad_project = mm_tn(normed, back_all)
         for i in range(3):
-            grads[pl.ds(i * channels, channels), :] += grad_project[:, i * LANES : (i + 1) * LANES]
+            project_grads[c, pl.ds(i * channels, channels), :] = grad_project[:, i * LANES : (i + 1) * LANES]
         gain_grad = gain_grad + column_sum(back_normed * unit)
-        for i in range(CHUNK):
-            s = c * CHUNK + i
+        for i in range(SPAN):
+            s = c * SPAN + i
             one = back_normed[i * ext : (i + 1) * ext]
             back_norm[s] = one[HALO : HALO + atoms]
             rows = pl.ds(pl.multiple_of(s * HALO, HALO), HALO)
@@ -322,18 +332,31 @@
             to_link[rows, :] = jnp.where(is_odd, high, low).astype(BF16)
         return gain_grad
 
-    gain_grad_one = lax.fori_loop(0, samples // CHUNK, projection, zero_row)
+    gain_grad_one = zero_row
+    for c in range(samples // SPAN):
+        gain_grad_one = projection(c, gain_grad_one)
 
     tail = 8 * channels + TRANS
-    grads[pl.ds(tail, 1), :] = gain_grad_one
-    grads[pl.ds(tail + 1, 1), :] = gain_grad_two
-    slots = grads.shape[0] - tail - SLOT
+    lead = 3 * channels
+
+    def add_up(parts, start, stop):
+        total = parts[0, start:stop, :]
+        for c in range(1, parts.shape[0]):
+            total = total + parts[c, start:stop, :]
+        return total
+
+    slots = total_sums.shape[0] - tail - SLOT
     device = lax.axis_index("samp") * places + place
-    grads[tail + SLOT :, :] = bias_slots(column_sum(bias_acc[...]), device, slots)
+    total_sums[:lead, :] = add_up(project_grads, 0, lead)
+    total_sums[lead:tail, :] = add_up(grads, lead, tail)
+    total_sums[tail : tail + SLOT, :] = jnp.concatenate(
+        [gain_grad_one, gain_grad_two, jnp.zeros((SLOT - 2, channels), F32)], axis=0
+    )
+    total_sums[tail + SLOT :, :] = bias_slots(column_sum(bias_acc[...]), device, slots)
     half = packed_keep.shape[0]
     mine = place % 2
-    packed_keep[...] = grads[pl.ds(pl.multiple_of(mine * half, 8), half), :].astype(BF16)
-    packed_send[...] = grads[pl.ds(pl.multiple_of((1 - mine) * half, 8), half), :].astype(BF16)
+    packed_keep[...] = total_sums[pl.ds(pl.multiple_of(mine * half, 8), half), :].astype(BF16)
+    packed_send[...] = total_sums[pl.ds(pl.multiple_of((1 - mine) * half, 8), half), :].astype(BF16)
 
 
 def lead_kernel(out):
@@ -539,6 +562,8 @@
             pltpu.VMEM((samples, atoms, channels), F32),
             pltpu.VMEM((samples, ext, channels), F32),
             pltpu.VMEM((samples, ext, channels), F32),
+            pltpu.VMEM((samples // CHUNK, 8 * channels + TRANS, channels), F32),
+            pltpu.VMEM((samples // SPAN, 3 * channels, channels), F32),
             pltpu.VMEM((total_rows, channels), F32),
             pltpu.VMEM((KWIN, HEADS * QWIN), F32),
         ),

time: 48.4 us -> 47 us (0.971)
  Pallas kernels: 13.6 us -> 12.1 us
    pallas_call x5, Pallas kernels: 13.6 us -> 12.1 us  [call(): pl.pallas_call(kernel, out_shape=[jax.ShapeDtypeStruct(shape, dtype) for...]
where the time goes in v4:
time: 47 us; the launch traced here: 46.8 us
  starting transfers between devices  16.5 us (35%)
  waiting for transfers between devices  15.3 us (33%)
  Pallas kernels  12.1 us (26%)
  local copies, waits for them, and re-layouts  1.83 us (4%)
  between operations  0.83 us (2%)
    ppermute x9, waiting for transfers between devices, swap(): lax.ppermute(value, axis, [(i, i ^ mask) for i in range(lax.axis_size(axi...  13 us
    ppermute x9, starting transfers between devices, swap(): lax.ppermute(value, axis, [(i, i ^ mask) for i in range(lax.axis_size(axi...  12.4 us
    pallas_call x5, Pallas kernels, call(): pl.pallas_call(kernel, out_shape=[jax.ShapeDtypeStruct(shape, dtype) for...  12.1 us
    ppermute x2, starting transfers between devices, pair_exchange(): return (lax.ppermute(to_link, axis, links), swap(to_partner, axis, 1))  4.08 us
    ppermute x2, waiting for transfers between devices, pair_exchange(): return (lax.ppermute(to_link, axis, links), swap(to_partner, axis, 1))  2.39 us
    unnamed x22, local copies, waits for them, and re-layouts  1.66 us
  transfers between devices with their start and end apart: 11, of which 9 were waited for; matrix products, arithmetic and copies ran while one was open for 0% of the time, Pallas kernels for 3%

profile of v4, /device:TPU:0, one launch (start us, length us, event | category | flops | bytes accessed | tf_op | source)
XLA Modules:
  0.0 46.8 jit_solution(16818293615151027797)
XLA Ops:
  0.7 0.6 %copy-done.7 = s32[10]{0:T(128)S(1)} copy-done((s32[10]{0:T(128)S(1)}, s32[10]{0:T(128)}, u32[]{:S(2)}) %copy-start.7) | copy-done | bytes 64
  1.3 0.3 copy-done
  1.6 0.0 copy-start.4
  1.7 0.8 %shard_map.179 = (f32[3,128]{1,0:T(4,128)S(1)}, bf16[208,128]{1,0:T(8,128)(2,1)S(1)}, bf16[208,128]{1,0:T(8,128)(2,1)S(1)}) custom-call(s32[10]{0:T(128)S(1)} %copy-done.7, f32[16,128]{1,0:T(8,128)S(1)} %shard_map.178.blank, bf16[4,320,128]{2,1,0:T(8,128)(2,1)S(1)} %copy-done, s32[320]{0:T(512)S(1)} %copy-done.6), custom_call_target="tpu_custom_call" | custom-call | flops 10000000000 | bytes 50337192 | tf_op jit(solution)/shard_map/pallas_call | solution.py:475
  2.5 0.0 copy-start.8
  2.5 0.6 %collective-permute-start = (bf16[208,128]{1,0:T(8,128)(2,1)S(1)}, bf16[208,128]{1,0:T(8,128)(2,1)S(1)}, u32[]{:S(2)}, u32[]{:S(2)}) collective-permute-start(bf16[208,128]{1,0:T(8,128)(2,1)S(1)} %get-tuple-element.32), channel_id=1, source_target_pairs={{0,1},{1,0},{2,3},{3,2},{4,5},{5,4},{6,7},{7,6},{8,9},{9,8},{10,11... | collective-permute-start | bytes 159752 | tf_op jit(solution)/shard_map/ppermute | solution.py:458
  3.0 3.5 %collective-permute-start.1 = (bf16[208,128]{1,0:T(8,128)(2,1)S(1)}, bf16[208,128]{1,0:T(8,128)(2,1)S(1)}, u32[]{:S(2)}, u32[]{:S(2)}) collective-permute-start(bf16[208,128]{1,0:T(8,128)(2,1)S(1)} %get-tuple-element.33), channel_id=1, source_target_pairs={{1,2},{3,4},{5,6},{7,0},{2,1},{4,3},{6,5},{0,7},{9,10},{11,12},{13... | collective-permute-start | bytes 159752 | tf_op jit(solution)/shard_map/ppermute | solution.py:465
  6.6 0.1 broadcast_in_dim.3
  6.7 0.1 stack_reshape.3
  6.7 0.7 %copy-done.9 = f32[128]{0:T(128)S(1)} copy-done((f32[128]{0:T(128)S(1)}, f32[128]{0:T(128)}, u32[]{:S(2)}) %copy-start.9) | copy-done | bytes 536
  7.4 0.0 copy-done.10
  7.4 1.0 %collective-permute-done.1.link_rows = bf16[208,128]{1,0:T(8,128)(2,1)S(1)} collective-permute-done((bf16[208,128]{1,0:T(8,128)(2,1)S(1)}, bf16[208,128]{1,0:T(8,128)(2,1)S(1)}, u32[]{:S(2)}, u32[]{:S(2)}) %collective-permute-start.1) | collective-permute-done | bytes 53280 | tf_op jit(solution)/shard_map/ppermute | solution.py:465
  8.4 8.5 %shard_map.180 = (bf16[4,320,128]{2,1,0:T(8,128)(2,1)}, f32[4,320,128]{2,1,0:T(8,128)S(1)}, f32[4,320,128]{2,1,0:T(8,128)S(1)}, bf16[192,128]{1,0:T(8,128)(2,1)S...) custom-call(f32[3,128]{1,0:T(4,128)S(1)} %get-tuple-element.31.own_codes, ...), custom_call_target="tpu_custom_call" | custom-call | flops 4000000000 | bytes 21092608 | tf_op jit(solution)/shard_map/pallas_call | solution.py:475
  16.9 0.1 collective-permute-start.2
  17.0 1.4 %collective-permute-done.2 = bf16[656,128]{1,0:T(8,128)(2,1)S(1)} collective-permute-done((bf16[656,128]{1,0:T(8,128)(2,1)S(1)}, bf16[656,128]{1,0:T(8,128)(2,1)S(1)}, u32[]{:S(2)}, u32[]{:S(2)}) %collective-permute-start.2) | collective-permute-done | bytes 167968 | tf_op jit(solution)/shard_map/ppermute | solution.py:458
  18.5 1.8 %collective-permute-start.3 = (bf16[328,128]{1,0:T(8,128)(2,1)S(1)}, bf16[328,128]{1,0:T(8,128)(2,1)S(1)}, u32[]{:S(2)}, u32[]{:S(2)}) collective-permute-start(bf16[328,128]{1,0:T(8,128)(2,1)S(1)} %constant_dynamic-slice_fusion), channel_id=1, source_target_pairs={{0,2},{1,3},{2,0},{3,1},{4,6},{5,7},{6,4},{7,5},{8,10},{9,11},{10,... | collective-permute-start | bytes 251912 | tf_op jit(solution)/shard_map/ppermute | solution.py:458
  20.3 3.0 %collective-permute-done.3 = bf16[328,128]{1,0:T(8,128)(2,1)S(1)} collective-permute-done((bf16[328,128]{1,0:T(8,128)(2,1)S(1)}, bf16[328,128]{1,0:T(8,128)(2,1)S(1)}, u32[]{:S(2)}, u32[]{:S(2)}) %collective-permute-start.3) | collective-permute-done | bytes 84000 | tf_op jit(solution)/shard_map/ppermute | solution.py:458
  23.3 1.6 %collective-permute-start.4 = (bf16[328,128]{1,0:T(8,128)(2,1)S(1)}, bf16[328,128]{1,0:T(8,128)(2,1)S(1)}, u32[]{:S(2)}, u32[]{:S(2)}) collective-permute-start(bf16[328,128]{1,0:T(8,128)(2,1)S(1)} %dynamic-slice_add_fusion), channel_id=1, source_target_pairs={{0,4},{1,5},{2,6},{3,7},{4,0},{5,1},{6,2},{7,3},{8,12},{9,13},{10,... | collective-permute-start | bytes 251912 | tf_op jit(solution)/shard_map/ppermute | solution.py:458
  24.9 0.5 %collective-permute-start.5 = (bf16[192,128]{1,0:T(8,128)(2,1)S(1)}, bf16[192,128]{1,0:T(8,128)(2,1)S(1)}, u32[]{:S(2)}, u32[]{:S(2)}) collective-permute-start(bf16[192,128]{1,0:T(8,128)(2,1)S(1)} %get-tuple-element.37), channel_id=1, source_target_pairs={{1,2},{3,4},{5,6},{7,0},{2,1},{4,3},{6,5},{0,7},{9,10},{11,12},{13... | collective-permute-start | bytes 147464 | tf_op jit(solution)/shard_map/ppermute | solution.py:465
  25.4 1.3 %collective-permute-start.6 = (bf16[192,128]{1,0:T(8,128)(2,1)S(1)}, bf16[192,128]{1,0:T(8,128)(2,1)S(1)}, u32[]{:S(2)}, u32[]{:S(2)}) collective-permute-start(bf16[192,128]{1,0:T(8,128)(2,1)S(1)} %get-tuple-element.38), channel_id=1, source_target_pairs={{0,1},{1,0},{2,3},{3,2},{4,5},{5,4},{6,7},{7,6},{8,9},{9,8},{10,11... | collective-permute-start | bytes 147464 | tf_op jit(solution)/shard_map/ppermute | solution.py:458
  26.7 1.1 %collective-permute-done.4 = bf16[328,128]{1,0:T(8,128)(2,1)S(1)} collective-permute-done((bf16[328,128]{1,0:T(8,128)(2,1)S(1)}, bf16[328,128]{1,0:T(8,128)(2,1)S(1)}, u32[]{:S(2)}, u32[]{:S(2)}) %collective-permute-start.4) | collective-permute-done | bytes 84000 | tf_op jit(solution)/shard_map/ppermute | solution.py:458
  27.9 1.4 %collective-permute-done.5.link_back = bf16[192,128]{1,0:T(8,128)(2,1)S(1)} collective-permute-done((bf16[192,128]{1,0:T(8,128)(2,1)S(1)}, bf16[192,128]{1,0:T(8,128)(2,1)S(1)}, u32[]{:S(2)}, u32[]{:S(2)}) %collective-permute-start.5) | collective-permute-done | bytes 49184 | tf_op jit(solution)/shard_map/ppermute | solution.py:465
  29.3 1.8 %collective-permute-start.7 = (bf16[328,128]{1,0:T(8,128)(2,1)S(1)}, bf16[328,128]{1,0:T(8,128)(2,1)S(1)}, u32[]{:S(2)}, u32[]{:S(2)}) collective-permute-start(bf16[328,128]{1,0:T(8,128)(2,1)S(1)} %add.31), channel_id=1, source_target_pairs={{0,8},{8,0},{16,24},{24,16},{1,9},{9,1},{17,25},{25,17},{2,10},{10... | collective-permute-start | bytes 251912 | tf_op jit(solution)/shard_map/ppermute | solution.py:458
  31.1 2.7 %collective-permute-done.7 = bf16[328,128]{1,0:T(8,128)(2,1)S(1)} collective-permute-done((bf16[328,128]{1,0:T(8,128)(2,1)S(1)}, bf16[328,128]{1,0:T(8,128)(2,1)S(1)}, u32[]{:S(2)}, u32[]{:S(2)}) %collective-permute-start.7) | collective-permute-done | bytes 84000 | tf_op jit(solution)/shard_map/ppermute | solution.py:458
  33.8 2.9 %collective-permute-start.8 = (bf16[328,128]{1,0:T(8,128)(2,1)S(1)}, bf16[328,128]{1,0:T(8,128)(2,1)S(1)}, u32[]{:S(2)}, u32[]{:S(2)}) collective-permute-start(bf16[328,128]{1,0:T(8,128)(2,1)S(1)} %add.32), channel_id=1, source_target_pairs={{0,16},{8,24},{16,0},{24,8},{1,17},{9,25},{17,1},{25,9},{2,18},{10... | collective-permute-start | bytes 251912 | tf_op jit(solution)/shard_map/ppermute | solution.py:458
  36.6 1.6 %shard_map.181 = bf16[4,320,128]{2,1,0:T(8,128)(2,1)} custom-call(bf16[4,320,128]{2,1,0:T(8,128)(2,1)S(1)} %copy-done, f32[3,128]{1,0:T(4,128)S(1)} %pad_maximum_fusion.vectors.gain, f32[4,320,128]{2,1,0:T(8,128)S(1)} %get-tuple-element.40.back_norm, f32[4,320,128]{2,1,0:T(8,128)S(1)} %get-tuple-element.41.back_res, ...), custom_call_target="tpu_custom_call" | custom-call | flops 100000000 | bytes 2238240 | tf_op jit(solution)/shard_map/pallas_call | solution.py:475
  38.3 0.9 %collective-permute-done.8 = bf16[328,128]{1,0:T(8,128)(2,1)S(1)} collective-permute-done((bf16[328,128]{1,0:T(8,128)(2,1)S(1)}, bf16[328,128]{1,0:T(8,128)(2,1)S(1)}, u32[]{:S(2)}, u32[]{:S(2)}) %collective-permute-start.8) | collective-permute-done | bytes 84000 | tf_op jit(solution)/shard_map/ppermute | solution.py:458
  39.2 2.4 %collective-permute-start.9 = (bf16[328,128]{1,0:T(8,128)(2,1)S(1)}, bf16[328,128]{1,0:T(8,128)(2,1)S(1)}, u32[]{:S(2)}, u32[]{:S(2)}) collective-permute-start(bf16[328,128]{1,0:T(8,128)(2,1)S(1)} %add.33), channel_id=1, source_target_pairs={{0,2},{1,3},{2,0},{3,1},{4,6},{5,7},{6,4},{7,5},{8,10},{9,11},{10,... | collective-permute-start | bytes 251912 | tf_op jit(solution)/shard_map/ppermute | solution.py:458
  41.7 2.4 %collective-permute-done.9 = bf16[328,128]{1,0:T(8,128)(2,1)S(1)} collective-permute-done((bf16[328,128]{1,0:T(8,128)(2,1)S(1)}, bf16[328,128]{1,0:T(8,128)(2,1)S(1)}, u32[]{:S(2)}, u32[]{:S(2)}) %collective-permute-start.9) | collective-permute-done | bytes 84000 | tf_op jit(solution)/shard_map/ppermute | solution.py:458
  44.2 0.1 collective-permute-start.10
  44.3 1.4 %collective-permute-done.10.other = bf16[656,128]{1,0:T(8,128)(2,1)S(1)} collective-permute-done((bf16[656,128]{1,0:T(8,128)(2,1)S(1)}, bf16[656,128]{1,0:T(8,128)(2,1)S(1)}, u32[]{:S(2)}, u32[]{:S(2)}) %collective-permute-start.10) | collective-permute-done | bytes 167968 | tf_op jit(solution)/shard_map/ppermute | solution.py:458
  45.6 1.2 %shard_map.182 = (f32[1,128]{1,0:T(1,128)}, f32[128,384]{1,0:T(8,128)}, f32[128,128]{1,0:T(8,128)}, f32[1,4]{1,0:T(1,128)}, f32[1,128]{1,0:T(1,128)}, /*index=5*/f32[128,512]{1,0:T(8,128)}, f32[256,128]{1,0:T(8,128)}) custom-call(bf16[656,128]{1,0:T(8,128)(2,1)S(1)} %maximum_select_fusion.own, bf16[656,128]{1,0:T(8,128)(2,1)S(1)} %collective-permute-done.10.other), custom_call_target="tpu_custom_call" | custom-call | bytes 335872 | tf_op jit(solution)/shard_map/pallas_call | solution.py:475
  (27 shorter events, 0.3 us)
Async XLA Ops:
  0.6 0.7 %copy-start.7 = (s32[10]{0:T(128)S(1)}, s32[10]{0:T(128)}, u32[]{:S(2)}) copy-start(s32[10]{0:T(128)} %valid.1) | copy-start | bytes 124
  0.7 1.0 %copy-start = (bf16[4,320,128]{2,1,0:T(8,128)(2,1)S(1)}, bf16[4,320,128]{2,1,0:T(8,128)(2,1)}, u32[]{:S(2)}) copy-start(bf16[4,320,128]{2,1,0:T(8,128)(2,1)} %state.5) | copy-start | bytes 983044
  0.7 1.0 %copy-start.6 = (s32[320]{0:T(512)S(1)}, s32[320]{0:T(512)}, u32[]{:S(2)}) copy-start(s32[320]{0:T(512)} %token_.1) | copy-start | bytes 3844
  1.6 6.8 %copy-start.1 = (bf16[4,320,128]{2,1,0:T(8,128)(2,1)S(1)}, bf16[4,320,128]{2,1,0:T(8,128)(2,1)}, u32[]{:S(2)}) copy-start(bf16[4,320,128]{2,1,0:T(8,128)(2,1)} %cot.1) | copy-start | bytes 983044
  1.6 6.8 %copy-start.2 = (bf16[128,512]{1,0:T(8,128)(2,1)S(1)}, bf16[128,512]{1,0:T(8,128)(2,1)}, u32[]{:S(2)}) copy-start(bf16[128,512]{1,0:T(8,128)(2,1)} %transit_weight.1) | copy-start | bytes 393220
  1.6 6.8 %copy-start.3 = (bf16[128,384]{1,0:T(8,128)(2,1)S(1)}, bf16[128,384]{1,0:T(8,128)(2,1)}, u32[]{:S(2)}) copy-start(bf16[128,384]{1,0:T(8,128)(2,1)} %project_weight.1) | copy-start | bytes 294916
  1.6 6.8 %copy-start.4 = (bf16[256,128]{1,0:T(8,128)(2,1)S(1)}, bf16[256,128]{1,0:T(8,128)(2,1)}, u32[]{:S(2)}) copy-start(bf16[256,128]{1,0:T(8,128)(2,1)} %return_weight.1) | copy-start | bytes 196612
  1.7 6.8 %copy-start.5 = (bf16[128,128]{1,0:T(8,128)(2,1)S(1)}, bf16[128,128]{1,0:T(8,128)(2,1)}, u32[]{:S(2)}) copy-start(bf16[128,128]{1,0:T(8,128)(2,1)} %output_weight.1) | copy-start | bytes 98308
  2.5 4.1 %copy-start.8 = (f32[4]{0:T(128)S(1)}, f32[4]{0:T(128)}, u32[]{:S(2)}) copy-start(f32[4]{0:T(128)} %param.17) | copy-start | bytes 52
  2.5 4.9 %collective-permute-start = (bf16[208,128]{1,0:T(8,128)(2,1)S(1)}, bf16[208,128]{1,0:T(8,128)(2,1)S(1)}, u32[]{:S(2)}, u32[]{:S(2)}) collective-permute-start(bf16[208,128]{1,0:T(8,128)(2,1)S(1)} %get-tuple-element.32), channel_id=1, source_target_pairs={{0,1},{1,0},{2,3},{3,2},{4,5},{5,4},{6,7},{7,6},{8,9},{9,8},{10,11... | collective-permute-start | bytes 159752 | tf_op jit(solution)/shard_map/ppermute | solution.py:458
  3.0 5.4 %collective-permute-start.1 = (bf16[208,128]{1,0:T(8,128)(2,1)S(1)}, bf16[208,128]{1,0:T(8,128)(2,1)S(1)}, u32[]{:S(2)}, u32[]{:S(2)}) collective-permute-start(bf16[208,128]{1,0:T(8,128)(2,1)S(1)} %get-tuple-element.33), channel_id=1, source_target_pairs={{1,2},{3,4},{5,6},{7,0},{2,1},{4,3},{6,5},{0,7},{9,10},{11,12},{13... | collective-permute-start | bytes 159752 | tf_op jit(solution)/shard_map/ppermute | solution.py:465
  6.7 0.7 %copy-start.9 = (f32[128]{0:T(128)S(1)}, f32[128]{0:T(128)}, u32[]{:S(2)}) copy-start(f32[128]{0:T(128)} %param.18) | copy-start | bytes 1540
  6.7 0.7 %copy-start.10 = (f32[128]{0:T(128)S(1)}, f32[128]{0:T(128)}, u32[]{:S(2)}) copy-start(f32[128]{0:T(128)} %param.14) | copy-start | bytes 1540
  16.9 1.5 %collective-permute-start.2 = (bf16[656,128]{1,0:T(8,128)(2,1)S(1)}, bf16[656,128]{1,0:T(8,128)(2,1)S(1)}, u32[]{:S(2)}, u32[]{:S(2)}) collective-permute-start(bf16[656,128]{1,0:T(8,128)(2,1)S(1)} %get-tuple-element.36), channel_id=1, source_target_pairs={{0,1},{1,0},{2,3},{3,2},{4,5},{5,4},{6,7},{7,6},{8,9},{9,8},{10,11... | collective-permute-start | bytes 503816 | tf_op jit(solution)/shard_map/ppermute | solution.py:458
  18.5 4.8 %collective-permute-start.3 = (bf16[328,128]{1,0:T(8,128)(2,1)S(1)}, bf16[328,128]{1,0:T(8,128)(2,1)S(1)}, u32[]{:S(2)}, u32[]{:S(2)}) collective-permute-start(bf16[328,128]{1,0:T(8,128)(2,1)S(1)} %constant_dynamic-slice_fusion), channel_id=1, source_target_pairs={{0,2},{1,3},{2,0},{3,1},{4,6},{5,7},{6,4},{7,5},{8,10},{9,11},{10,... | collective-permute-start | bytes 251912 | tf_op jit(solution)/shard_map/ppermute | solution.py:458
  23.3 4.5 %collective-permute-start.4 = (bf16[328,128]{1,0:T(8,128)(2,1)S(1)}, bf16[328,128]{1,0:T(8,128)(2,1)S(1)}, u32[]{:S(2)}, u32[]{:S(2)}) collective-permute-start(bf16[328,128]{1,0:T(8,128)(2,1)S(1)} %dynamic-slice_add_fusion), channel_id=1, source_target_pairs={{0,4},{1,5},{2,6},{3,7},{4,0},{5,1},{6,2},{7,3},{8,12},{9,13},{10,... | collective-permute-start | bytes 251912 | tf_op jit(solution)/shard_map/ppermute | solution.py:458
  24.9 4.4 %collective-permute-start.5 = (bf16[192,128]{1,0:T(8,128)(2,1)S(1)}, bf16[192,128]{1,0:T(8,128)(2,1)S(1)}, u32[]{:S(2)}, u32[]{:S(2)}) collective-permute-start(bf16[192,128]{1,0:T(8,128)(2,1)S(1)} %get-tuple-element.37), channel_id=1, source_target_pairs={{1,2},{3,4},{5,6},{7,0},{2,1},{4,3},{6,5},{0,7},{9,10},{11,12},{13... | collective-permute-start | bytes 147464 | tf_op jit(solution)/shard_map/ppermute | solution.py:465
  25.4 3.9 %collective-permute-start.6 = (bf16[192,128]{1,0:T(8,128)(2,1)S(1)}, bf16[192,128]{1,0:T(8,128)(2,1)S(1)}, u32[]{:S(2)}, u32[]{:S(2)}) collective-permute-start(bf16[192,128]{1,0:T(8,128)(2,1)S(1)} %get-tuple-element.38), channel_id=1, source_target_pairs={{0,1},{1,0},{2,3},{3,2},{4,5},{5,4},{6,7},{7,6},{8,9},{9,8},{10,11... | collective-permute-start | bytes 147464 | tf_op jit(solution)/shard_map/ppermute | solution.py:458
  29.3 4.5 %collective-permute-start.7 = (bf16[328,128]{1,0:T(8,128)(2,1)S(1)}, bf16[328,128]{1,0:T(8,128)(2,1)S(1)}, u32[]{:S(2)}, u32[]{:S(2)}) collective-permute-start(bf16[328,128]{1,0:T(8,128)(2,1)S(1)} %add.31), channel_id=1, source_target_pairs={{0,8},{8,0},{16,24},{24,16},{1,9},{9,1},{17,25},{25,17},{2,10},{10... | collective-permute-start | bytes 251912 | tf_op jit(solution)/shard_map/ppermute | solution.py:458
  33.8 5.4 %collective-permute-start.8 = (bf16[328,128]{1,0:T(8,128)(2,1)S(1)}, bf16[328,128]{1,0:T(8,128)(2,1)S(1)}, u32[]{:S(2)}, u32[]{:S(2)}) collective-permute-start(bf16[328,128]{1,0:T(8,128)(2,1)S(1)} %add.32), channel_id=1, source_target_pairs={{0,16},{8,24},{16,0},{24,8},{1,17},{9,25},{17,1},{25,9},{2,18},{10... | collective-permute-start | bytes 251912 | tf_op jit(solution)/shard_map/ppermute | solution.py:458
  39.2 4.9 %collective-permute-start.9 = (bf16[328,128]{1,0:T(8,128)(2,1)S(1)}, bf16[328,128]{1,0:T(8,128)(2,1)S(1)}, u32[]{:S(2)}, u32[]{:S(2)}) collective-permute-start(bf16[328,128]{1,0:T(8,128)(2,1)S(1)} %add.33), channel_id=1, source_target_pairs={{0,2},{1,3},{2,0},{3,1},{4,6},{5,7},{6,4},{7,5},{8,10},{9,11},{10,... | collective-permute-start | bytes 251912 | tf_op jit(solution)/shard_map/ppermute | solution.py:458
  44.2 1.5 %collective-permute-start.10 = (bf16[656,128]{1,0:T(8,128)(2,1)S(1)}, bf16[656,128]{1,0:T(8,128)(2,1)S(1)}, u32[]{:S(2)}, u32[]{:S(2)}) collective-permute-start(bf16[656,128]{1,0:T(8,128)(2,1)S(1)} %maximum_select_fusion.own), channel_id=1, source_target_pairs={{0,1},{1,0},{2,3},{3,2},{4,5},{5,4},{6,7},{7,6},{8,9},{9,8},{10,11... | collective-permute-start | bytes 503816 | tf_op jit(solution)/shard_map/ppermute | solution.py:458

commit v5 on v4

--- a/solution.py
+++ b/solution.py
@@ -94,11 +94,96 @@
     return jnp.where(here, jnp.broadcast_to(line, (rows, LANES)), 0.0)
 
 
+def is_inner(w, atoms):
+    return w * QWIN >= HALO and w * QWIN + KWIN - HALO <= atoms
+
+
+def down_lanes(row):
+    return jnp.transpose(jnp.broadcast_to(row, (LANES, LANES)))
+
+
+def fill_own_codes(codes, own_codes, atoms):
+    for i in range(own_codes.shape[0]):
+        count = min(LANES, atoms - i * LANES)
+        start = HALO + i * LANES
+        codes[start : start + count, :] = down_lanes(own_codes[i : i + 1, :])[0:count]
+
+
+def query_row(own_codes, w):
+    row, lane = divmod(w * QWIN, LANES)
+    return jnp.concatenate([own_codes[row : row + 1, lane : lane + QWIN]] * HEADS, axis=1)
+
+
+def window_mask(codes, own_codes, w):
+    key_code = codes[w * QWIN : w * QWIN + KWIN, :]
+    return key_code, key_code == query_row(own_codes, w)
+
+
+def attend_windows(picked, samples, query_of, key_of, value_of, codes, own_codes, bias_row, probs, att):
+    scale = 1.0 / math.sqrt(LANES // HEADS)
+    units = [(w, s) for w in picked for s in range(samples)]
+    scores = [mm_nt(key_of(s, w), spread_heads(query_of(s, w))) for w, s in units]
+    offsets = {}
+    for w in picked:
+        key_code, same = window_mask(codes, own_codes, w)
+        offset = jnp.where(same, bias_row * LOG2E, 0.0)
+        offsets[w] = jnp.where(key_code > 0, offset, -1e30)
+    packed = []
+    for (w, s), score in zip(units, scores):
+        score = score * (scale * LOG2E) + offsets[w]
+        weights = jnp.exp2(score - jnp.max(score, axis=0, keepdims=True))
+        weights = weights * (1.0 / column_sum(weights))
+        probs[w * samples + s] = weights
+        packed.append(weights.astype(BF16))
+    outcomes = [mm_tn(weights, value_of(s, w)) for (w, s), weights in zip(units, packed)]
+    for (w, s), outcome in zip(units, outcomes):
+        att[s, w * QWIN : (w + 1) * QWIN, :] = gather_heads(outcome).astype(BF16)
+
+
+def inner_kernel(
+    own_codes, vectors, state, project_weight, norm_own, unit_own, q_own, k_own, v_own, probs, att, codes
+):
+    samples, atoms, channels = state.shape
+    fill_own_codes(codes, own_codes, atoms)
+    for s in range(samples):
+        unit, _ = split_norm(state[s].astype(F32))
+        unit_own[s] = unit
+        normed = (unit * vectors[0:1, :]).astype(BF16)
+        norm_own[s] = normed
+        projected = mm(normed, project_weight[...]).astype(BF16)
+        q_own[s] = projected[:, :channels]
+        k_own[s] = projected[:, channels : 2 * channels]
+        v_own[s] = projected[:, 2 * channels :]
+
+    def own_window(ref, s, w):
+        return ref[s, w * QWIN - HALO : w * QWIN - HALO + KWIN, :]
+
+    attend_windows(
+        [w for w in range(atoms // QWIN) if is_inner(w, atoms)],
+        samples,
+        lambda s, w: q_own[s, w * QWIN : (w + 1) * QWIN, :],
+        lambda s, w: own_window(k_own, s, w),
+        lambda s, w: own_window(v_own, s, w),
+        codes,
+        own_codes,
+        vectors[2:3, :],
+        probs,
+        att,
+    )
+
+
 def block_kernel(
     own_codes,
     pair_rows,
     link_rows,
     vectors,
+    norm_own,
+    unit_own,
+    q_all,
+    k_own,
+    v_own,
+    probs_own,
+    att_own,
     state,
     project_weight,
     output_weight,
@@ -112,9 +197,8 @@
     to_link,
     packed_keep,
     packed_send,
-    norm_ext,
-    unit_ext,
-    q_all,
+    norm_rim,
+    unit_rim,
     k_all,
     v_all,
     codes,
@@ -145,16 +229,11 @@
         low = part[halo_rows + 1 : halo_rows + 2, :].astype(F32)
         return high * 256.0 + low
 
-    def down_lanes(row):
-        return jnp.transpose(jnp.broadcast_to(row, (LANES, LANES)))
-
     first_code = jnp.where(place == 0, 0.0, edge_codes(before))
     last_code = jnp.where(place == places - 1, 0.0, edge_codes(after))
     last_lane = (atoms - HALO) % LANES
     codes[0:HALO, :] = down_lanes(first_code)[last_lane : last_lane + HALO]
-    for i in range(own_codes.shape[0]):
-        count = min(LANES, atoms - i * LANES)
-        codes[HALO + i * LANES : HALO + i * LANES + count, :] = down_lanes(own_codes[i : i + 1, :])[0:count]
+    fill_own_codes(codes, own_codes, atoms)
     codes[HALO + atoms : ext, :] = down_lanes(last_code)[0:HALO]
 
     bias_acc[...] = jnp.zeros_like(bias_acc)
@@ -164,64 +243,52 @@
     gain_one = vectors[0:1, :]
     gain_two = vectors[1:2, :]
     bias_row = vectors[2:3, :]
+    keep_rows = KWIN - QWIN + HALO
+    keep_rows = min(atoms, keep_rows + QWIN)
+    both_rims = jnp.concatenate([before[:halo_rows], after[:halo_rows]], axis=0).astype(F32)
+    unit, _ = split_norm(both_rims)
+    unit_rim[...] = unit
+    normed = (unit * gain_one).astype(BF16)
+    norm_rim[...] = normed
+    rim_pairs = mm(normed, project_weight[:, channels:]).astype(BF16)
+    for ref, own, column in ((k_all, k_own, 0), (v_all, v_own, channels)):
+        part = rim_pairs[:, column : column + channels]
+        for s in range(samples):
+            ref[s, :HALO, :] = part[s * HALO : (s + 1) * HALO]
+            ref[s, HALO : HALO + keep_rows, :] = own[s, :keep_rows, :]
+            ref[s, HALO + atoms - keep_rows : HALO + atoms, :] = own[s, atoms - keep_rows :, :]
+            ref[s, HALO + atoms :, :] = part[halo_rows + s * HALO : halo_rows + (s + 1) * HALO]
+
+    def pair_window(ext_ref, own_ref, s, w):
+        if is_inner(w, atoms):
+            return own_ref[s, w * QWIN - HALO : w * QWIN - HALO + KWIN, :]
+        return ext_ref[s, w * QWIN : w * QWIN + KWIN, :]
+
+    def key_of(s, w):
+        return pair_window(k_all, k_own, s, w)
+
+    def value_of(s, w):
+        return pair_window(v_all, v_own, s, w)
+
+    def query_of(s, w):
+        return q_all[s, w * QWIN : (w + 1) * QWIN, :]
+
+    def prob_of(s, w):
+        return (probs_own if is_inner(w, atoms) else probs)[w * samples + s]
+
+    outer = [w for w in range(windows) if not is_inner(w, atoms)]
+    attend_windows(
+        outer, samples, query_of, key_of, value_of, codes, own_codes, bias_row, probs, att
+    )
     for s in range(samples):
-        rows = jnp.concatenate(
-            [before[s * HALO : (s + 1) * HALO], state[s], after[s * HALO : (s + 1) * HALO]], axis=0
-        ).astype(F32)
-        unit, _ = split_norm(rows)
-        unit_ext[s] = unit
-        normed = (unit * gain_one).astype(BF16)
-        norm_ext[s] = normed
-        projected = mm(normed, project_weight[...]).astype(BF16)
-        q_all[s] = projected[HALO : HALO + atoms, :channels]
-        k_all[s] = projected[:, channels : 2 * channels]
-        v_all[s] = projected[:, 2 * channels :]
-
-    def query_row(w):
-        row, lane = divmod(w * QWIN, LANES)
-        return jnp.concatenate([own_codes[row : row + 1, lane : lane + QWIN]] * HEADS, axis=1)
-
-    query_rows = [query_row(w) for w in range(windows)]
-
-    def window_mask(w):
-        key_code = codes[w * QWIN : w * QWIN + KWIN, :]
-        return key_code, key_code == query_rows[w]
+        for w in range(windows):
+            if is_inner(w, atoms):
+                span = slice(w * QWIN, (w + 1) * QWIN)
+                att[s, span, :] = att_own[s, span, :]
 
     def group_units(g):
         starts = [(g * GROUP + i) * QWIN for i in range(GROUP)]
         return starts, [(i, s) for i in range(GROUP) for s in range(samples)]
-
-    def forward_group(g, carry):
-        starts, units = group_units(g)
-        scores = [
-            mm_nt(
-                k_all[s, pl.ds(starts[i], KWIN), :],
-                spread_heads(q_all[s, pl.ds(starts[i], QWIN), :]),
-            )
-            for i, s in units
-        ]
-        offsets = []
-        for i in range(GROUP):
-            key_code, same = window_mask(g * GROUP + i)
-            offset = jnp.where(same, bias_row * LOG2E, 0.0)
-            offsets.append(jnp.where(key_code > 0, offset, -1e30))
-        packed = []
-        for (i, s), score in zip(units, scores):
-            score = score * (scale * LOG2E) + offsets[i]
-            weights = jnp.exp2(score - jnp.max(score, axis=0, keepdims=True))
-            weights = weights * (1.0 / column_sum(weights))
-            probs[(g * GROUP + i) * samples + s] = weights
-            packed.append(weights.astype(BF16))
-        outcomes = [
-            mm_tn(weights, v_all[s, pl.ds(starts[i], KWIN), :])
-            for (i, s), weights in zip(units, packed)
-        ]
-        for (i, s), outcome in zip(units, outcomes):
-            att[s, pl.ds(starts[i], QWIN), :] = gather_heads(outcome).astype(BF16)
-        return carry
-
-    for g in range(windows // GROUP):
-        forward_group(g, 0)
 
     chunk_rows = CHUNK * atoms
 
@@ -270,13 +337,13 @@
         starts, units = group_units(g)
         backs = [spread_heads(d_att[s, pl.ds(starts[i], QWIN), :]) for i, s in units]
         back_weights = [
-            mm_nt(v_all[s, pl.ds(starts[i], KWIN), :], back) for (i, s), back in zip(units, backs)
+            mm_nt(value_of(s, g * GROUP + i), back) for (i, s), back in zip(units, backs)
         ]
         packed = []
         scores16 = []
         bias_parts = [None] * GROUP
         for (i, s), back_weight in zip(units, back_weights):
-            weights = probs[(g * GROUP + i) * samples + s]
+            weights = prob_of(s, g * GROUP + i)
             weighted = weights * back_weight
             back_scores = weighted - weights * column_sum(weighted)
             bias_parts[i] = back_scores if bias_parts[i] is None else bias_parts[i] + back_scores
@@ -288,7 +355,7 @@
             for (i, s), scores in zip(units, scores16)
         ]
         back_queries = [
-            mm_tn(scores, k_all[s, pl.ds(starts[i], KWIN), :])
+            mm_tn(scores, key_of(s, g * GROUP + i))
             for (i, s), scores in zip(units, scores16)
         ]
         for (i, s), value, key, query in zip(units, back_values, back_keys, back_queries):
@@ -297,7 +364,7 @@
             dk_all[s, span, :] += key
             dq_all[s, pl.ds(starts[i], QWIN), :] = gather_heads(query)
         for i, bias_part in enumerate(bias_parts):
-            _, same = window_mask(g * GROUP + i)
+            _, same = window_mask(codes, own_codes, g * GROUP + i)
             bias_acc[...] += jnp.where(same, bias_part, 0.0)
         return carry
 
@@ -315,8 +382,18 @@
             parts.append(jnp.concatenate([back_q, back_k, dv_all[s].astype(BF16)], axis=1))
         back_all = jnp.concatenate(parts, axis=0)
         back_normed = mm_nt(back_all, project_weight[...])
-        normed = norm_ext[pl.ds(c * SPAN, SPAN)].reshape(SPAN * ext, channels)
-        unit = unit_ext[pl.ds(c * SPAN, SPAN)].reshape(SPAN * ext, channels)
+
+        def with_rims(own, rims):
+            pieces = []
+            for i in range(SPAN):
+                s = c * SPAN + i
+                low = rims[s * HALO : (s + 1) * HALO, :]
+                high = rims[halo_rows + s * HALO : halo_rows + (s + 1) * HALO, :]
+                pieces += [low, own[s], high]
+            return jnp.concatenate(pieces, axis=0)
+
+        normed = with_rims(norm_own, norm_rim)
+        unit = with_rims(unit_own, unit_rim)
         grad_project = mm_tn(normed, back_all)
         for i in range(3):
             project_grads[c, pl.ds(i * channels, channels), :] = grad_project[:, i * LANES : (i + 1) * LANES]
@@ -363,23 +440,15 @@
     out[...] = jnp.zeros_like(out)
 
 
-def pack_kernel(valid, blank, state, token, own_codes, partner, link, line, sem):
+def pack_kernel(valid, blank, state, token, own_codes, partner, link, line):
     samples, atoms, _ = state.shape
     odd = lax.axis_index("atom") % 2
-    copies = []
     for target, start in (
         (partner, (1 - odd) * (atoms - HALO)),
         (link, odd * (atoms - HALO)),
     ):
         for s in range(samples):
-            copies.append(
-                pltpu.make_async_copy(
-                    state.at[s, pl.ds(pl.multiple_of(start, 16), HALO)],
-                    target.at[pl.ds(s * HALO, HALO)],
-                    sem.at[len(copies)],
-                )
-            )
-            copies[-1].start()
+            target[s * HALO : (s + 1) * HALO, :] = state[s, pl.ds(pl.multiple_of(start, 16), HALO), :]
     rows = own_codes.shape[0]
     line[...] = jnp.zeros_like(line)
     line[:, :atoms] = token[...].reshape(1, atoms)
@@ -403,8 +472,6 @@
     base = samples * HALO
     partner[base:, :] = jnp.where(odd == 1, ends[0], ends[1]).astype(BF16)
     link[base:, :] = jnp.where(odd == 1, ends[1], ends[0]).astype(BF16)
-    for copy in copies:
-        copy.wait()
 
 
 def rim_kernel(state, gain, back_norm, back_res, pair_back, link_back, out):
@@ -467,7 +534,6 @@
 
 VMEM = pl.BlockSpec(memory_space=pltpu.VMEM)
 SMEM = pl.BlockSpec(memory_space=pltpu.SMEM)
-HBM = pl.BlockSpec(memory_space=pltpu.HBM)
 
 
 def call(kernel, operands, specs, outs, scratch=(), flops=0, limit=16):
@@ -511,7 +577,7 @@
     own_codes, to_partner, to_link = call(
         pack_kernel,
         (window_valid, blank, atom_state, atom_token),
-        (SMEM, VMEM, HBM, VMEM),
+        (SMEM, VMEM, VMEM, VMEM),
         (
             ((code_rows, LANES), F32),
             ((pack_rows, channels), BF16),
@@ -519,12 +585,28 @@
         ),
         (
             pltpu.VMEM((1, code_rows * LANES), jnp.int32),
-            pltpu.SemaphoreType.DMA((2 * samples,)),
         ),
         flops=10_000_000_000,
     )
     link_rows, pair_rows = pair_exchange(to_partner, to_link, "atom")
     vectors = jnp.stack([attend_gain, transit_gain, jnp.repeat(token_bias, QWIN)])
+    rows_shape = (samples, atoms, channels)
+    inner = call(
+        inner_kernel,
+        (own_codes, vectors, atom_state, project_weight),
+        (VMEM,) * 4,
+        (
+            (rows_shape, BF16),
+            (rows_shape, F32),
+            (rows_shape, BF16),
+            (rows_shape, BF16),
+            (rows_shape, BF16),
+            ((windows * samples, KWIN, HEADS * QWIN), F32),
+            (rows_shape, BF16),
+        ),
+        (pltpu.VMEM((ext, LANES), F32),),
+        flops=2_000_000_000,
+    )
     block_out, back_norm, back_res, to_partner, to_link, keep, send = call(
         block_kernel,
         (
@@ -532,6 +614,7 @@
             pair_rows,
             link_rows,
             vectors,
+            *inner,
             atom_state,
             project_weight,
             output_weight,
@@ -539,7 +622,7 @@
             return_weight,
             cotangent,
         ),
-        (VMEM,) * 10,
+        (VMEM,) * 17,
         (
             ((samples, atoms, channels), BF16),
             ((samples, atoms, channels), F32),
@@ -550,9 +633,8 @@
             ((half, channels), BF16),
         ),
         (
-            pltpu.VMEM((samples, ext, channels), BF16),
-            pltpu.VMEM((samples, ext, channels), F32),
-            pltpu.VMEM((samples, atoms, channels), BF16),
+            pltpu.VMEM((2 * halo_rows, channels), BF16),
+            pltpu.VMEM((2 * halo_rows, channels), F32),
             pltpu.VMEM((samples, ext, channels), BF16),
             pltpu.VMEM((samples, ext, channels), BF16),
             pltpu.VMEM((ext, LANES), F32),
@@ -568,7 +650,7 @@
             pltpu.VMEM((KWIN, HEADS * QWIN), F32),
         ),
         flops=4_000_000_000,
-        limit=48,
+        limit=24,
     )
 
     link_back, pair_back = pair_exchange(to_partner, to_link, "atom")

time: 47 us -> 45.6 us (0.970)
  waiting for transfers between devices: 15.3 us -> 14.4 us
  local copies, waits for them, and re-layouts: 1.83 us -> 1.16 us
  Pallas kernels: 12.1 us -> 12.6 us
    ppermute x2, waiting for transfers between devices: 2.39 us -> 1.39 us  [pair_exchange(): return (lax.ppermute(to_link, axis, links), swap(to_partner, axis, 1))]
    unnamed x22, local copies, waits for them, and re-layouts: 1.66 us -> 0.99 us
    pallas_call x5 -> x6, Pallas kernels: 12.1 us -> 12.6 us  [call(): pl.pallas_call(kernel, out_shape=[jax.ShapeDtypeStruct(shape, dtype) for...]
  transfers between devices with their start and end apart: 11 -> 11, of which waited for: 9 -> 8; matrix products, arithmetic and copies ran while one was open for 0% -> 0% of each run, Pallas kernels for 3% -> 7%
where the time goes in v5:
time: 45.6 us; the launch traced here: 45.5 us
  starting transfers between devices  16.2 us (36%)
  waiting for transfers between devices  14.4 us (32%)
  Pallas kernels  12.6 us (28%)
  local copies, waits for them, and re-layouts  1.16 us (3%)
  between operations  0.89 us (2%)
    ppermute x9, waiting for transfers between devices, swap(): lax.ppermute(value, axis, [(i, i ^ mask) for i in range(lax.axis_size(axi...  13 us
    pallas_call x6, Pallas kernels, call(): pl.pallas_call(kernel, out_shape=[jax.ShapeDtypeStruct(shape, dtype) for...  12.6 us
    ppermute x9, starting transfers between devices, swap(): lax.ppermute(value, axis, [(i, i ^ mask) for i in range(lax.axis_size(axi...  12.1 us
    ppermute x2, starting transfers between devices, pair_exchange(): return (lax.ppermute(to_link, axis, links), swap(to_partner, axis, 1))  4.08 us
    ppermute x2, waiting for transfers between devices, pair_exchange(): return (lax.ppermute(to_link, axis, links), swap(to_partner, axis, 1))  1.39 us
    unnamed x22, local copies, waits for them, and re-layouts  0.99 us
  transfers between devices with their start and end apart: 11, of which 8 were waited for; matrix products, arithmetic and copies ran while one was open for 0% of the time, Pallas kernels for 7%

profile of v5, /device:TPU:0, one launch (start us, length us, event | category | flops | bytes accessed | tf_op | source)
XLA Modules:
  0.0 45.5 jit_solution(13200691574663523265)
XLA Ops:
  0.7 0.9 %copy-done = bf16[4,320,128]{2,1,0:T(8,128)(2,1)S(1)} copy-done((bf16[4,320,128]{2,1,0:T(8,128)(2,1)S(1)}, bf16[4,320,128]{2,1,0:T(8,128)(2,1)}, u32[]{:S(2)}) %copy-start) | copy-done | bytes 327704
  1.6 0.0 copy-start.10
  1.6 0.0 copy-start.3
  1.7 0.6 %shard_map.179 = (f32[3,128]{1,0:T(4,128)S(1)}, bf16[208,128]{1,0:T(8,128)(2,1)S(1)}, bf16[208,128]{1,0:T(8,128)(2,1)S(1)}) custom-call(s32[10]{0:T(128)S(1)} %copy-done.7, f32[16,128]{1,0:T(8,128)S(1)} %shard_map.178.blank, bf16[4,320,128]{2,1,0:T(8,128)(2,1)S(1)} %copy-done, s32[320]{0:T(512)S(1)} %copy-done.6), custom_call_target="tpu_custom_call" | custom-call | flops 10000000000 | bytes 50337192 | tf_op jit(solution)/shard_map/pallas_call | solution.py:541
  2.2 0.6 %collective-permute-start = (bf16[208,128]{1,0:T(8,128)(2,1)S(1)}, bf16[208,128]{1,0:T(8,128)(2,1)S(1)}, u32[]{:S(2)}, u32[]{:S(2)}) collective-permute-start(bf16[208,128]{1,0:T(8,128)(2,1)S(1)} %get-tuple-element.39), channel_id=1, source_target_pairs={{0,1},{1,0},{2,3},{3,2},{4,5},{5,4},{6,7},{7,6},{8,9},{9,8},{10,11... | collective-permute-start | bytes 159752 | tf_op jit(solution)/shard_map/ppermute | solution.py:525
  2.8 3.5 %collective-permute-start.1 = (bf16[208,128]{1,0:T(8,128)(2,1)S(1)}, bf16[208,128]{1,0:T(8,128)(2,1)S(1)}, u32[]{:S(2)}, u32[]{:S(2)}) collective-permute-start(bf16[208,128]{1,0:T(8,128)(2,1)S(1)} %get-tuple-element.40), channel_id=1, source_target_pairs={{1,2},{3,4},{5,6},{7,0},{2,1},{4,3},{6,5},{0,7},{9,10},{11,12},{13... | collective-permute-start | bytes 159752 | tf_op jit(solution)/shard_map/ppermute | solution.py:532
  6.3 0.1 broadcast_in_dim.3
  6.4 0.1 stack_reshape.3
  6.5 0.0 copy-start.1
  6.5 0.0 copy-start.4
  6.6 0.0 copy-start.5
  6.6 1.8 %shard_map.180 = (bf16[4,320,128]{2,1,0:T(8,128)(2,1)S(1)}, f32[4,320,128]{2,1,0:T(8,128)S(1)}, bf16[4,320,128]{2,1,0:T(8,128)(2,1)S(1)}, bf16[4,320,128]{2,1,0:...) custom-call(f32[3,128]{1,0:T(4,128)S(1)} %get-tuple-element.38.own_c, ...), custom_call_target="tpu_custom_call" | custom-call | flops 2000000000 | bytes 10429056 | tf_op jit(solution)/shard_map/pallas_call | solution.py:541
  8.4 7.4 %shard_map.181 = (bf16[4,320,128]{2,1,0:T(8,128)(2,1)}, f32[4,320,128]{2,1,0:T(8,128)S(1)}, f32[4,320,128]{2,1,0:T(8,128)S(1)}, bf16[192,128]{1,0:T(8,128)(2,1)S...) custom-call(f32[3,128]{1,0:T(4,128)S(1)} %get-tuple-element.38.own_codes, ...), custom_call_target="tpu_custom_call" | custom-call | flops 4000000000 | bytes 26007808 | tf_op jit(solution)/shard_map/pallas_call | solution.py:541
  15.8 0.1 collective-permute-start.2
  15.9 1.4 %collective-permute-done.2 = bf16[656,128]{1,0:T(8,128)(2,1)S(1)} collective-permute-done((bf16[656,128]{1,0:T(8,128)(2,1)S(1)}, bf16[656,128]{1,0:T(8,128)(2,1)S(1)}, u32[]{:S(2)}, u32[]{:S(2)}) %collective-permute-start.2) | collective-permute-done | bytes 167968 | tf_op jit(solution)/shard_map/ppermute | solution.py:525
  17.4 1.5 %collective-permute-start.3 = (bf16[328,128]{1,0:T(8,128)(2,1)S(1)}, bf16[328,128]{1,0:T(8,128)(2,1)S(1)}, u32[]{:S(2)}, u32[]{:S(2)}) collective-permute-start(bf16[328,128]{1,0:T(8,128)(2,1)S(1)} %constant_dynamic-slice_fusion), channel_id=1, source_target_pairs={{0,2},{1,3},{2,0},{3,1},{4,6},{5,7},{6,4},{7,5},{8,10},{9,11},{10,... | collective-permute-start | bytes 251912 | tf_op jit(solution)/shard_map/ppermute | solution.py:525
  18.9 3.1 %collective-permute-done.3 = bf16[328,128]{1,0:T(8,128)(2,1)S(1)} collective-permute-done((bf16[328,128]{1,0:T(8,128)(2,1)S(1)}, bf16[328,128]{1,0:T(8,128)(2,1)S(1)}, u32[]{:S(2)}, u32[]{:S(2)}) %collective-permute-start.3) | collective-permute-done | bytes 84000 | tf_op jit(solution)/shard_map/ppermute | solution.py:525
  22.0 1.5 %collective-permute-start.4 = (bf16[328,128]{1,0:T(8,128)(2,1)S(1)}, bf16[328,128]{1,0:T(8,128)(2,1)S(1)}, u32[]{:S(2)}, u32[]{:S(2)}) collective-permute-start(bf16[328,128]{1,0:T(8,128)(2,1)S(1)} %dynamic-slice_add_fusion), channel_id=1, source_target_pairs={{0,4},{1,5},{2,6},{3,7},{4,0},{5,1},{6,2},{7,3},{8,12},{9,13},{10,... | collective-permute-start | bytes 251912 | tf_op jit(solution)/shard_map/ppermute | solution.py:525
  23.5 0.5 %collective-permute-start.5 = (bf16[192,128]{1,0:T(8,128)(2,1)S(1)}, bf16[192,128]{1,0:T(8,128)(2,1)S(1)}, u32[]{:S(2)}, u32[]{:S(2)}) collective-permute-start(bf16[192,128]{1,0:T(8,128)(2,1)S(1)} %get-tuple-element.51), channel_id=1, source_target_pairs={{1,2},{3,4},{5,6},{7,0},{2,1},{4,3},{6,5},{0,7},{9,10},{11,12},{13... | collective-permute-start | bytes 147464 | tf_op jit(solution)/shard_map/ppermute | solution.py:532
  24.1 1.3 %collective-permute-start.6 = (bf16[192,128]{1,0:T(8,128)(2,1)S(1)}, bf16[192,128]{1,0:T(8,128)(2,1)S(1)}, u32[]{:S(2)}, u32[]{:S(2)}) collective-permute-start(bf16[192,128]{1,0:T(8,128)(2,1)S(1)} %get-tuple-element.52), channel_id=1, source_target_pairs={{0,1},{1,0},{2,3},{3,2},{4,5},{5,4},{6,7},{7,6},{8,9},{9,8},{10,11... | collective-permute-start | bytes 147464 | tf_op jit(solution)/shard_map/ppermute | solution.py:525
  25.4 1.1 %collective-permute-done.4 = bf16[328,128]{1,0:T(8,128)(2,1)S(1)} collective-permute-done((bf16[328,128]{1,0:T(8,128)(2,1)S(1)}, bf16[328,128]{1,0:T(8,128)(2,1)S(1)}, u32[]{:S(2)}, u32[]{:S(2)}) %collective-permute-start.4) | collective-permute-done | bytes 84000 | tf_op jit(solution)/shard_map/ppermute | solution.py:525
  26.6 1.4 %collective-permute-done.5.link_back = bf16[192,128]{1,0:T(8,128)(2,1)S(1)} collective-permute-done((bf16[192,128]{1,0:T(8,128)(2,1)S(1)}, bf16[192,128]{1,0:T(8,128)(2,1)S(1)}, u32[]{:S(2)}, u32[]{:S(2)}) %collective-permute-start.5) | collective-permute-done | bytes 49184 | tf_op jit(solution)/shard_map/ppermute | solution.py:532
  28.0 1.8 %collective-permute-start.7 = (bf16[328,128]{1,0:T(8,128)(2,1)S(1)}, bf16[328,128]{1,0:T(8,128)(2,1)S(1)}, u32[]{:S(2)}, u32[]{:S(2)}) collective-permute-start(bf16[328,128]{1,0:T(8,128)(2,1)S(1)} %add.31), channel_id=1, source_target_pairs={{0,8},{8,0},{16,24},{24,16},{1,9},{9,1},{17,25},{25,17},{2,10},{10... | collective-permute-start | bytes 251912 | tf_op jit(solution)/shard_map/ppermute | solution.py:525
  29.7 2.7 %collective-permute-done.7 = bf16[328,128]{1,0:T(8,128)(2,1)S(1)} collective-permute-done((bf16[328,128]{1,0:T(8,128)(2,1)S(1)}, bf16[328,128]{1,0:T(8,128)(2,1)S(1)}, u32[]{:S(2)}, u32[]{:S(2)}) %collective-permute-start.7) | collective-permute-done | bytes 84000 | tf_op jit(solution)/shard_map/ppermute | solution.py:525
  32.4 2.8 %collective-permute-start.8 = (bf16[328,128]{1,0:T(8,128)(2,1)S(1)}, bf16[328,128]{1,0:T(8,128)(2,1)S(1)}, u32[]{:S(2)}, u32[]{:S(2)}) collective-permute-start(bf16[328,128]{1,0:T(8,128)(2,1)S(1)} %add.32), channel_id=1, source_target_pairs={{0,16},{8,24},{16,0},{24,8},{1,17},{9,25},{17,1},{25,9},{2,18},{10... | collective-permute-start | bytes 251912 | tf_op jit(solution)/shard_map/ppermute | solution.py:525
  35.3 1.6 %shard_map.182 = bf16[4,320,128]{2,1,0:T(8,128)(2,1)} custom-call(bf16[4,320,128]{2,1,0:T(8,128)(2,1)S(1)} %copy-done, f32[3,128]{1,0:T(4,128)S(1)} %pad_maximum_fusion.vectors.gain, f32[4,320,128]{2,1,0:T(8,128)S(1)} %get-tuple-element.54.back_norm, f32[4,320,128]{2,1,0:T(8,128)S(1)} %get-tuple-element.55.back_res, ...), custom_call_target="tpu_custom_call" | custom-call | flops 100000000 | bytes 2238240 | tf_op jit(solution)/shard_map/pallas_call | solution.py:541
  36.9 1.0 %collective-permute-done.8 = bf16[328,128]{1,0:T(8,128)(2,1)S(1)} collective-permute-done((bf16[328,128]{1,0:T(8,128)(2,1)S(1)}, bf16[328,128]{1,0:T(8,128)(2,1)S(1)}, u32[]{:S(2)}, u32[]{:S(2)}) %collective-permute-start.8) | collective-permute-done | bytes 84000 | tf_op jit(solution)/shard_map/ppermute | solution.py:525
  37.9 2.4 %collective-permute-start.9 = (bf16[328,128]{1,0:T(8,128)(2,1)S(1)}, bf16[328,128]{1,0:T(8,128)(2,1)S(1)}, u32[]{:S(2)}, u32[]{:S(2)}) collective-permute-start(bf16[328,128]{1,0:T(8,128)(2,1)S(1)} %add.33), channel_id=1, source_target_pairs={{0,2},{1,3},{2,0},{3,1},{4,6},{5,7},{6,4},{7,5},{8,10},{9,11},{10,... | collective-permute-start | bytes 251912 | tf_op jit(solution)/shard_map/ppermute | solution.py:525
  40.3 2.4 %collective-permute-done.9 = bf16[328,128]{1,0:T(8,128)(2,1)S(1)} collective-permute-done((bf16[328,128]{1,0:T(8,128)(2,1)S(1)}, bf16[328,128]{1,0:T(8,128)(2,1)S(1)}, u32[]{:S(2)}, u32[]{:S(2)}) %collective-permute-start.9) | collective-permute-done | bytes 84000 | tf_op jit(solution)/shard_map/ppermute | solution.py:525
  42.8 0.1 collective-permute-start.10
  42.9 1.4 %collective-permute-done.10.other = bf16[656,128]{1,0:T(8,128)(2,1)S(1)} collective-permute-done((bf16[656,128]{1,0:T(8,128)(2,1)S(1)}, bf16[656,128]{1,0:T(8,128)(2,1)S(1)}, u32[]{:S(2)}, u32[]{:S(2)}) %collective-permute-start.10) | collective-permute-done | bytes 167968 | tf_op jit(solution)/shard_map/ppermute | solution.py:525
  44.3 1.2 %shard_map.183 = (f32[1,128]{1,0:T(1,128)}, f32[128,384]{1,0:T(8,128)}, f32[128,128]{1,0:T(8,128)}, f32[1,4]{1,0:T(1,128)}, f32[1,128]{1,0:T(1,128)}, /*index=5*/f32[128,512]{1,0:T(8,128)}, f32[256,128]{1,0:T(8,128)}) custom-call(bf16[656,128]{1,0:T(8,128)(2,1)S(1)} %maximum_select_fusion.own, bf16[656,128]{1,0:T(8,128)(2,1)S(1)} %collective-permute-done.10.other), custom_call_target="tpu_custom_call" | custom-call | bytes 335872 | tf_op jit(solution)/shard_map/pallas_call | solution.py:541
  (28 shorter events, 0.3 us)
Async XLA Ops:
  0.6 1.0 %copy-start = (bf16[4,320,128]{2,1,0:T(8,128)(2,1)S(1)}, bf16[4,320,128]{2,1,0:T(8,128)(2,1)}, u32[]{:S(2)}) copy-start(bf16[4,320,128]{2,1,0:T(8,128)(2,1)} %state.7) | copy-start | bytes 983044
  0.7 1.0 %copy-start.6 = (s32[320]{0:T(512)S(1)}, s32[320]{0:T(512)}, u32[]{:S(2)}) copy-start(s32[320]{0:T(512)} %token_.1) | copy-start | bytes 3844
  0.7 1.0 %copy-start.7 = (s32[10]{0:T(128)S(1)}, s32[10]{0:T(128)}, u32[]{:S(2)}) copy-start(s32[10]{0:T(128)} %valid.1) | copy-start | bytes 124
  1.6 4.7 %copy-start.8 = (f32[4]{0:T(128)S(1)}, f32[4]{0:T(128)}, u32[]{:S(2)}) copy-start(f32[4]{0:T(128)} %param.17) | copy-start | bytes 52
  1.6 4.9 %copy-start.9 = (f32[128]{0:T(128)S(1)}, f32[128]{0:T(128)}, u32[]{:S(2)}) copy-start(f32[128]{0:T(128)} %param.18) | copy-start | bytes 1540
  1.6 4.9 %copy-start.10 = (f32[128]{0:T(128)S(1)}, f32[128]{0:T(128)}, u32[]{:S(2)}) copy-start(f32[128]{0:T(128)} %param.14) | copy-start | bytes 1540
  1.6 4.9 %copy-start.3 = (bf16[128,384]{1,0:T(8,128)(2,1)S(1)}, bf16[128,384]{1,0:T(8,128)(2,1)}, u32[]{:S(2)}) copy-start(bf16[128,384]{1,0:T(8,128)(2,1)} %project_weight.3) | copy-start | bytes 294916
  2.2 6.1 %collective-permute-start = (bf16[208,128]{1,0:T(8,128)(2,1)S(1)}, bf16[208,128]{1,0:T(8,128)(2,1)S(1)}, u32[]{:S(2)}, u32[]{:S(2)}) collective-permute-start(bf16[208,128]{1,0:T(8,128)(2,1)S(1)} %get-tuple-element.39), channel_id=1, source_target_pairs={{0,1},{1,0},{2,3},{3,2},{4,5},{5,4},{6,7},{7,6},{8,9},{9,8},{10,11... | collective-permute-start | bytes 159752 | tf_op jit(solution)/shard_map/ppermute | solution.py:525
  2.8 5.6 %collective-permute-start.1 = (bf16[208,128]{1,0:T(8,128)(2,1)S(1)}, bf16[208,128]{1,0:T(8,128)(2,1)S(1)}, u32[]{:S(2)}, u32[]{:S(2)}) collective-permute-start(bf16[208,128]{1,0:T(8,128)(2,1)S(1)} %get-tuple-element.40), channel_id=1, source_target_pairs={{1,2},{3,4},{5,6},{7,0},{2,1},{4,3},{6,5},{0,7},{9,10},{11,12},{13... | collective-permute-start | bytes 159752 | tf_op jit(solution)/shard_map/ppermute | solution.py:532
  6.5 1.9 %copy-start.1 = (bf16[4,320,128]{2,1,0:T(8,128)(2,1)S(1)}, bf16[4,320,128]{2,1,0:T(8,128)(2,1)}, u32[]{:S(2)}) copy-start(bf16[4,320,128]{2,1,0:T(8,128)(2,1)} %cot.1) | copy-start | bytes 983044
  6.5 1.9 %copy-start.2 = (bf16[128,512]{1,0:T(8,128)(2,1)S(1)}, bf16[128,512]{1,0:T(8,128)(2,1)}, u32[]{:S(2)}) copy-start(bf16[128,512]{1,0:T(8,128)(2,1)} %transit_weight.1) | copy-start | bytes 393220
  6.5 1.9 %copy-start.4 = (bf16[256,128]{1,0:T(8,128)(2,1)S(1)}, bf16[256,128]{1,0:T(8,128)(2,1)}, u32[]{:S(2)}) copy-start(bf16[256,128]{1,0:T(8,128)(2,1)} %return_weight.1) | copy-start | bytes 196612
  6.6 1.9 %copy-start.5 = (bf16[128,128]{1,0:T(8,128)(2,1)S(1)}, bf16[128,128]{1,0:T(8,128)(2,1)}, u32[]{:S(2)}) copy-start(bf16[128,128]{1,0:T(8,128)(2,1)} %output_weight.1) | copy-start | bytes 98308
  15.8 1.5 %collective-permute-start.2 = (bf16[656,128]{1,0:T(8,128)(2,1)S(1)}, bf16[656,128]{1,0:T(8,128)(2,1)S(1)}, u32[]{:S(2)}, u32[]{:S(2)}) collective-permute-start(bf16[656,128]{1,0:T(8,128)(2,1)S(1)} %get-tuple-element.50), channel_id=1, source_target_pairs={{0,1},{1,0},{2,3},{3,2},{4,5},{5,4},{6,7},{7,6},{8,9},{9,8},{10,11... | collective-permute-start | bytes 503816 | tf_op jit(solution)/shard_map/ppermute | solution.py:525
  17.4 4.6 %collective-permute-start.3 = (bf16[328,128]{1,0:T(8,128)(2,1)S(1)}, bf16[328,128]{1,0:T(8,128)(2,1)S(1)}, u32[]{:S(2)}, u32[]{:S(2)}) collective-permute-start(bf16[328,128]{1,0:T(8,128)(2,1)S(1)} %constant_dynamic-slice_fusion), channel_id=1, source_target_pairs={{0,2},{1,3},{2,0},{3,1},{4,6},{5,7},{6,4},{7,5},{8,10},{9,11},{10,... | collective-permute-start | bytes 251912 | tf_op jit(solution)/shard_map/ppermute | solution.py:525
  22.0 4.5 %collective-permute-start.4 = (bf16[328,128]{1,0:T(8,128)(2,1)S(1)}, bf16[328,128]{1,0:T(8,128)(2,1)S(1)}, u32[]{:S(2)}, u32[]{:S(2)}) collective-permute-start(bf16[328,128]{1,0:T(8,128)(2,1)S(1)} %dynamic-slice_add_fusion), channel_id=1, source_target_pairs={{0,4},{1,5},{2,6},{3,7},{4,0},{5,1},{6,2},{7,3},{8,12},{9,13},{10,... | collective-permute-start | bytes 251912 | tf_op jit(solution)/shard_map/ppermute | solution.py:525
  23.5 4.4 %collective-permute-start.5 = (bf16[192,128]{1,0:T(8,128)(2,1)S(1)}, bf16[192,128]{1,0:T(8,128)(2,1)S(1)}, u32[]{:S(2)}, u32[]{:S(2)}) collective-permute-start(bf16[192,128]{1,0:T(8,128)(2,1)S(1)} %get-tuple-element.51), channel_id=1, source_target_pairs={{1,2},{3,4},{5,6},{7,0},{2,1},{4,3},{6,5},{0,7},{9,10},{11,12},{13... | collective-permute-start | bytes 147464 | tf_op jit(solution)/shard_map/ppermute | solution.py:532
  24.1 3.9 %collective-permute-start.6 = (bf16[192,128]{1,0:T(8,128)(2,1)S(1)}, bf16[192,128]{1,0:T(8,128)(2,1)S(1)}, u32[]{:S(2)}, u32[]{:S(2)}) collective-permute-start(bf16[192,128]{1,0:T(8,128)(2,1)S(1)} %get-tuple-element.52), channel_id=1, source_target_pairs={{0,1},{1,0},{2,3},{3,2},{4,5},{5,4},{6,7},{7,6},{8,9},{9,8},{10,11... | collective-permute-start | bytes 147464 | tf_op jit(solution)/shard_map/ppermute | solution.py:525
  28.0 4.5 %collective-permute-start.7 = (bf16[328,128]{1,0:T(8,128)(2,1)S(1)}, bf16[328,128]{1,0:T(8,128)(2,1)S(1)}, u32[]{:S(2)}, u32[]{:S(2)}) collective-permute-start(bf16[328,128]{1,0:T(8,128)(2,1)S(1)} %add.31), channel_id=1, source_target_pairs={{0,8},{8,0},{16,24},{24,16},{1,9},{9,1},{17,25},{25,17},{2,10},{10... | collective-permute-start | bytes 251912 | tf_op jit(solution)/shard_map/ppermute | solution.py:525
  32.4 5.4 %collective-permute-start.8 = (bf16[328,128]{1,0:T(8,128)(2,1)S(1)}, bf16[328,128]{1,0:T(8,128)(2,1)S(1)}, u32[]{:S(2)}, u32[]{:S(2)}) collective-permute-start(bf16[328,128]{1,0:T(8,128)(2,1)S(1)} %add.32), channel_id=1, source_target_pairs={{0,16},{8,24},{16,0},{24,8},{1,17},{9,25},{17,1},{25,9},{2,18},{10... | collective-permute-start | bytes 251912 | tf_op jit(solution)/shard_map/ppermute | solution.py:525
  37.9 4.9 %collective-permute-start.9 = (bf16[328,128]{1,0:T(8,128)(2,1)S(1)}, bf16[328,128]{1,0:T(8,128)(2,1)S(1)}, u32[]{:S(2)}, u32[]{:S(2)}) collective-permute-start(bf16[328,128]{1,0:T(8,128)(2,1)S(1)} %add.33), channel_id=1, source_target_pairs={{0,2},{1,3},{2,0},{3,1},{4,6},{5,7},{6,4},{7,5},{8,10},{9,11},{10,... | collective-permute-start | bytes 251912 | tf_op jit(solution)/shard_map/ppermute | solution.py:525
  42.8 1.5 %collective-permute-start.10 = (bf16[656,128]{1,0:T(8,128)(2,1)S(1)}, bf16[656,128]{1,0:T(8,128)(2,1)S(1)}, u32[]{:S(2)}, u32[]{:S(2)}) collective-permute-start(bf16[656,128]{1,0:T(8,128)(2,1)S(1)} %maximum_select_fusion.own), channel_id=1, source_target_pairs={{0,1},{1,0},{2,3},{3,2},{4,5},{5,4},{6,7},{7,6},{8,9},{9,8},{10,11... | collective-permute-start | bytes 503816 | tf_op jit(solution)/shard_map/ppermute | solution.py:525

commit v6 on v5

--- a/solution.py
+++ b/solution.py
@@ -17,8 +17,8 @@
 CLIP_NORM = 256.0
 LANES = 128
 GROUP = 10
-CHUNK = 2
-SPAN = 2
+CHUNK = 4
+SPAN = 4
 SLOT = 16
 LOG2E = 1.0 / math.log(2.0)
 
@@ -307,13 +307,13 @@
         both = mm(transit_in, transit_weight[...])
         gate = both[:, :TRANS]
         up = both[:, TRANS:]
-        sigmoid = 1.0 / (1.0 + jnp.exp(-gate))
+        sigmoid = 1.0 / (1.0 + jnp.exp2(gate * -LOG2E))
         silu = gate * sigmoid
         gated = (silu * up).astype(BF16)
         fill(block_out, c, (residual + mm(gated, return_weight[...])).astype(BF16))
         cot16 = flat(cot, c)
         back_gated = mm_nt(cot16, return_weight[...])
-        back_gate = back_gated * up * sigmoid * (1.0 + gate * (1.0 - sigmoid))
+        back_gate = back_gated * up * (sigmoid + silu * (1.0 - sigmoid))
         back_hidden = jnp.concatenate([back_gate, back_gated * silu], axis=1).astype(BF16)
         grads[c, pl.ds(8 * channels, TRANS), :] = mm_tn(gated, cot16)
         grad_transit = mm_tn(transit_in, back_hidden)

time: 45.6 us -> 45.2 us (level)
  Pallas kernels: 12.6 us -> 12.1 us
  transfers between devices with their start and end apart: 11 -> 11, of which waited for: 8 -> 8; matrix products, arithmetic and copies ran while one was open for 0% -> 0% of each run, Pallas kernels for 7% -> 8%
where the time goes in v6:
time: 45.2 us; the launch traced here: 45 us
  starting transfers between devices  16.2 us (36%)
  waiting for transfers between devices  14.4 us (32%)
  Pallas kernels  12.1 us (27%)
  local copies, waits for them, and re-layouts  1.16 us (3%)
  between operations  0.89 us (2%)
    ppermute x9, waiting for transfers between devices, swap(): lax.ppermute(value, axis, [(i, i ^ mask) for i in range(lax.axis_size(axi...  13.1 us
    ppermute x9, starting transfers between devices, swap(): lax.ppermute(value, axis, [(i, i ^ mask) for i in range(lax.axis_size(axi...  12.1 us
    pallas_call x6, Pallas kernels, call(): pl.pallas_call(kernel, out_shape=[jax.ShapeDtypeStruct(shape, dtype) for...  12.1 us
    ppermute x2, starting transfers between devices, pair_exchange(): return (lax.ppermute(to_link, axis, links), swap(to_partner, axis, 1))  4.08 us
    ppermute x2, waiting for transfers between devices, pair_exchange(): return (lax.ppermute(to_link, axis, links), swap(to_partner, axis, 1))  1.39 us
    unnamed x22, local copies, waits for them, and re-layouts  0.99 us
  transfers between devices with their start and end apart: 11, of which 8 were waited for; matrix products, arithmetic and copies ran while one was open for 0% of the time, Pallas kernels for 8%

profile of v6, /device:TPU:0, one launch (start us, length us, event | category | flops | bytes accessed | tf_op | source)
XLA Modules:
  0.0 45.0 jit_solution(13124196818757818713)
XLA Ops:
  0.7 0.9 %copy-done = bf16[4,320,128]{2,1,0:T(8,128)(2,1)S(1)} copy-done((bf16[4,320,128]{2,1,0:T(8,128)(2,1)S(1)}, bf16[4,320,128]{2,1,0:T(8,128)(2,1)}, u32[]{:S(2)}) %copy-start) | copy-done | bytes 327704
  1.6 0.0 copy-start.10
  1.6 0.0 copy-start.3
  1.7 0.6 %shard_map.179 = (f32[3,128]{1,0:T(4,128)S(1)}, bf16[208,128]{1,0:T(8,128)(2,1)S(1)}, bf16[208,128]{1,0:T(8,128)(2,1)S(1)}) custom-call(s32[10]{0:T(128)S(1)} %copy-done.7, f32[16,128]{1,0:T(8,128)S(1)} %shard_map.178.blank, bf16[4,320,128]{2,1,0:T(8,128)(2,1)S(1)} %copy-done, s32[320]{0:T(512)S(1)} %copy-done.6), custom_call_target="tpu_custom_call" | custom-call | flops 10000000000 | bytes 50337192 | tf_op jit(solution)/shard_map/pallas_call | solution.py:541
  2.2 0.6 %collective-permute-start = (bf16[208,128]{1,0:T(8,128)(2,1)S(1)}, bf16[208,128]{1,0:T(8,128)(2,1)S(1)}, u32[]{:S(2)}, u32[]{:S(2)}) collective-permute-start(bf16[208,128]{1,0:T(8,128)(2,1)S(1)} %get-tuple-element.39), channel_id=1, source_target_pairs={{0,1},{1,0},{2,3},{3,2},{4,5},{5,4},{6,7},{7,6},{8,9},{9,8},{10,11... | collective-permute-start | bytes 159752 | tf_op jit(solution)/shard_map/ppermute | solution.py:525
  2.8 3.5 %collective-permute-start.1 = (bf16[208,128]{1,0:T(8,128)(2,1)S(1)}, bf16[208,128]{1,0:T(8,128)(2,1)S(1)}, u32[]{:S(2)}, u32[]{:S(2)}) collective-permute-start(bf16[208,128]{1,0:T(8,128)(2,1)S(1)} %get-tuple-element.40), channel_id=1, source_target_pairs={{1,2},{3,4},{5,6},{7,0},{2,1},{4,3},{6,5},{0,7},{9,10},{11,12},{13... | collective-permute-start | bytes 159752 | tf_op jit(solution)/shard_map/ppermute | solution.py:532
  6.3 0.1 broadcast_in_dim.3
  6.4 0.1 stack_reshape.3
  6.5 0.0 copy-start.1
  6.5 0.0 copy-start.2
  6.5 0.0 copy-start.4
  6.6 1.8 %shard_map.180 = (bf16[4,320,128]{2,1,0:T(8,128)(2,1)S(1)}, f32[4,320,128]{2,1,0:T(8,128)S(1)}, bf16[4,320,128]{2,1,0:T(8,128)(2,1)S(1)}, bf16[4,320,128]{2,1,0:...) custom-call(f32[3,128]{1,0:T(4,128)S(1)} %get-tuple-element.38.own_c, ...), custom_call_target="tpu_custom_call" | custom-call | flops 2000000000 | bytes 10429056 | tf_op jit(solution)/shard_map/pallas_call | solution.py:541
  8.4 7.0 %shard_map.181 = (bf16[4,320,128]{2,1,0:T(8,128)(2,1)}, f32[4,320,128]{2,1,0:T(8,128)S(1)}, f32[4,320,128]{2,1,0:T(8,128)S(1)}, bf16[192,128]{1,0:T(8,128)(2,1)S...) custom-call(f32[3,128]{1,0:T(4,128)S(1)} %get-tuple-element.38.own_codes, ...), custom_call_target="tpu_custom_call" | custom-call | flops 4000000000 | bytes 26007808 | tf_op jit(solution)/shard_map/pallas_call | solution.py:541
  15.4 0.1 collective-permute-start.2
  15.5 1.4 %collective-permute-done.2 = bf16[656,128]{1,0:T(8,128)(2,1)S(1)} collective-permute-done((bf16[656,128]{1,0:T(8,128)(2,1)S(1)}, bf16[656,128]{1,0:T(8,128)(2,1)S(1)}, u32[]{:S(2)}, u32[]{:S(2)}) %collective-permute-start.2) | collective-permute-done | bytes 167968 | tf_op jit(solution)/shard_map/ppermute | solution.py:525
  16.9 1.5 %collective-permute-start.3 = (bf16[328,128]{1,0:T(8,128)(2,1)S(1)}, bf16[328,128]{1,0:T(8,128)(2,1)S(1)}, u32[]{:S(2)}, u32[]{:S(2)}) collective-permute-start(bf16[328,128]{1,0:T(8,128)(2,1)S(1)} %constant_dynamic-slice_fusion), channel_id=1, source_target_pairs={{0,2},{1,3},{2,0},{3,1},{4,6},{5,7},{6,4},{7,5},{8,10},{9,11},{10,... | collective-permute-start | bytes 251912 | tf_op jit(solution)/shard_map/ppermute | solution.py:525
  18.5 3.1 %collective-permute-done.3 = bf16[328,128]{1,0:T(8,128)(2,1)S(1)} collective-permute-done((bf16[328,128]{1,0:T(8,128)(2,1)S(1)}, bf16[328,128]{1,0:T(8,128)(2,1)S(1)}, u32[]{:S(2)}, u32[]{:S(2)}) %collective-permute-start.3) | collective-permute-done | bytes 84000 | tf_op jit(solution)/shard_map/ppermute | solution.py:525
  21.6 1.5 %collective-permute-start.4 = (bf16[328,128]{1,0:T(8,128)(2,1)S(1)}, bf16[328,128]{1,0:T(8,128)(2,1)S(1)}, u32[]{:S(2)}, u32[]{:S(2)}) collective-permute-start(bf16[328,128]{1,0:T(8,128)(2,1)S(1)} %dynamic-slice_add_fusion), channel_id=1, source_target_pairs={{0,4},{1,5},{2,6},{3,7},{4,0},{5,1},{6,2},{7,3},{8,12},{9,13},{10,... | collective-permute-start | bytes 251912 | tf_op jit(solution)/shard_map/ppermute | solution.py:525
  23.1 0.5 %collective-permute-start.5 = (bf16[192,128]{1,0:T(8,128)(2,1)S(1)}, bf16[192,128]{1,0:T(8,128)(2,1)S(1)}, u32[]{:S(2)}, u32[]{:S(2)}) collective-permute-start(bf16[192,128]{1,0:T(8,128)(2,1)S(1)} %get-tuple-element.51), channel_id=1, source_target_pairs={{1,2},{3,4},{5,6},{7,0},{2,1},{4,3},{6,5},{0,7},{9,10},{11,12},{13... | collective-permute-start | bytes 147464 | tf_op jit(solution)/shard_map/ppermute | solution.py:532
  23.6 1.3 %collective-permute-start.6 = (bf16[192,128]{1,0:T(8,128)(2,1)S(1)}, bf16[192,128]{1,0:T(8,128)(2,1)S(1)}, u32[]{:S(2)}, u32[]{:S(2)}) collective-permute-start(bf16[192,128]{1,0:T(8,128)(2,1)S(1)} %get-tuple-element.52), channel_id=1, source_target_pairs={{0,1},{1,0},{2,3},{3,2},{4,5},{5,4},{6,7},{7,6},{8,9},{9,8},{10,11... | collective-permute-start | bytes 147464 | tf_op jit(solution)/shard_map/ppermute | solution.py:525
  24.9 1.1 %collective-permute-done.4 = bf16[328,128]{1,0:T(8,128)(2,1)S(1)} collective-permute-done((bf16[328,128]{1,0:T(8,128)(2,1)S(1)}, bf16[328,128]{1,0:T(8,128)(2,1)S(1)}, u32[]{:S(2)}, u32[]{:S(2)}) %collective-permute-start.4) | collective-permute-done | bytes 84000 | tf_op jit(solution)/shard_map/ppermute | solution.py:525
  26.1 1.4 %collective-permute-done.5.link_back = bf16[192,128]{1,0:T(8,128)(2,1)S(1)} collective-permute-done((bf16[192,128]{1,0:T(8,128)(2,1)S(1)}, bf16[192,128]{1,0:T(8,128)(2,1)S(1)}, u32[]{:S(2)}, u32[]{:S(2)}) %collective-permute-start.5) | collective-permute-done | bytes 49184 | tf_op jit(solution)/shard_map/ppermute | solution.py:532
  27.5 1.8 %collective-permute-start.7 = (bf16[328,128]{1,0:T(8,128)(2,1)S(1)}, bf16[328,128]{1,0:T(8,128)(2,1)S(1)}, u32[]{:S(2)}, u32[]{:S(2)}) collective-permute-start(bf16[328,128]{1,0:T(8,128)(2,1)S(1)} %add.31), channel_id=1, source_target_pairs={{0,8},{8,0},{16,24},{24,16},{1,9},{9,1},{17,25},{25,17},{2,10},{10... | collective-permute-start | bytes 251912 | tf_op jit(solution)/shard_map/ppermute | solution.py:525
  29.3 2.7 %collective-permute-done.7 = bf16[328,128]{1,0:T(8,128)(2,1)S(1)} collective-permute-done((bf16[328,128]{1,0:T(8,128)(2,1)S(1)}, bf16[328,128]{1,0:T(8,128)(2,1)S(1)}, u32[]{:S(2)}, u32[]{:S(2)}) %collective-permute-start.7) | collective-permute-done | bytes 84000 | tf_op jit(solution)/shard_map/ppermute | solution.py:525
  32.0 2.8 %collective-permute-start.8 = (bf16[328,128]{1,0:T(8,128)(2,1)S(1)}, bf16[328,128]{1,0:T(8,128)(2,1)S(1)}, u32[]{:S(2)}, u32[]{:S(2)}) collective-permute-start(bf16[328,128]{1,0:T(8,128)(2,1)S(1)} %add.32), channel_id=1, source_target_pairs={{0,16},{8,24},{16,0},{24,8},{1,17},{9,25},{17,1},{25,9},{2,18},{10... | collective-permute-start | bytes 251912 | tf_op jit(solution)/shard_map/ppermute | solution.py:525
  34.8 1.6 %shard_map.182 = bf16[4,320,128]{2,1,0:T(8,128)(2,1)} custom-call(bf16[4,320,128]{2,1,0:T(8,128)(2,1)S(1)} %copy-done, f32[3,128]{1,0:T(4,128)S(1)} %pad_maximum_fusion.vectors.gain, f32[4,320,128]{2,1,0:T(8,128)S(1)} %get-tuple-element.54.back_norm, f32[4,320,128]{2,1,0:T(8,128)S(1)} %get-tuple-element.55.back_res, ...), custom_call_target="tpu_custom_call" | custom-call | flops 100000000 | bytes 2238240 | tf_op jit(solution)/shard_map/pallas_call | solution.py:541
  36.5 1.0 %collective-permute-done.8 = bf16[328,128]{1,0:T(8,128)(2,1)S(1)} collective-permute-done((bf16[328,128]{1,0:T(8,128)(2,1)S(1)}, bf16[328,128]{1,0:T(8,128)(2,1)S(1)}, u32[]{:S(2)}, u32[]{:S(2)}) %collective-permute-start.8) | collective-permute-done | bytes 84000 | tf_op jit(solution)/shard_map/ppermute | solution.py:525
  37.5 2.4 %collective-permute-start.9 = (bf16[328,128]{1,0:T(8,128)(2,1)S(1)}, bf16[328,128]{1,0:T(8,128)(2,1)S(1)}, u32[]{:S(2)}, u32[]{:S(2)}) collective-permute-start(bf16[328,128]{1,0:T(8,128)(2,1)S(1)} %add.33), channel_id=1, source_target_pairs={{0,2},{1,3},{2,0},{3,1},{4,6},{5,7},{6,4},{7,5},{8,10},{9,11},{10,... | collective-permute-start | bytes 251912 | tf_op jit(solution)/shard_map/ppermute | solution.py:525
  39.9 2.4 %collective-permute-done.9 = bf16[328,128]{1,0:T(8,128)(2,1)S(1)} collective-permute-done((bf16[328,128]{1,0:T(8,128)(2,1)S(1)}, bf16[328,128]{1,0:T(8,128)(2,1)S(1)}, u32[]{:S(2)}, u32[]{:S(2)}) %collective-permute-start.9) | collective-permute-done | bytes 84000 | tf_op jit(solution)/shard_map/ppermute | solution.py:525
  42.4 0.1 collective-permute-start.10
  42.5 1.4 %collective-permute-done.10.other = bf16[656,128]{1,0:T(8,128)(2,1)S(1)} collective-permute-done((bf16[656,128]{1,0:T(8,128)(2,1)S(1)}, bf16[656,128]{1,0:T(8,128)(2,1)S(1)}, u32[]{:S(2)}, u32[]{:S(2)}) %collective-permute-start.10) | collective-permute-done | bytes 167968 | tf_op jit(solution)/shard_map/ppermute | solution.py:525
  43.9 1.2 %shard_map.183 = (f32[1,128]{1,0:T(1,128)}, f32[128,384]{1,0:T(8,128)}, f32[128,128]{1,0:T(8,128)}, f32[1,4]{1,0:T(1,128)}, f32[1,128]{1,0:T(1,128)}, /*index=5*/f32[128,512]{1,0:T(8,128)}, f32[256,128]{1,0:T(8,128)}) custom-call(bf16[656,128]{1,0:T(8,128)(2,1)S(1)} %maximum_select_fusion.own, bf16[656,128]{1,0:T(8,128)(2,1)S(1)} %collective-permute-done.10.other), custom_call_target="tpu_custom_call" | custom-call | bytes 335872 | tf_op jit(solution)/shard_map/pallas_call | solution.py:541
  (28 shorter events, 0.3 us)
Async XLA Ops:
  0.6 1.0 %copy-start = (bf16[4,320,128]{2,1,0:T(8,128)(2,1)S(1)}, bf16[4,320,128]{2,1,0:T(8,128)(2,1)}, u32[]{:S(2)}) copy-start(bf16[4,320,128]{2,1,0:T(8,128)(2,1)} %state.7) | copy-start | bytes 983044
  0.7 1.0 %copy-start.6 = (s32[320]{0:T(512)S(1)}, s32[320]{0:T(512)}, u32[]{:S(2)}) copy-start(s32[320]{0:T(512)} %token_.1) | copy-start | bytes 3844
  0.7 1.0 %copy-start.7 = (s32[10]{0:T(128)S(1)}, s32[10]{0:T(128)}, u32[]{:S(2)}) copy-start(s32[10]{0:T(128)} %valid.1) | copy-start | bytes 124
  1.6 4.7 %copy-start.8 = (f32[4]{0:T(128)S(1)}, f32[4]{0:T(128)}, u32[]{:S(2)}) copy-start(f32[4]{0:T(128)} %param.17) | copy-start | bytes 52
  1.6 4.9 %copy-start.9 = (f32[128]{0:T(128)S(1)}, f32[128]{0:T(128)}, u32[]{:S(2)}) copy-start(f32[128]{0:T(128)} %param.18) | copy-start | bytes 1540
  1.6 4.9 %copy-start.10 = (f32[128]{0:T(128)S(1)}, f32[128]{0:T(128)}, u32[]{:S(2)}) copy-start(f32[128]{0:T(128)} %param.14) | copy-start | bytes 1540
  1.6 4.9 %copy-start.3 = (bf16[128,384]{1,0:T(8,128)(2,1)S(1)}, bf16[128,384]{1,0:T(8,128)(2,1)}, u32[]{:S(2)}) copy-start(bf16[128,384]{1,0:T(8,128)(2,1)} %project_weight.3) | copy-start | bytes 294916
  2.2 6.1 %collective-permute-start = (bf16[208,128]{1,0:T(8,128)(2,1)S(1)}, bf16[208,128]{1,0:T(8,128)(2,1)S(1)}, u32[]{:S(2)}, u32[]{:S(2)}) collective-permute-start(bf16[208,128]{1,0:T(8,128)(2,1)S(1)} %get-tuple-element.39), channel_id=1, source_target_pairs={{0,1},{1,0},{2,3},{3,2},{4,5},{5,4},{6,7},{7,6},{8,9},{9,8},{10,11... | collective-permute-start | bytes 159752 | tf_op jit(solution)/shard_map/ppermute | solution.py:525
  2.8 5.6 %collective-permute-start.1 = (bf16[208,128]{1,0:T(8,128)(2,1)S(1)}, bf16[208,128]{1,0:T(8,128)(2,1)S(1)}, u32[]{:S(2)}, u32[]{:S(2)}) collective-permute-start(bf16[208,128]{1,0:T(8,128)(2,1)S(1)} %get-tuple-element.40), channel_id=1, source_target_pairs={{1,2},{3,4},{5,6},{7,0},{2,1},{4,3},{6,5},{0,7},{9,10},{11,12},{13... | collective-permute-start | bytes 159752 | tf_op jit(solution)/shard_map/ppermute | solution.py:532
  6.5 1.9 %copy-start.1 = (bf16[4,320,128]{2,1,0:T(8,128)(2,1)S(1)}, bf16[4,320,128]{2,1,0:T(8,128)(2,1)}, u32[]{:S(2)}) copy-start(bf16[4,320,128]{2,1,0:T(8,128)(2,1)} %cot.1) | copy-start | bytes 983044
  6.5 1.9 %copy-start.2 = (bf16[128,512]{1,0:T(8,128)(2,1)S(1)}, bf16[128,512]{1,0:T(8,128)(2,1)}, u32[]{:S(2)}) copy-start(bf16[128,512]{1,0:T(8,128)(2,1)} %transit_weight.1) | copy-start | bytes 393220
  6.5 1.9 %copy-start.4 = (bf16[256,128]{1,0:T(8,128)(2,1)S(1)}, bf16[256,128]{1,0:T(8,128)(2,1)}, u32[]{:S(2)}) copy-start(bf16[256,128]{1,0:T(8,128)(2,1)} %return_weight.1) | copy-start | bytes 196612
  6.6 1.9 %copy-start.5 = (bf16[128,128]{1,0:T(8,128)(2,1)S(1)}, bf16[128,128]{1,0:T(8,128)(2,1)}, u32[]{:S(2)}) copy-start(bf16[128,128]{1,0:T(8,128)(2,1)} %output_weight.1) | copy-start | bytes 98308
  15.4 1.5 %collective-permute-start.2 = (bf16[656,128]{1,0:T(8,128)(2,1)S(1)}, bf16[656,128]{1,0:T(8,128)(2,1)S(1)}, u32[]{:S(2)}, u32[]{:S(2)}) collective-permute-start(bf16[656,128]{1,0:T(8,128)(2,1)S(1)} %get-tuple-element.50), channel_id=1, source_target_pairs={{0,1},{1,0},{2,3},{3,2},{4,5},{5,4},{6,7},{7,6},{8,9},{9,8},{10,11... | collective-permute-start | bytes 503816 | tf_op jit(solution)/shard_map/ppermute | solution.py:525
  16.9 4.6 %collective-permute-start.3 = (bf16[328,128]{1,0:T(8,128)(2,1)S(1)}, bf16[328,128]{1,0:T(8,128)(2,1)S(1)}, u32[]{:S(2)}, u32[]{:S(2)}) collective-permute-start(bf16[328,128]{1,0:T(8,128)(2,1)S(1)} %constant_dynamic-slice_fusion), channel_id=1, source_target_pairs={{0,2},{1,3},{2,0},{3,1},{4,6},{5,7},{6,4},{7,5},{8,10},{9,11},{10,... | collective-permute-start | bytes 251912 | tf_op jit(solution)/shard_map/ppermute | solution.py:525
  21.6 4.5 %collective-permute-start.4 = (bf16[328,128]{1,0:T(8,128)(2,1)S(1)}, bf16[328,128]{1,0:T(8,128)(2,1)S(1)}, u32[]{:S(2)}, u32[]{:S(2)}) collective-permute-start(bf16[328,128]{1,0:T(8,128)(2,1)S(1)} %dynamic-slice_add_fusion), channel_id=1, source_target_pairs={{0,4},{1,5},{2,6},{3,7},{4,0},{5,1},{6,2},{7,3},{8,12},{9,13},{10,... | collective-permute-start | bytes 251912 | tf_op jit(solution)/shard_map/ppermute | solution.py:525
  23.1 4.4 %collective-permute-start.5 = (bf16[192,128]{1,0:T(8,128)(2,1)S(1)}, bf16[192,128]{1,0:T(8,128)(2,1)S(1)}, u32[]{:S(2)}, u32[]{:S(2)}) collective-permute-start(bf16[192,128]{1,0:T(8,128)(2,1)S(1)} %get-tuple-element.51), channel_id=1, source_target_pairs={{1,2},{3,4},{5,6},{7,0},{2,1},{4,3},{6,5},{0,7},{9,10},{11,12},{13... | collective-permute-start | bytes 147464 | tf_op jit(solution)/shard_map/ppermute | solution.py:532
  23.6 3.9 %collective-permute-start.6 = (bf16[192,128]{1,0:T(8,128)(2,1)S(1)}, bf16[192,128]{1,0:T(8,128)(2,1)S(1)}, u32[]{:S(2)}, u32[]{:S(2)}) collective-permute-start(bf16[192,128]{1,0:T(8,128)(2,1)S(1)} %get-tuple-element.52), channel_id=1, source_target_pairs={{0,1},{1,0},{2,3},{3,2},{4,5},{5,4},{6,7},{7,6},{8,9},{9,8},{10,11... | collective-permute-start | bytes 147464 | tf_op jit(solution)/shard_map/ppermute | solution.py:525
  27.5 4.5 %collective-permute-start.7 = (bf16[328,128]{1,0:T(8,128)(2,1)S(1)}, bf16[328,128]{1,0:T(8,128)(2,1)S(1)}, u32[]{:S(2)}, u32[]{:S(2)}) collective-permute-start(bf16[328,128]{1,0:T(8,128)(2,1)S(1)} %add.31), channel_id=1, source_target_pairs={{0,8},{8,0},{16,24},{24,16},{1,9},{9,1},{17,25},{25,17},{2,10},{10... | collective-permute-start | bytes 251912 | tf_op jit(solution)/shard_map/ppermute | solution.py:525
  32.0 5.4 %collective-permute-start.8 = (bf16[328,128]{1,0:T(8,128)(2,1)S(1)}, bf16[328,128]{1,0:T(8,128)(2,1)S(1)}, u32[]{:S(2)}, u32[]{:S(2)}) collective-permute-start(bf16[328,128]{1,0:T(8,128)(2,1)S(1)} %add.32), channel_id=1, source_target_pairs={{0,16},{8,24},{16,0},{24,8},{1,17},{9,25},{17,1},{25,9},{2,18},{10... | collective-permute-start | bytes 251912 | tf_op jit(solution)/shard_map/ppermute | solution.py:525
  37.5 4.9 %collective-permute-start.9 = (bf16[328,128]{1,0:T(8,128)(2,1)S(1)}, bf16[328,128]{1,0:T(8,128)(2,1)S(1)}, u32[]{:S(2)}, u32[]{:S(2)}) collective-permute-start(bf16[328,128]{1,0:T(8,128)(2,1)S(1)} %add.33), channel_id=1, source_target_pairs={{0,2},{1,3},{2,0},{3,1},{4,6},{5,7},{6,4},{7,5},{8,10},{9,11},{10,... | collective-permute-start | bytes 251912 | tf_op jit(solution)/shard_map/ppermute | solution.py:525
  42.4 1.5 %collective-permute-start.10 = (bf16[656,128]{1,0:T(8,128)(2,1)S(1)}, bf16[656,128]{1,0:T(8,128)(2,1)S(1)}, u32[]{:S(2)}, u32[]{:S(2)}) collective-permute-start(bf16[656,128]{1,0:T(8,128)(2,1)S(1)} %maximum_select_fusion.own), channel_id=1, source_target_pairs={{0,1},{1,0},{2,3},{3,2},{4,5},{5,4},{6,7},{7,6},{8,9},{9,8},{10,11... | collective-permute-start | bytes 503816 | tf_op jit(solution)/shard_map/ppermute | solution.py:525
